TPU v7x, 32 devices: a whole 2x2x4 slice. The times are simulated.
32 devices in a mesh: tp: 4 (over z), fsdp: 8 (over y, x, core).
Axes of the slice: x: 2, y: 2, z: 4, core: 2. Of those that a mesh axis runs over, the one named last changes fastest.
Arguments:
- x_in: bfloat16 [64, 256, 2560], P('fsdp')
- grad_y: bfloat16 [64, 256, 2560], P('fsdp')
- w_query: bfloat16 [2560, 2560], P('fsdp', 'tp')
- w_key: bfloat16 [2560, 2560], P('fsdp', 'tp')
- w_value: bfloat16 [2560, 2560], P('fsdp', 'tp')
- w_out: bfloat16 [2560, 2560], P('tp', 'fsdp')
- w_up: bfloat16 [2560, 10240], P('fsdp', 'tp')
- b_up: float32 [10240], P('tp')
- w_down: bfloat16 [10240, 2560], P('tp', 'fsdp')
- ln_scale: float32 [2560], replicated
- q_scale: float32 [80], replicated
- k_scale: float32 [80], replicated
Outputs:
- output 1: bfloat16 [64, 256, 2560], P('fsdp')
- output 2: float32 [2560, 2560], P('fsdp', 'tp')
- output 3: float32 [2560, 2560], P('fsdp', 'tp')
- output 4: float32 [2560, 2560], P('fsdp', 'tp')
- output 5: float32 [2560, 2560], P('tp', 'fsdp')
- output 6: float32 [2560, 10240], P('fsdp', 'tp')
- output 7: float32 [10240], P('tp')
- output 8: float32 [10240, 2560], P('tp', 'fsdp')
- output 9: float32 [2560], replicated
- output 10: float32 [2560], replicated
- output 11: float32 [80], replicated
- output 12: float32 [80], replicated
All inputs are finite; a program needn't handle non-finite values.
Results may differ from a plain program's by a relative error of at most 0.012411.
Values are sent between devices in bfloat16 or wider.
A program may use at most 1 GiB of HBM per device.

v0:
```python
import functools
import jax
import jax.numpy as jnp
from jax import lax
from jax.sharding import PartitionSpec as P

EPS = 1e-6


def scaled_norm(values, scale_vec):
    row_mean = jnp.mean(values, axis=-1, keepdims=True)
    centred = values - row_mean
    row_var = jnp.mean(centred * centred, axis=-1, keepdims=True)
    return centred * lax.rsqrt(row_var + EPS) * scale_vec


def exact_gelu(values):
    return jax.nn.gelu(values, approximate=False)


def solution(mesh):
    act_spec = P('fsdp', None, None)
    row_spec = P('fsdp', 'tp')
    col_spec = P('tp', 'fsdp')
    in_specs = (act_spec, act_spec, row_spec, row_spec, row_spec, col_spec, row_spec, P('tp'), col_spec, P(), P(), P())
    out_specs = (act_spec, row_spec, row_spec, row_spec, col_spec, row_spec, P('tp'), col_spec, P(), P(), P(), P())
    gather_rows = functools.partial(lax.all_gather, axis_name='fsdp', axis=0, tiled=True)
    gather_cols = functools.partial(lax.all_gather, axis_name='fsdp', axis=1, tiled=True)
    scatter_rows = functools.partial(lax.psum_scatter, axis_name='fsdp', scatter_dimension=0, tiled=True)
    scatter_cols = functools.partial(lax.psum_scatter, axis_name='fsdp', scatter_dimension=1, tiled=True)

    def local_step(x_in, grad_y, w_query, w_key, w_value, w_out, w_up, b_up, w_down, ln_scale, q_scale, k_scale):
        bf16 = jnp.bfloat16
        fp32 = jnp.float32
        wq_full = gather_rows(w_query)
        wk_full = gather_rows(w_key)
        wv_full = gather_rows(w_value)
        wo_full = gather_cols(w_out)
        wu_full = gather_rows(w_up)
        wd_full = gather_cols(w_down)
        head_dim = q_scale.shape[0]
        num_img = x_in.shape[0]
        num_tok = x_in.shape[1]
        num_heads = wq_full.shape[1] // head_dim
        score_scale = head_dim ** -0.5

        normed_f, ln_pull = jax.vjp(scaled_norm, x_in.astype(fp32), ln_scale)
        normed = normed_f.astype(bf16)

        def project(weight):
            return jnp.einsum('btd,dn->btn', normed, weight, preferred_element_type=fp32).astype(bf16)

        q_proj = project(wq_full).reshape(num_img, num_tok, num_heads, head_dim)
        k_proj = project(wk_full).reshape(num_img, num_tok, num_heads, head_dim)
        v_proj = project(wv_full).reshape(num_img, num_tok, num_heads, head_dim)
        qn_f, q_pull = jax.vjp(scaled_norm, q_proj.astype(fp32), q_scale)
        kn_f, k_pull = jax.vjp(scaled_norm, k_proj.astype(fp32), k_scale)
        q_norm = qn_f.astype(bf16)
        k_norm = kn_f.astype(bf16)
        logits = jnp.einsum('bqhd,bkhd->bhqk', q_norm, k_norm, preferred_element_type=fp32)
        attn_prob = jax.nn.softmax(logits * score_scale, axis=-1)
        prob_b16 = attn_prob.astype(bf16)
        attn_out = jnp.einsum('bhqk,bkhd->bqhd', prob_b16, v_proj, preferred_element_type=fp32).astype(bf16)
        attn_flat = attn_out.reshape(num_img, num_tok, -1)
        hidden = (jnp.einsum('btd,df->btf', normed, wu_full, preferred_element_type=fp32) + b_up).astype(bf16)
        act_f, gelu_pull = jax.vjp(exact_gelu, hidden.astype(fp32))
        act_out = act_f.astype(bf16)

        d_act = jnp.einsum('btd,fd->btf', grad_y, wd_full, preferred_element_type=fp32).astype(bf16)
        d_hidden = gelu_pull(d_act.astype(fp32))[0].astype(bf16)
        grad_w_down = jnp.einsum('btf,btd->fd', act_out, grad_y, preferred_element_type=fp32)
        grad_w_up = jnp.einsum('btd,btf->df', normed, d_hidden, preferred_element_type=fp32)
        grad_b_up = jnp.sum(d_hidden, axis=(0, 1), dtype=fp32)
        d_normed = jnp.einsum('btf,df->btd', d_hidden, wu_full, preferred_element_type=fp32)

        d_attn = jnp.einsum('btd,nd->btn', grad_y, wo_full, preferred_element_type=fp32).astype(bf16)
        grad_w_out = jnp.einsum('btn,btd->nd', attn_flat, grad_y, preferred_element_type=fp32)
        d_attn_heads = d_attn.reshape(num_img, num_tok, num_heads, head_dim)
        d_prob = jnp.einsum('bqhd,bkhd->bhqk', d_attn_heads, v_proj, preferred_element_type=fp32).astype(bf16).astype(fp32)
        d_value = jnp.einsum('bhqk,bqhd->bkhd', prob_b16, d_attn_heads, preferred_element_type=fp32).astype(bf16)
        d_logit = (attn_prob * (d_prob - jnp.sum(attn_prob * d_prob, axis=-1, keepdims=True)) * score_scale).astype(bf16)
        d_qnorm = jnp.einsum('bhqk,bkhd->bqhd', d_logit, k_norm, preferred_element_type=fp32).astype(bf16)
        d_knorm = jnp.einsum('bhqk,bqhd->bkhd', d_logit, q_norm, preferred_element_type=fp32).astype(bf16)
        d_query_f, grad_q_scale = q_pull(d_qnorm.astype(fp32))
        d_key_f, grad_k_scale = k_pull(d_knorm.astype(fp32))
        d_query = d_query_f.astype(bf16).reshape(num_img, num_tok, -1)
        d_key = d_key_f.astype(bf16).reshape(num_img, num_tok, -1)
        d_value_flat = d_value.reshape(num_img, num_tok, -1)
        grad_w_query = jnp.einsum('btd,btn->dn', normed, d_query, preferred_element_type=fp32)
        grad_w_key = jnp.einsum('btd,btn->dn', normed, d_key, preferred_element_type=fp32)
        grad_w_value = jnp.einsum('btd,btn->dn', normed, d_value_flat, preferred_element_type=fp32)
        d_normed = (d_normed
                    + jnp.einsum('btn,dn->btd', d_query, wq_full, preferred_element_type=fp32)
                    + jnp.einsum('btn,dn->btd', d_key, wk_full, preferred_element_type=fp32)
                    + jnp.einsum('btn,dn->btd', d_value_flat, wv_full, preferred_element_type=fp32))
        d_normed = lax.psum(d_normed, 'tp')
        d_x_f, grad_ln_scale = ln_pull(d_normed.astype(bf16).astype(fp32))
        grad_x = (grad_y.astype(fp32) + d_x_f).astype(bf16)
        grad_b_down = jnp.sum(grad_y, axis=(0, 1), dtype=fp32)
        return (grad_x, scatter_rows(grad_w_query), scatter_rows(grad_w_key), scatter_rows(grad_w_value),
                scatter_cols(grad_w_out), scatter_rows(grad_w_up), lax.psum(grad_b_up, 'fsdp'),
                scatter_cols(grad_w_down), lax.psum(grad_b_down, 'fsdp'), lax.psum(grad_ln_scale, 'fsdp'),
                lax.psum(grad_q_scale, ('tp', 'fsdp')), lax.psum(grad_k_scale, ('tp', 'fsdp')))

    return jax.shard_map(local_step, mesh=mesh, in_specs=in_specs, out_specs=out_specs, check_vma=False)
```

profile of v0, /device:TPU:0, one launch (start us, length us, event | category | flops | bytes accessed | tf_op | source)
XLA Modules:
  0.0 1422.6 jit_solution(7578014386347157705)
XLA Ops:
  7.2 0.7 all-gather.17.cloned.1.call-update
  8.0 0.7 all-gather.13.cloned.1.call-update
  8.7 0.7 all-gather.11.cloned.1.call-update
  9.4 0.5 all-gather.15.cloned.1.call-update
  10.0 0.5 all-gather.7.cloned.1.call-update
  10.6 0.5 all-gather.9.cloned.1.call-update
  11.1 0.0 reduce-scatter.13.cloned.1.call-start
  11.2 5.6 convert_reduce_fusion
  16.8 1.4 copy-done
  18.2 2.9 fusion.12
  21.0 0.6 copy-done.15
  21.6 23.5 %all-gather.17.cloned.1.call-done = bf16[2560,640]{1,0:T(8,128)(2,1)} async-done(((bf16[320,640]{1,0:T(8,128)(2,1)}), bf16[2560,640]{1,0:T(8,128)(2,1)}) %all-gather.17.cloned.1.call-update) | async-done | bytes 3276816 | tf_op jit(solution)/shard_map/all_gather | solution.py:37
  45.1 13.0 fusion.108
  58.1 2.6 copy.50
  60.7 18.8 %all-gather.13.cloned.1.call-done = bf16[2560,640]{1,0:T(8,128)(2,1)} async-done(((bf16[320,640]{1,0:T(8,128)(2,1)}), bf16[2560,640]{1,0:T(8,128)(2,1)}) %all-gather.13.cloned.1.call-update) | async-done | bytes 3276816 | tf_op jit(solution)/shard_map/all_gather | solution.py:35
  79.5 13.9 convert_convert_fusion
  93.4 5.9 copy.48
  99.3 14.5 %all-gather.11.cloned.1.call-done = bf16[2560,640]{1,0:T(8,128)(2,1)} async-done(((bf16[320,640]{1,0:T(8,128)(2,1)}), bf16[2560,640]{1,0:T(8,128)(2,1)}) %all-gather.11.cloned.1.call-update) | async-done | bytes 3276816 | tf_op jit(solution)/shard_map/all_gather | solution.py:36
  113.9 14.0 convert_convert_fusion.1
  127.8 6.0 copy.47
  133.9 3.2 reduce_sum.174
  137.1 3.1 reduce_sum.169
  140.3 3.7 multiply_reduce_fusion.1
  144.0 3.6 multiply_reduce_fusion.2
  147.7 7.5 multiply_convert_fusion
  155.2 10.9 fusion.138
  166.1 7.4 fusion.114
  173.5 13.3 convolution_bitcast_fusion.5
  186.8 0.0 reduce-scatter.7.cloned.1.call-start
  186.9 13.0 fusion.105
  199.9 3.0 copy.49
  202.9 7.5 convolution_convert_fusion
  210.4 21.4 %fusion.80 = (f32[8,256,8]{1,2,0:T(8,128)S(1)}, bf16[8,8,80,256]{3,2,1,0:T(8,128)(2,1)}) fusion(f32[8,256,8,80]{1,3,2,0:T(8,128)} %bitcast.141, f32[80]{0:T(128)S(1)} %copy-done.18, f32[8,256,8]{1,2,0:T(8,128)S(1)} %broadcast_multiply_fusion, bf16[8,256,8,80]{1,3,2,0:T(8,128)(2,1)} %get-tuple-element.36, ...), kind=kOutput, calls=%fused_computation.106 | convolution fusion | flops 716701952 | bytes 35848512 | tf_op jit(solution)/shard_map/bhqk,bkhd->bqhd/dot_general | solution.py:82
  231.9 5.2 fusion.81
  237.1 5.3 add_convert_fusion.2
  242.5 1.5 copy-done.5
  244.0 12.5 convolution_bitcast_fusion.4
  256.5 0.0 reduce-scatter.9.cloned.1.call-start
  256.5 21.7 %fusion.76 = (f32[8,256,8]{1,2,0:T(8,128)S(1)}, bf16[8,8,80,256]{3,2,1,0:T(8,128)(2,1)}) fusion(f32[8,256,8,80]{1,3,2,0:T(8,128)} %bitcast.132, f32[80]{0:T(128)S(1)} %copy-done.19, f32[8,256,8]{1,2,0:T(8,128)S(1)} %broadcast_multiply_fusion.1, bf16[8,256,8,80]{1,3,2,0:T(8,128)(2,1)} %get-tuple-element.35, ...), kind=kOutput, calls=%fused_computation.100 | convolution fusion | flops 716701952 | bytes 35848512 | tf_op jit(solution)/shard_map/bhqk,bqhd->bkhd/dot_general | solution.py:83
  278.2 5.2 fusion.77
  283.5 5.3 add_convert_fusion.1
  288.9 1.5 copy-done.7
  290.4 12.4 convolution_bitcast_fusion.3
  302.8 0.4 reduce-scatter.11.cloned.1.call-start
  303.2 8.4 fusion.111
  311.7 1.6 copy-done.4
  313.2 14.4 %convolution_bitcast_fusion.2 = f32[2560,640]{1,0:T(8,128)} fusion(bf16[8,256,640]{1,2,0:T(8,128)(2,1)S(1)} %bitcast.150, bf16[8,256,2560]{2,1,0:T(8,128)(2,1)} %param.12, f32[2560]{0:T(1024)S(1)} %copy-done.11, f32[8,256]{1,0:T(8,128)S(1)} %fusion.123, f32[8,256]{1,0:T(8,128)S(1)} %broadcast_multiply_fusion.2), kind=kOutput, calls=%fused_computation.92 | convolution fusion | flops 6737100800 | bytes 19687424 | tf_op jit(solution)/shard_map/btd,btn->dn/dot_general | solution.py:91
  327.7 0.0 reduce-scatter.17.cloned.1.call-start
  327.8 78.6 %fusion.42 = (f32[8,256,2560]{2,1,0:T(8,128)}, bf16[8,256,2560]{2,1,0:T(8,128)(2,1)}) fusion(f32[2560]{0:T(1024)S(1)} %copy-done.23, bf16[2560,2560]{1,0:T(8,128)(2,1)} %all-gather.7.cloned.1.call-done, bf16[8,256,2560]{2,1,0:T(8,128)(2,1)} %param.12, f32[2560]{0:T(1024)S(1)} %copy-done.11, f32[8,256]{1,0:T(8,128)S(1)} %fusion.123, ...), kind=kOutput, calls=%fused_computation.56 | convolution fusion | flops 27210547200 | bytes 55087104 | tf_op jit(solution)/shard_map/btd,df->btf/dot_general | solution.py:65
  406.4 36.6 %convolution_bitcast_fusion = f32[2560,2560]{0,1:T(8,128)} fusion(bf16[8,256,2560]{2,1,0:T(8,128)(2,1)} %param.13, f32[8,256,2560]{2,1,0:T(8,128)} %get-tuple-element.29, bf16[8,256,2560]{2,1,0:T(8,128)(2,1)} %get-tuple-element.30), kind=kOutput, calls=%fused_computation.68 | convolution fusion | flops 26864517120 | bytes 68157440 | tf_op jit(solution)/shard_map/btf,btd->fd/dot_general | solution.py:71
  443.0 0.0 reduce-scatter.15.cloned.1.call-start
  443.1 0.6 copy-done.20
  443.7 39.5 %all-reduce = (f32[80]{0:T(128)}, f32[80]{0:T(128)}) all-reduce(f32[80]{0:T(128)S(1)} %copy-done.20, f32[80]{0:T(128)S(1)} %copy-done.21), channel_id=1, replica_groups=mesh['tp'=4,'fsdp'=8] {'tp','fsdp'}, use_global_device_ids=true, to_apply=%region_29.0 | all-reduce | flops 160 | bytes 1280 | tf_op jit(solution)/shard_map/psum | solution.py:103
  483.2 13.6 fusion.95
  496.8 11.6 fusion.91
  508.4 43.4 %convert_reduce_fusion.2 = (f32[2560]{0:T(1024)}, bf16[8,256,2560]{2,1,0:T(8,128)(2,1)}) fusion(f32[8,256,2560]{2,1,0:T(8,128)} %get-tuple-element.29, bf16[8,256,2560]{2,1,0:T(8,128)(2,1)} %param.13, bf16[2560,2560]{0,1:T(8,128)(2,1)} %all-gather.9.cloned.1.call-done, bf16[8,256,2560]{2,1,0:T(8,128)(2,1)} %get-tuple-element.30), kind=kOutput, calls=%fused_computation.65 | convolution fusion | flops 26943158272 | bytes 65546240 | tf_op jit(solution)/shard_map/btd,fd->btf/dot_general | solution.py:69
  551.8 36.8 %convolution_bitcast_fusion.1 = f32[2560,2560]{1,0:T(8,128)} fusion(bf16[8,256,2560]{2,1,0:T(8,128)(2,1)} %get-tuple-element.34, bf16[8,256,2560]{2,1,0:T(8,128)(2,1)} %param.12, f32[2560]{0:T(1024)S(1)} %copy-done.12, f32[8,256]{1,0:T(8,128)S(1)} %copy-done.14, f32[8,256]{1,0:T(8,128)S(1)} %copy-done.10), kind=kOutput, calls=%fused_computation.69 | convolution fusion | flops 26869760000 | bytes 47212544 | tf_op jit(solution)/shard_map/btd,btf->df/dot_general | solution.py:72
  588.6 35.3 %fusion.60 = f32[8,256,2560]{2,1,0:T(8,128)} fusion(bf16[8,256,2560]{2,1,0:T(8,128)(2,1)} %get-tuple-element.34, bf16[2560,2560]{1,0:T(8,128)(2,1)} %all-gather.7.cloned.1.call-done), kind=kOutput, calls=%fused_computation.79 | convolution fusion | flops 26843545600 | bytes 44564480 | tf_op jit(solution)/shard_map/btf,df->btd/dot_general | solution.py:74
  623.9 31.5 %add_add_fusion.1 = f32[8,256,2560]{2,1,0:T(8,128)} fusion(f32[8,256,2560]{2,1,0:T(8,128)} %fusion.95, f32[8,256,2560]{2,1,0:T(8,128)} %fusion.60, f32[8,256,2560]{2,1,0:T(8,128)} %fusion.91, bf16[8,256,640]{1,2,0:T(8,128)(2,1)} %bitcast.151, bf16[2560,640]{1,0:T(8,128)(2,1)S(1)} %copy-done.3), kind=kOutput, calls=%fused_computation.66 | convolution fusion | flops 6726615040 | bytes 89784320 | tf_op jit(solution)/shard_map/btn,dn->btd/dot_general | solution.py:95
  655.4 695.4 %all-reduce.3 = bf16[8,256,2560]{2,1,0:T(8,128)(2,1)} all-reduce(f32[8,256,2560]{2,1,0:T(8,128)} %add_add_fusion.1), channel_id=1, replica_groups=mesh['tp'=4,'fsdp'=8] {'tp'}, use_global_device_ids=true, to_apply=%region_13.0 | all-reduce | flops 5242880 | bytes 31457280 | tf_op jit(solution)/shard_map/psum | solution.py:96
  1350.8 12.7 fusion.13
  1363.6 13.6 fusion.50
  1377.2 14.9 %convert_reduce_fusion.1 = (f32[2560]{0:T(1024)S(1)}, bf16[8,256,2560]{2,1,0:T(8,128)(2,1)}) fusion(bf16[8,256,2560]{2,1,0:T(8,128)(2,1)S(1)} %bitcast.149, f32[8,256]{1,0:T(8,128)S(1)} %negate_multiply_fusion.2, f32[8,256]{1,0:T(8,128)S(1)} %multiply_multiply_fusion.2, f32[8,256]{1,0:T(8,128)S(1)} %copy-done.10, bf16[8,256,2560]{2,1,0:T(8,128)(2,1)S(1)} %bitcast.129, ...), kind=kLoop, calls=%fused_computation.16 | loop fusion | flops 68154880 | bytes 41996288 | tf_op jit(solution)/shard_map/reduce_sum | solution.py:99
  1392.1 23.3 %all-reduce.1 = (f32[2560]{0:T(1024)}, f32[2560]{0:T(1024)}, f32[2560]{0:T(1024)}) all-reduce(f32[2560]{0:T(1024)S(1)} %copy-done.17, f32[2560]{0:T(1024)S(1)} %get-tuple-element.23, f32[2560]{0:T(1024)S(1)} %get-tuple-element.12), channel_id=1, replica_groups=mesh['tp'=4,'fsdp'=8] {'fsdp'}, use_global_device_ids=true, to_apply=%region_22.0 | all-reduce | flops 7680 | bytes 61440 | tf_op jit(solution)/shard_map/psum | solution.py:101
  (108 shorter events, 0.8 us)
Async XLA Ops:
  7.2 37.9 %all-gather.17.cloned.1.call-start = ((), (), s32[]{:S(2)}) async-start(), calls=%async_computation.11 | async-start | bytes 3686400 | tf_op jit(solution)/shard_map/all_gather | solution.py:37
  7.9 71.6 %all-gather.13.cloned.1.call-start = ((), (), s32[]{:S(2)}) async-start(), calls=%async_computation.9 | async-start | bytes 3686400 | tf_op jit(solution)/shard_map/all_gather | solution.py:35
  8.7 105.2 %all-gather.11.cloned.1.call-start = ((), (), s32[]{:S(2)}) async-start(), calls=%async_computation.8 | async-start | bytes 3686400 | tf_op jit(solution)/shard_map/all_gather | solution.py:36
  9.4 177.5 %all-gather.15.cloned.1.call-start = ((), (), s32[]{:S(2)}) async-start(), calls=%async_computation.10 | async-start | bytes 3686400 | tf_op jit(solution)/shard_map/all_gather | solution.py:38
  10.0 317.8 %all-gather.7.cloned.1.call-start = ((), (), s32[]{:S(2)}) async-start(), calls=%async_computation.6 | async-start | bytes 14745600 | tf_op jit(solution)/shard_map/all_gather | solution.py:39
  10.6 497.8 %all-gather.9.cloned.1.call-start = ((), (), s32[]{:S(2)}) async-start(), calls=%async_computation.7 | async-start | bytes 14745600 | tf_op jit(solution)/shard_map/all_gather | solution.py:40
  11.1 34.0 %copy-start.11 = (f32[2560]{0:T(1024)S(1)}, f32[2560]{0:T(1024)}, u32[]{:S(2)}) copy-start(f32[2560]{0:T(1024)} %param.21) | copy-start | bytes 30724
  11.1 1404.3 %reduce-scatter.13.cloned.1.call-start = ((), (), s32[]{:S(2)}) async-start(), calls=%async_computation.15 | async-start | bytes 7372800 | tf_op jit(solution)/shard_map/reduce_scatter | solution.py:101
  11.2 7.0 copy-start
  18.2 309.6 %copy-start.9 = (f32[8,256]{1,0:T(8,128)}, f32[8,256]{1,0:T(8,128)S(1)}, u32[]{:S(2)}) copy-start(f32[8,256]{1,0:T(8,128)S(1)} %broadcast_multiply_fusion.2) | copy-start | bytes 24580
  21.0 0.6 copy-start.15
  21.6 306.1 %copy-start.13 = (f32[8,256]{1,0:T(8,128)}, f32[8,256]{1,0:T(8,128)S(1)}, u32[]{:S(2)}) copy-start(f32[8,256]{1,0:T(8,128)S(1)} %fusion.123) | copy-start | bytes 24580
  133.9 13.8 slice-start.9
  133.9 13.8 copy-start.18
  133.9 13.8 copy-start.19
  140.3 7.4 slice-start.10
  155.2 10.9 copy-start.2
  186.8 1228.6 %reduce-scatter.7.cloned.1.call-start = ((), (), s32[]{:S(2)}) async-start(), calls=%async_computation.12 | async-start | bytes 7372800 | tf_op jit(solution)/shard_map/reduce_scatter | solution.py:100
  231.8 12.2 slice-start
  231.8 12.2 slice-start.1
  237.1 6.9 slice-start.2
  242.5 1.5 copy-start.5
  256.5 1159.0 %reduce-scatter.9.cloned.1.call-start = ((), (), s32[]{:S(2)}) async-start(), calls=%async_computation.13 | async-start | bytes 7372800 | tf_op jit(solution)/shard_map/reduce_scatter | solution.py:100
  278.2 12.1 slice-start.3
  278.2 12.1 slice-start.4
  283.5 6.8 slice-start.5
  288.8 1.5 copy-start.7
  302.8 1112.7 %reduce-scatter.11.cloned.1.call-start = ((), (), s32[]{:S(2)}) async-start(), calls=%async_computation.14 | async-start | bytes 7372800 | tf_op jit(solution)/shard_map/reduce_scatter | solution.py:100
  311.6 1.6 copy-start.4
  313.2 14.5 %copy-start.23 = (f32[2560]{0:T(1024)S(1)}, f32[2560]{0:T(1024)}, u32[]{:S(2)}) copy-start(f32[2560]{0:T(1024)} %param.19) | copy-start | bytes 30724
  327.7 1087.8 %reduce-scatter.17.cloned.1.call-start = ((), (), s32[]{:S(2)}) async-start(), calls=%async_computation.17 | async-start | bytes 29491200 | tf_op jit(solution)/shard_map/reduce_scatter | solution.py:102
  443.0 0.7 copy-start.20
  443.0 0.7 copy-start.21
  443.0 40.2 %copy-start.8 = (bf16[8,256,8,80]{1,3,2,0:T(8,128)(2,1)S(1)}, bf16[8,256,8,80]{1,3,2,0:T(8,128)(2,1)}, u32[]{:S(2)}) copy-start(bf16[8,256,8,80]{1,3,2,0:T(8,128)(2,1)} %copy-done.7) | copy-start | bytes 7864324
  443.0 972.5 %reduce-scatter.15.cloned.1.call-start = ((), (), s32[]{:S(2)}) async-start(), calls=%async_computation.16 | async-start | bytes 29491200 | tf_op jit(solution)/shard_map/reduce_scatter | solution.py:101
  483.2 13.6 copy-start.6
  483.2 13.6 copy-start.22
  508.4 43.4 %copy-start.10 = (f32[8,256]{1,0:T(8,128)S(1)}, f32[8,256]{1,0:T(8,128)}, u32[]{:S(2)}) copy-start(f32[8,256]{1,0:T(8,128)} %copy-done.9) | copy-start | bytes 24580
  508.4 43.4 %copy-start.12 = (f32[2560]{0:T(1024)S(1)}, f32[2560]{0:T(1024)}, u32[]{:S(2)}) copy-start(f32[2560]{0:T(1024)} %param.21) | copy-start | bytes 30724
  508.4 43.4 %copy-start.14 = (f32[8,256]{1,0:T(8,128)S(1)}, f32[8,256]{1,0:T(8,128)}, u32[]{:S(2)}) copy-start(f32[8,256]{1,0:T(8,128)} %copy-done.13) | copy-start | bytes 24580
  588.6 35.3 %copy-start.3 = (bf16[2560,640]{1,0:T(8,128)(2,1)S(1)}, bf16[2560,640]{1,0:T(8,128)(2,1)}, u32[]{:S(2)}) copy-start(bf16[2560,640]{1,0:T(8,128)(2,1)} %all-gather.17.cloned.1.call-done) | copy-start | bytes 9830404
  655.4 708.1 %copy-start.16 = (f32[8,256]{1,0:T(8,128)S(1)}, f32[8,256]{1,0:T(8,128)}, u32[]{:S(2)}) copy-start(f32[8,256]{1,0:T(8,128)} %copy-done.15) | copy-start | bytes 24580
  1350.8 12.8 copy-start.1
  1350.8 26.4 %slice-start.6 = ((s8[10485760]{0:T(1024)(128)(4,1)}), s8[4194304]{0:T(1024)(128)(4,1)S(1)}, s32[]{:S(2)}) async-start(s8[10485760]{0:T(1024)(128)(4,1)} %bitcast.128), calls=%async_computation.24 | async-start | bytes 8388608
  1350.8 26.4 %slice-start.7 = ((s8[10485760]{0:T(1024)(128)(4,1)}), s8[4194304]{0:T(1024)(128)(4,1)S(1)}, s32[]{:S(2)}) async-start(s8[10485760]{0:T(1024)(128)(4,1)} %bitcast.128), calls=%async_computation.25 | async-start | bytes 8388608
  1350.8 26.4 %slice-start.11 = ((s8[10485760]{0:T(1024)(128)(4,1)}), s8[4194304]{0:T(1024)(128)(4,1)S(1)}, s32[]{:S(2)}) async-start(s8[10485760]{0:T(1024)(128)(4,1)} %bitcast.148), calls=%async_computation.29 | async-start | bytes 8388608
  1350.8 26.4 %slice-start.12 = ((s8[10485760]{0:T(1024)(128)(4,1)}), s8[4194304]{0:T(1024)(128)(4,1)S(1)}, s32[]{:S(2)}) async-start(s8[10485760]{0:T(1024)(128)(4,1)} %bitcast.148), calls=%async_computation.30 | async-start | bytes 8388608
  1363.5 13.7 slice-start.8
  1363.5 13.7 slice-start.13
  1377.2 14.9 %copy-start.17 = (f32[2560]{0:T(1024)S(1)}, f32[2560]{0:T(1024)}, u32[]{:S(2)}) copy-start(f32[2560]{0:T(1024)} %get-tuple-element.33) | copy-start | bytes 30724
Sparse Core Ops, SparseCore 0:
  9.9 35.2 all-gather.16
  47.0 32.4 all-gather.12
  81.4 32.4 all-gather.10
  115.6 32.4 all-gather.14
  149.8 74.0 all-gather.6
  225.7 74.0 all-gather.8
  303.8 62.3 reduce-scatter.12
  370.2 62.3 reduce-scatter.6
  436.6 62.6 reduce-scatter.8
  503.2 62.3 reduce-scatter.10
  569.8 159.4 reduce-scatter.16
  733.5 159.4 reduce-scatter.14
where the time goes:
time: 1430 us; the launch traced here: 1420 us
  blocking collectives  758 us (53%)
  matrix products  471 us (33%)
  other arithmetic  92 us (6%)
  waiting for transfers between devices  60.6 us (4%)
  local copies, waits for them, and re-layouts  24.8 us (2%)
  between operations  14.9 us (1%)
    psum x1, blocking collectives, local_step(): d_normed = lax.psum(d_normed, 'tp')  695 us
    dot_general x1, matrix products, local_step(): jnp.einsum('btd,df->btf', normed, wu_full, preferred_element_type=fp32)  78.6 us
    dot_general x1, matrix products, local_step(): jnp.einsum('btd,fd->btf', grad_y, wd_full, preferred_element_type=fp32)  43.4 us
    dot_general x3, matrix products, project(): jnp.einsum('btd,dn->btn', normed, weight, preferred_element_type=fp32)  40.9 us
    psum x1, blocking collectives, local_step(): lax.psum(grad_q_scale, ('tp', 'fsdp'))  39.5 us
    dot_general x1, matrix products, local_step(): jnp.einsum('btd,btf->df', normed, d_hidden, preferred_element_type=fp32)  36.8 us
    reduce_sum x4, other arithmetic, scaled_norm(): return centred * lax.rsqrt(row_var + EPS) * scale_vec  36.8 us
    dot_general x1, matrix products, local_step(): jnp.einsum('btf,btd->fd', act_out, grad_y, preferred_element_type=fp32)  36.6 us
  transfers between devices with their start and end apart: 12, of which 3 were waited for; matrix products, arithmetic and copies ran while one was open for 41% of the time, Pallas kernels for 0%

commit v1 on v0

v1 whole, which is shorter than its diff:
```python
import functools
import jax
import jax.numpy as jnp
from jax import lax
from jax.experimental import pallas as pl
from jax.experimental.pallas import tpu as pltpu
from jax.sharding import PartitionSpec as P

EPS = 1e-6


MESH = pl.DeviceIdType.MESH
SKEW = 2
SLOTS = 4
STEP = 32
COLS = 256
P_SLOTS, R0, R1, R2 = 6, 3, 4, 4
TILE = 512


def flipped(index, rel):
    out = index
    for bit in (1, 2, 4):
        if rel & bit:
            out = out + bit - 2 * bit * lax.rem(index // bit, 2)
    return out


def remote(src, dst, send, recv, where):
    return pltpu.make_async_remote_copy(src_ref=src, dst_ref=dst, send_sem=send, recv_sem=recv,
                                        device_id=where, device_id_type=MESH)


def fused_kernel(cfg, h_hbm, dy_hbm, x_hbm, dna_hbm, ht_hbm, dyt_hbm, wu_hbm, wdt_hbm, bias, scale, b_sum, gq, gk,
                 gx, g_up, g_dn, act_hbm, dh_hbm, dn_hbm, small_out,
                 wu, wdt, hb, yb, actb, dhb, gb, psum, s0, r0, r1, r2, bblk,
                 part, part2, xb, dyb, recv, sbuf, dxb, ln_acc, pack, rs_f, rs_t,
                 w_sem, hb_sem, out_sem, dn_sem, b_sem, s0_send, r0_sem, d_send, r1_sem, xy_send, r2_sem, g_sem,
                 c0, c1, c2,
                 part_sem, part2_sem, x_sem, dy_sem, fsend, frecv, bsend, brecv, lsem, credit, xs_send, xs_recv):
    n_tp, n_fsdp, n_img, n_tok = cfg
    f32, bf16 = jnp.float32, jnp.bfloat16
    rows, width = h_hbm.shape
    n_hid = wu_hbm.shape[1]
    blk = width // n_fsdp
    half = blk // 2
    me = lax.axis_index('fsdp')
    my_tp = lax.axis_index('tp')
    last = n_tp - 1
    rows_half = rows // 2
    n_chunk = rows_half // STEP
    sib = {'fsdp': flipped(me, 1)}
    nbr = ({'fsdp': flipped(me, 2)}, {'fsdp': flipped(me, 4)})

    load_w = [pltpu.make_async_copy(wu_hbm, wu.at[:, pl.ds(0, n_hid)], w_sem.at[0]),
              pltpu.make_async_copy(wdt_hbm, wdt.at[:, pl.ds(0, n_hid)], w_sem.at[1])]
    for c in load_w:
        c.start()
    barrier = pltpu.get_barrier_semaphore()
    for rel in range(1, n_fsdp):
        pl.semaphore_signal(barrier, inc=1, device_id={'fsdp': flipped(me, rel)}, device_id_type=MESH)
    for rel in range(1, n_tp):
        pl.semaphore_signal(barrier, inc=1, device_id={'tp': flipped(my_tp, rel)}, device_id_type=MESH)
    pl.semaphore_wait(barrier, n_fsdp + n_tp - 2)
    ln_acc[...] = jnp.zeros_like(ln_acc)
    gb[...] = jnp.zeros_like(gb)

    def rows_at(side, k):
        return pl.ds(pl.multiple_of(side * rows_half + k * STEP, STEP), STEP)

    def side_ends(side):
        pos = my_tp if side == 0 else last - my_tp
        nxt = {'tp': my_tp + 1 if side == 0 else my_tp - 1}
        prv = {'tp': my_tp - 1 if side == 0 else my_tp + 1}
        return pos, nxt, prv

    def part_loads(side, k):
        slot = lax.rem(k, 2)
        return [pltpu.make_async_copy(dn_hbm.at[rows_at(side, k)], part.at[side, slot], part_sem.at[side, slot]),
                pltpu.make_async_copy(dna_hbm.at[rows_at(side, k)], part2.at[side, slot], part2_sem.at[side, slot])]

    def root_loads(side, k):
        slot = lax.rem(k, 2)
        return [pltpu.make_async_copy(x_hbm.at[rows_at(side, k)], xb.at[side, slot], x_sem.at[side, slot]),
                pltpu.make_async_copy(dy_hbm.at[rows_at(side, k)], dyb.at[side, slot], dy_sem.at[side, slot])]

    def fsend_at(side, k):
        return remote(sbuf.at[side, lax.rem(k, 2)], recv.at[side, lax.rem(k, SLOTS)],
                      fsend.at[side, lax.rem(k, 2)], frecv.at[side, lax.rem(k, SLOTS)], side_ends(side)[1])

    def back_at(side, k):
        return remote(dxb.at[side, lax.rem(k, 2)], gx.at[rows_at(side, k)],
                      bsend.at[side, lax.rem(k, 2)], brecv.at[side, k], side_ends(side)[2])

    def relay_at(side, k):
        return remote(gx.at[rows_at(side, k)], gx.at[rows_at(side, k)],
                      bsend.at[side, lax.rem(k, 2)], brecv.at[side, k], side_ends(side)[2])

    def local_at(side, k):
        return pltpu.make_async_copy(dxb.at[side, lax.rem(k, 2)], gx.at[rows_at(side, k)], lsem.at[side, lax.rem(k, 2)])

    def chain_step(side, i):
        pos, nxt, prv = side_ends(side)
        k = i - 3 - 2 * side - SKEW * pos

        @pl.when((k + 1 >= 0) & (k + 1 < n_chunk))
        def _():
            for c in part_loads(side, k + 1):
                c.start()

            @pl.when(pos == last)
            def _():
                for c in root_loads(side, k + 1):
                    c.start()

        @pl.when((k >= 0) & (k < n_chunk))
        def _():
            slot = lax.rem(k, 2)
            for c in part_loads(side, k):
                c.wait()

            @pl.when(pos > 0)
            def _():
                fsend_at(side, k).wait_recv()

            @pl.when(pos < last)
            def _():
                @pl.when(k >= 2)
                def _():
                    fsend_at(side, k).wait_send()

                @pl.when(pos == 0)
                def _():
                    sbuf[side, slot] = part[side, slot] + part2[side, slot]

                @pl.when(pos > 0)
                def _():
                    sbuf[side, slot] = part[side, slot] + part2[side, slot] + recv[side, lax.rem(k, SLOTS)]

                @pl.when(k >= SLOTS)
                def _():
                    pl.semaphore_wait(credit.at[side], 1)
                fsend_at(side, k).start()

            @pl.when(pos == last)
            def _():
                for c in root_loads(side, k):
                    c.wait()

                @pl.when(k >= 2)
                def _():
                    back_at(side, k).wait_send()
                    local_at(side, k).wait()
                val = part[side, slot] + part2[side, slot] + recv[side, lax.rem(k, SLOTS)]
                d = val.astype(bf16).astype(f32)
                xv = xb[side, slot].astype(f32)
                cen = xv - jnp.mean(xv, axis=-1, keepdims=True)
                inv = lax.rsqrt(jnp.mean(cen * cen, axis=-1, keepdims=True) + EPS)
                xh = cen * inv
                dxh = d * xh
                ln_acc[...] += jnp.sum(dxh.reshape(STEP // 8, 8, width), axis=0)
                w = d * scale[...]
                mean_w = jnp.mean(w, axis=-1, keepdims=True)
                mean_wx = jnp.mean(w * xh, axis=-1, keepdims=True)
                d_x = inv * (w - mean_w - xh * mean_wx)
                dxb[side, slot] = (dyb[side, slot].astype(f32) + d_x).astype(bf16)
                back_at(side, k).start()
                local_at(side, k).start()

            @pl.when((pos > 0) & (k < n_chunk - SLOTS))
            def _():
                pl.semaphore_signal(credit.at[side], inc=1, device_id=prv, device_id_type=MESH)

        kb = i - 3 - 2 * side - SKEW * last - SKEW * (last - pos)

        @pl.when((pos < last) & (kb >= 0) & (kb < n_chunk))
        def _():
            relay_at(side, kb).wait_recv()

            @pl.when(pos > 0)
            def _():
                @pl.when(kb >= 2)
                def _():
                    relay_at(side, kb).wait_send()
                relay_at(side, kb).start()

    def image_rows(i):
        img = lax.rem(i, 2) * (n_img // 2) + i // 2
        return pl.ds(pl.multiple_of(img * n_tok, n_tok), n_tok)

    def image_loads(i):
        slot = lax.rem(i, 2)
        return [pltpu.make_async_copy(h_hbm.at[image_rows(i)], hb.at[slot], hb_sem.at[0, slot]),
                pltpu.make_async_copy(dy_hbm.at[image_rows(i)], yb.at[slot], hb_sem.at[1, slot])]

    def image_outs(i):
        return [pltpu.make_async_copy(actb, act_hbm.at[image_rows(i)], out_sem.at[0]),
                pltpu.make_async_copy(dhb, dh_hbm.at[image_rows(i)], out_sem.at[1])]

    n_tiles = width // COLS
    per_slot = psum.shape[1] // n_tok

    def dn_stage(i, t):
        slots = -(-n_tiles // per_slot)
        slot = lax.rem(i, P_SLOTS // slots) * slots + t // per_slot
        return slot, pl.ds((t % per_slot) * n_tok, n_tok)

    def dn_out(i, t):
        slot, where = dn_stage(i, t)
        return pltpu.make_async_copy(psum.at[slot, where], dn_hbm.at[image_rows(i), pl.ds(t * COLS, COLS)], dn_sem.at[t])

    def finish_image(i):
        for c in image_outs(i):
            c.wait()
        for t in range(n_tiles):
            dn_out(i, t).wait()

    def mlp_hidden(i):
        slot = lax.rem(i, 2)

        @pl.when(i + 1 < n_img)
        def _():
            for c in image_loads(i + 1):
                c.start()
        for c in image_loads(i):
            c.wait()
        tile = min(TILE, n_hid)
        for f in range(0, n_hid, tile):
            cols = pl.ds(f, tile)
            u = (jnp.dot(hb[slot], wu[:, cols], preferred_element_type=f32) + bias[:, cols]).astype(bf16).astype(f32)
            d_act = jnp.dot(yb[slot], wdt[:, cols], preferred_element_type=f32).astype(bf16).astype(f32)
            cdf = 0.5 * (1.0 + lax.erf(u * (0.5 ** 0.5)))
            actb[:, cols] = (u * cdf).astype(bf16)
            slope = cdf + u * (jnp.exp(-0.5 * u * u) * (1.0 / (2.0 * jnp.pi) ** 0.5))
            d_u = (d_act * slope).astype(bf16)
            dhb[:, cols] = d_u
            gb[:, cols] += jnp.sum(d_u.astype(f32).reshape(-1, 8, tile), axis=0)
        for c in image_outs(i):
            c.start()

    def mlp_back(i):
        for t in range(n_tiles):
            stage, where = dn_stage(i, t)
            psum[stage, where] = lax.dot_general(dhb[...], wu[pl.ds(t * COLS, COLS), pl.ds(0, n_hid)],
                                                 (((1,), (1,)), ((), ())), preferred_element_type=f32)
            dn_out(i, t).start()

    for c in image_loads(0):
        c.start()
    for c in load_w:
        c.wait()

    def phase1(i, carry):
        @pl.when(i > 0)
        def _():
            finish_image(i - 1)
        for side in range(2):
            chain_step(side, 2 * i)
        mlp_hidden(i)
        for side in range(2):
            chain_step(side, 2 * i + 1)
        mlp_back(i)
        return carry

    lax.fori_loop(0, n_img, phase1, 0)
    finish_image(n_img - 1)

    load_t = [pltpu.make_async_copy(ht_hbm, wu.at[:, pl.ds(0, rows)], w_sem.at[0]),
              pltpu.make_async_copy(dyt_hbm, wdt.at[:, pl.ds(0, rows)], w_sem.at[1])]
    for c in load_t:
        c.start()
    per_group = n_hid // COLS
    n_blocks = 2 * per_group

    def cols_at(j):
        return pl.ds(pl.multiple_of(lax.rem(j, per_group) * COLS, COLS), COLS)

    def start_block(j):
        slot = lax.rem(j, 2)

        @pl.when(j < per_group)
        def _():
            pltpu.make_async_copy(dh_hbm.at[:, cols_at(j)], bblk.at[slot], b_sem.at[slot]).start()

        @pl.when(j >= per_group)
        def _():
            pltpu.make_async_copy(act_hbm.at[:, cols_at(j)], bblk.at[slot], b_sem.at[slot]).start()

    def wait_block(j):
        slot = lax.rem(j, 2)
        pltpu.make_async_copy(dh_hbm.at[:, cols_at(j)], bblk.at[slot], b_sem.at[slot]).wait()

    def s0_at(j):
        return remote(s0.at[lax.rem(j, 2)], r0.at[lax.rem(j, R0)], s0_send.at[lax.rem(j, 2)],
                      r0_sem.at[lax.rem(j, R0)], sib)

    def diag_at(j, d):
        return remote(psum.at[lax.rem(j, P_SLOTS), pl.ds(3 * blk + d * half, half)], r1.at[d, lax.rem(j, R1)],
                      d_send.at[d, lax.rem(j, P_SLOTS)], r1_sem.at[d, lax.rem(j, R1)], nbr[d])

    def near_at(j, d):
        return remote(psum.at[lax.rem(j, P_SLOTS), pl.ds((1 + d) * blk, blk)], r2.at[d, lax.rem(j, R2)],
                      xy_send.at[d, lax.rem(j, P_SLOTS)], r2_sem.at[d, lax.rem(j, R2)], nbr[d])

    def grad_out(j, ref):
        return pltpu.make_async_copy(psum.at[lax.rem(j, P_SLOTS), pl.ds(0, blk)], ref.at[:, cols_at(j)],
                                     g_sem.at[lax.rem(j, P_SLOTS)])
    def free_slot(j):
        for d in range(2):
            diag_at(j, d).wait_send()
            near_at(j, d).wait_send()
        grad_out(j, g_up).wait()

    def stage_a(j):
        @pl.when(j + 1 < n_blocks)
        def _():
            start_block(j + 1)
        wait_block(j)

        @pl.when(j == per_group)
        def _():
            load_t[1].wait()

        @pl.when(j >= 2)
        def _():
            s0_at(j).wait_send()

        @pl.when(j >= P_SLOTS)
        def _():
            free_slot(j - P_SLOTS)
        slot = lax.rem(j, P_SLOTS)

        def dots(lhs):
            rhs = bblk[lax.rem(j, 2)]
            for q in range(4):
                for odd in (1, 0):
                    where = pl.ds(pl.multiple_of(flipped(me, 2 * q + odd) * blk, blk), blk)
                    val = jnp.dot(lhs[where, pl.ds(0, rows)], rhs, preferred_element_type=f32)
                    if odd:
                        s0[lax.rem(j, 2), pl.ds(q * blk, blk)] = val
                    else:
                        psum[slot, pl.ds(q * blk, blk)] = val

        @pl.when(j < per_group)
        def _():
            dots(wu)

        @pl.when(j >= per_group)
        def _():
            dots(wdt)

        @pl.when(j >= R0)
        def _():
            pl.semaphore_wait(c0, 1)
        s0_at(j).start()

    def stage_b(j):
        s0_at(j).wait_recv()
        psum[lax.rem(j, P_SLOTS)] += r0[lax.rem(j, R0)]

        @pl.when(j < n_blocks - R0)
        def _():
            pl.semaphore_signal(c0, inc=1, device_id=sib, device_id_type=MESH)
        for d in range(2):
            @pl.when(j >= R1)
            def _():
                pl.semaphore_wait(c1.at[d], 1)
            diag_at(j, d).start()

    def stage_c(j):
        slot = lax.rem(j, P_SLOTS)
        for d in range(2):
            diag_at(j, d).wait_recv()
            psum[slot, pl.ds((2 - d) * blk + d * half, half)] += r1[d, lax.rem(j, R1)]

            @pl.when(j < n_blocks - R1)
            def _():
                pl.semaphore_signal(c1.at[d], inc=1, device_id=nbr[d], device_id_type=MESH)
        for d in range(2):
            @pl.when(j >= R2)
            def _():
                pl.semaphore_wait(c2.at[d], 1)
            near_at(j, d).start()

    def stage_d(j):
        slot = lax.rem(j, P_SLOTS)
        for d in range(2):
            near_at(j, d).wait_recv()
        psum[slot, pl.ds(0, blk)] += r2[0, lax.rem(j, R2)] + r2[1, lax.rem(j, R2)]
        for d in range(2):
            @pl.when(j < n_blocks - R2)
            def _():
                pl.semaphore_signal(c2.at[d], inc=1, device_id=nbr[d], device_id_type=MESH)

        @pl.when(j < per_group)
        def _():
            grad_out(j, g_up).start()

        @pl.when(j >= per_group)
        def _():
            grad_out(j, g_dn).start()

    start_block(0)
    load_t[0].wait()

    def phase2(i, carry):
        j = i - n_img
        for lag, stage in ((5, stage_d), (3, stage_c)):
            @pl.when((j >= lag) & (j - lag < n_blocks))
            def _():
                stage(j - lag)
        for side in range(2):
            chain_step(side, n_img + i)

        @pl.when(j < n_blocks)
        def _():
            stage_a(j)

        @pl.when((j >= 1) & (j - 1 < n_blocks))
        def _():
            stage_b(j - 1)
        return carry

    n_iter = max(n_chunk + 5 + 2 * SKEW * last - n_img, n_img + n_blocks + 5)
    lax.fori_loop(n_img, n_iter, phase2, 0)

    for j in range(n_blocks - P_SLOTS, n_blocks):
        free_slot(j)
    for j in (n_blocks - 2, n_blocks - 1):
        s0_at(j).wait_send()
    for side in range(2):
        pos = side_ends(side)[0]
        for k in (n_chunk - 2, n_chunk - 1):
            @pl.when(pos < last)
            def _():
                fsend_at(side, k).wait_send()

            @pl.when((pos > 0) & (pos < last))
            def _():
                relay_at(side, k).wait_send()

            @pl.when(pos == last)
            def _():
                back_at(side, k).wait_send()
                local_at(side, k).wait()

    lanes = 128
    n_rows = pack.shape[0]
    tp_lo = n_rows - rs_t.shape[1]
    pack[...] = jnp.zeros_like(pack)
    gb_row = jnp.sum(gb[...], axis=0, keepdims=True)
    for j in range(n_hid // lanes):
        pack[pl.ds(j, 1), :] = gb_row[:, j * lanes:(j + 1) * lanes]
    ln_row = jnp.sum(ln_acc[...], axis=0, keepdims=True)
    bs_row = jnp.sum(b_sum[...], axis=0, keepdims=True)
    n_wide = width // lanes
    for j in range(n_wide):
        pack[pl.ds(tp_lo - n_wide + j, 1), :] = bs_row[:, j * lanes:(j + 1) * lanes]
        pack[pl.ds(tp_lo + j, 1), :] = ln_row[:, j * lanes:(j + 1) * lanes]
    for j, ref in enumerate((gq, gk)):
        pack[pl.ds(tp_lo + n_wide + j, 1), pl.ds(0, ref.shape[0])] = jnp.sum(ref[...].T, axis=0, keepdims=True)

    def to_fsdp(rel):
        return remote(pack, rs_f.at[rel - 1], xs_send.at[rel - 1], xs_recv.at[rel - 1], {'fsdp': flipped(me, rel)})

    for rel in range(1, n_fsdp):
        to_fsdp(rel).start()
    for rel in range(1, n_fsdp):
        to_fsdp(rel).wait()

    def tree(terms):
        while len(terms) > 1:
            terms = [terms[j] + terms[j + 1] for j in range(0, len(terms), 2)]
        return terms[0]

    pack[...] = tree([pack[...]] + [rs_f[rel - 1] for rel in range(1, n_fsdp)])

    def to_tp(rel):
        return remote(pack.at[pl.ds(tp_lo, n_rows - tp_lo)], rs_t.at[rel - 1], xs_send.at[n_fsdp + rel - 2],
                      xs_recv.at[n_fsdp + rel - 2], {'tp': flipped(my_tp, rel)})

    for rel in range(1, n_tp):
        to_tp(rel).start()
    for rel in range(1, n_tp):
        to_tp(rel).wait()
    small_out[...] = pack[...]
    small_out[pl.ds(tp_lo, n_rows - tp_lo), :] = tree(
        [pack[pl.ds(tp_lo, n_rows - tp_lo)]] + [rs_t[rel - 1] for rel in range(1, n_tp)])


def small_rows(n_hid, width):
    n_up, n_wide = n_hid // 128, width // 128
    return n_up, n_wide, n_wide + 2 + -(n_up + 2 * n_wide + 2) % 8


def fused_call(mesh, normed, dy, x2, dn_attn, normed_t, dy_t, wu, wdt, b_up, ln_scale, b_sum, gq, gk, n_img):
    rows, width = x2.shape
    pack_up, pack_wide, tp_rows = small_rows(wu.shape[1], width)
    pack_shape = (pack_up + pack_wide + tp_rows, 128)
    n_hid = wu.shape[1]
    n_tok = rows // n_img
    n_tp, n_fsdp = mesh.shape['tp'], mesh.shape['fsdp']
    blk = width // n_fsdp
    n_chunk = rows // 2 // STEP
    f32, bf16 = jnp.float32, jnp.bfloat16
    dma = pltpu.SemaphoreType.DMA
    reg = pltpu.SemaphoreType.REGULAR
    vm = pltpu.VMEM
    any_spec = pl.BlockSpec(memory_space=pl.ANY)
    vmem = pl.BlockSpec(memory_space=pltpu.VMEM)
    shape = jax.ShapeDtypeStruct
    lane = max(n_hid, rows)
    kern = functools.partial(fused_kernel, (n_tp, n_fsdp, n_img, n_tok))
    return pl.pallas_call(
        kern,
        out_shape=(shape((rows, width), bf16), shape((blk, n_hid), f32), shape((blk, n_hid), f32),
                   shape((rows, n_hid), bf16), shape((rows, n_hid), bf16), shape((rows, width), f32),
                   shape(pack_shape, f32)),
        in_specs=[any_spec] * 8 + [vmem] * 5,
        out_specs=(any_spec,) * 6 + (vmem,),
        scratch_shapes=[
            vm((width, lane), bf16), vm((width, lane), bf16),
            vm((2, n_tok, width), bf16), vm((2, n_tok, width), bf16),
            vm((n_tok, n_hid), bf16), vm((n_tok, n_hid), bf16),
            vm((8, n_hid), f32),
            vm((P_SLOTS, 4 * blk, COLS), f32),
            vm((2, 4 * blk, COLS), f32), vm((R0, 4 * blk, COLS), f32),
            vm((2, R1, blk // 2, COLS), f32), vm((2, R2, blk, COLS), f32),
            vm((2, rows, COLS), bf16),
            vm((2, 2, STEP, width), f32), vm((2, 2, STEP, width), f32),
            vm((2, 2, STEP, width), bf16), vm((2, 2, STEP, width), bf16),
            vm((2, SLOTS, STEP, width), f32), vm((2, 2, STEP, width), f32),
            vm((2, 2, STEP, width), bf16),
            vm((8, width), f32), vm(pack_shape, f32),
            vm((n_fsdp - 1,) + pack_shape, f32), vm((n_tp - 1, tp_rows, 128), f32),
            dma((2,)), dma((2, 2)), dma((2,)), dma((width // COLS,)), dma((2,)),
            dma((2,)), dma((R0,)), dma((2, P_SLOTS)), dma((2, R1)),
            dma((2, P_SLOTS)), dma((2, R2)), dma((P_SLOTS,)),
            reg, reg((2,)), reg((2,)),
            dma((2, 2)), dma((2, 2)), dma((2, 2)), dma((2, 2)),
            dma((2, 2)), dma((2, SLOTS)), dma((2, 2)), dma((2, n_chunk)), dma((2, 2)),
            reg((2,)), dma((n_fsdp + n_tp - 2,)), dma((n_fsdp + n_tp - 2,)),
        ],
        compiler_params=pltpu.CompilerParams(collective_id=0, has_side_effects=True, vmem_limit_bytes=67_043_328),
        cost_estimate=pl.CostEstimate(flops=200_000_000_000, bytes_accessed=200_000_000, transcendentals=0),
        name='mlp_chain',
    )(normed, dy, x2, dn_attn, normed_t, dy_t, wu, wdt, b_up.reshape(1, n_hid), ln_scale.reshape(1, width), b_sum, gq, gk)


def attn_kernel(n_heads, head_dim, qkv, do, qs, ks, o_out, dqkv, gq, gk):
    f32, bf16 = jnp.float32, jnp.bfloat16
    scale = head_dim ** -0.5
    n_feat = n_heads * head_dim

    @pl.when(pl.program_id(0) == 0)
    def _():
        gq[...] = jnp.zeros_like(gq)
        gk[...] = jnp.zeros_like(gk)

    def norm(raw):
        cen = raw - jnp.mean(raw, axis=0, keepdims=True)
        inv = lax.rsqrt(jnp.mean(cen * cen, axis=0, keepdims=True) + EPS)
        return cen * inv, inv

    def norm_back(d, hat, inv, gain):
        w = d * gain
        return inv * (w - jnp.mean(w, axis=0, keepdims=True) - hat * jnp.mean(w * hat, axis=0, keepdims=True))

    def mm(lhs, rhs, dims):
        return lax.dot_general(lhs, rhs, (dims, ((), ())), preferred_element_type=f32)

    for h in range(n_heads):
        lo = h * head_dim
        q_rows, k_rows, v_rows = (pl.ds(j * n_feat + lo, head_dim) for j in range(3))
        q_hat, q_inv = norm(qkv[q_rows, :].astype(f32))
        k_hat, k_inv = norm(qkv[k_rows, :].astype(f32))
        qn = (q_hat * qs[...]).astype(bf16)
        kn = (k_hat * ks[...]).astype(bf16)
        v = qkv[v_rows, :]
        d_o = do[pl.ds(lo, head_dim), :]
        logits = mm(kn, qn, ((0,), (0,))) * scale
        e = jnp.exp(logits - jnp.max(logits, axis=0, keepdims=True))
        p = e * (1.0 / jnp.sum(e, axis=0, keepdims=True))
        pb = p.astype(bf16)
        o_out[pl.ds(lo, head_dim), :] = mm(v, pb, ((1,), (0,))).astype(bf16)
        dqkv[v_rows, :] = mm(d_o, pb, ((1,), (1,))).astype(bf16)
        dp = mm(v, d_o, ((0,), (0,))).astype(bf16).astype(f32)
        ds = (p * (dp - jnp.sum(p * dp, axis=0, keepdims=True)) * scale).astype(bf16)
        dqn = mm(kn, ds, ((1,), (0,))).astype(bf16).astype(f32)
        dkn = mm(qn, ds, ((1,), (1,))).astype(bf16).astype(f32)
        gq[...] += dqn * q_hat
        gk[...] += dkn * k_hat
        dqkv[q_rows, :] = norm_back(dqn, q_hat, q_inv, qs[...]).astype(bf16)
        dqkv[k_rows, :] = norm_back(dkn, k_hat, k_inv, ks[...]).astype(bf16)


def attn_call(qkv_t, do_t, q_scale, k_scale, n_img):
    n_feat, rows = do_t.shape
    head_dim = q_scale.shape[0]
    n_tok = rows // n_img
    f32, bf16 = jnp.float32, jnp.bfloat16
    col = lambda n: pl.BlockSpec((n, n_tok), lambda i: (0, i))
    whole = lambda shape: pl.BlockSpec(shape, lambda i: (0, 0))
    n_heads = n_feat // head_dim
    return pl.pallas_call(
        functools.partial(attn_kernel, n_heads, head_dim),
        grid=(n_img,),
        out_shape=(jax.ShapeDtypeStruct((n_feat, rows), bf16), jax.ShapeDtypeStruct((3 * n_feat, rows), bf16),
                   jax.ShapeDtypeStruct((head_dim, n_tok), f32), jax.ShapeDtypeStruct((head_dim, n_tok), f32)),
        in_specs=[col(3 * n_feat), col(n_feat), whole((head_dim, 1)), whole((head_dim, 1))],
        out_specs=(col(n_feat), col(3 * n_feat), whole((head_dim, n_tok)), whole((head_dim, n_tok))),
        compiler_params=pltpu.CompilerParams(dimension_semantics=('arbitrary',), vmem_limit_bytes=32 << 20),
        cost_estimate=pl.CostEstimate(flops=25_000_000_000, bytes_accessed=8 * n_feat * rows * 2,
                                      transcendentals=n_img * n_heads * n_tok * n_tok),
        name='attention',
    )(qkv_t, do_t, q_scale.reshape(head_dim, 1), k_scale.reshape(head_dim, 1))


def outer_kernel(n_qkv_tiles, h_t, dy_t, dqkv_t, o_t, out):
    n = pl.program_id(0)

    def nt(lhs, rhs):
        return lax.dot_general(lhs[...], rhs[...], (((1,), (1,)), ((), ())), preferred_element_type=jnp.float32)

    @pl.when(n < n_qkv_tiles)
    def _():
        out[...] = nt(h_t, dqkv_t)

    @pl.when(n >= n_qkv_tiles)
    def _():
        out[...] = nt(dy_t, o_t)


def attn_grads_call(h_t, dy_t, d_qkv_t, o_t):
    width, rows = h_t.shape
    n_feat = o_t.shape[0]
    tile = 256
    q_tiles = d_qkv_t.shape[0] // n_feat
    return pl.pallas_call(
        functools.partial(outer_kernel, q_tiles),
        grid=(q_tiles + 1, width // tile),
        out_shape=jax.ShapeDtypeStruct((width, (q_tiles + 1) * n_feat), jnp.float32),
        in_specs=[pl.BlockSpec((tile, rows), lambda n, d: (jnp.where(n < q_tiles, d, width // tile - 1), 0)),
                  pl.BlockSpec((tile, rows), lambda n, d: (jnp.where(n < q_tiles, 0, d), 0)),
                  pl.BlockSpec((n_feat, rows), lambda n, d: (jnp.minimum(n, q_tiles - 1), 0)),
                  pl.BlockSpec((n_feat, rows), lambda n, d: (0, 0))],
        out_specs=pl.BlockSpec((tile, n_feat), lambda n, d: (d, n)),
        compiler_params=pltpu.CompilerParams(dimension_semantics=('arbitrary', 'arbitrary'), vmem_limit_bytes=40 << 20),
        cost_estimate=pl.CostEstimate(flops=2 * width * rows * (q_tiles + 1) * n_feat, bytes_accessed=100_000_000,
                                      transcendentals=0),
        name='attn_grads',
    )(h_t, dy_t, d_qkv_t, o_t)


def prep_kernel(n_fsdp, n_img, x, dy, gain, wq, wk, wv, wo_t, h, h_t, dy_t, b_sum, w_full, shard, own_sem, put_sem,
                send, got, half_send, half_got, sib_send, sib_got):
    f32, bf16 = jnp.float32, jnp.bfloat16
    i = pl.program_id(0)
    me = lax.axis_index('fsdp')
    blk = shard.shape[0]
    half = blk // 2
    sib = {'fsdp': flipped(me, 1)}
    nbr = ({'fsdp': flipped(me, 2)}, {'fsdp': flipped(me, 4)})
    pieces = (wq, wk, wv, wo_t)

    def rows_of(rel):
        return pl.ds(pl.multiple_of(flipped(me, rel) * blk, blk), blk)

    def half_of(rel, d):
        return pl.ds(pl.multiple_of(flipped(me, rel) * blk + d * half, half), half)

    def load(j):
        n = pieces[j].shape[1]
        return pltpu.make_async_copy(pieces[j], shard.at[:, pl.ds(j * n, n)], own_sem.at[j])

    def put():
        return pltpu.make_async_copy(shard, w_full.at[rows_of(0)], put_sem)

    def own_to(d):
        return remote(shard, w_full.at[rows_of(0)], send.at[d], got.at[d], nbr[d])

    def half_to(d):
        rel = 4 - 2 * d
        return remote(w_full.at[half_of(rel, 1 - d)], w_full.at[half_of(rel, 1 - d)], half_send.at[d], half_got.at[d],
                      nbr[d])

    def to_sib(q):
        src = shard if q == 0 else w_full.at[rows_of(2 * q)]
        return remote(src, w_full.at[rows_of(2 * q)], sib_send.at[q], sib_got.at[q], sib)

    @pl.when(i == 0)
    def _():
        for j in range(4):
            load(j).start()
        barrier = pltpu.get_barrier_semaphore()
        for where in (sib,) + nbr:
            pl.semaphore_signal(barrier, inc=1, device_id=where, device_id_type=MESH)
        pl.semaphore_wait(barrier, 3)
        for j in range(4):
            load(j).wait()
        for d in range(2):
            own_to(d).start()
        to_sib(0).start()
        put().start()
        b_sum[...] = jnp.zeros_like(b_sum)

    width = x.shape[1]
    xv = x[...].astype(f32)
    cen = xv - jnp.mean(xv, axis=-1, keepdims=True)
    inv = lax.rsqrt(jnp.mean(cen * cen, axis=-1, keepdims=True) + EPS)
    hv = (cen * inv * gain[...]).astype(bf16)
    h[...] = hv
    h_t[...] = hv.T
    dv = dy[...]
    dy_t[...] = dv.T
    b_sum[...] += jnp.sum(dv.astype(f32).reshape(-1, 8, width), axis=0)

    @pl.when(i == n_img - 1)
    def _():
        own_to(0).wait_recv()
        half_to(1).start()
        to_sib(1).start()
        own_to(1).wait_recv()
        half_to(0).start()
        to_sib(2).start()
        half_to(0).wait_recv()
        half_to(1).wait_recv()
        to_sib(3).start()
        put().wait()
        for d in range(2):
            own_to(d).wait_send()
            half_to(d).wait_send()
        for q in range(4):
            to_sib(q).wait()


def prep_call(mesh, x2, dy, ln_scale, attn_weights, n_img):
    rows, width = x2.shape
    n_tok = rows // n_img
    n_fsdp = mesh.shape['fsdp']
    blk = attn_weights[0].shape[0]
    n_all = sum(w.shape[1] for w in attn_weights)
    f32, bf16 = jnp.float32, jnp.bfloat16
    dma = pltpu.SemaphoreType.DMA
    row = pl.BlockSpec((n_tok, width), lambda i: (i, 0))
    col = pl.BlockSpec((width, n_tok), lambda i: (0, i))
    any_spec = pl.BlockSpec(memory_space=pl.ANY)
    shape = jax.ShapeDtypeStruct
    return pl.pallas_call(
        functools.partial(prep_kernel, n_fsdp, n_img),
        grid=(n_img,),
        out_shape=(shape((rows, width), bf16), shape((width, rows), bf16), shape((width, rows), bf16),
                   shape((8, width), f32), shape((width, n_all), bf16)),
        in_specs=[row, row, pl.BlockSpec((1, width), lambda i: (0, 0))] + [any_spec] * 4,
        out_specs=(row, col, col, pl.BlockSpec((8, width), lambda i: (0, 0)), any_spec),
        scratch_shapes=[pltpu.VMEM((blk, n_all), bf16), dma((4,)), dma, dma((2,)), dma((2,)), dma((2,)), dma((2,)),
                        dma((4,)), dma((4,))],
        compiler_params=pltpu.CompilerParams(dimension_semantics=('arbitrary',), collective_id=1, has_side_effects=True,
                                             vmem_limit_bytes=48 << 20),
        cost_estimate=pl.CostEstimate(flops=60_000_000_000, bytes_accessed=10 * rows * width, transcendentals=0),
        name='prep',
    )(x2, dy, ln_scale.reshape(1, width), *attn_weights)


def solution(mesh):
    act_spec = P('fsdp', None, None)
    row_spec = P('fsdp', 'tp')
    col_spec = P('tp', 'fsdp')
    in_specs = (act_spec, act_spec, row_spec, row_spec, row_spec, col_spec, row_spec, P('tp'), col_spec, P(), P(), P())
    out_specs = (act_spec, row_spec, row_spec, row_spec, col_spec, row_spec, P('tp'), col_spec, P(), P(), P(), P())
    gather_rows = functools.partial(lax.all_gather, axis_name='fsdp', axis=0, tiled=True)
    scatter_rows = functools.partial(lax.psum_scatter, axis_name='fsdp', scatter_dimension=0, tiled=True)

    def local_step(x_in, grad_y, w_query, w_key, w_value, w_out, w_up, b_up, w_down, ln_scale, q_scale, k_scale):
        bf16 = jnp.bfloat16
        fp32 = jnp.float32
        head_dim = q_scale.shape[0]
        num_img = x_in.shape[0]
        num_tok = x_in.shape[1]
        num_rows = num_img * num_tok
        width = x_in.shape[2]
        n_qkv = w_query.shape[1]

        x2 = x_in.reshape(num_rows, width)
        dy = grad_y.reshape(num_rows, width)
        normed, normed_t, dy_t, b_sum, attn_full = prep_call(
            mesh, x2, dy, ln_scale, (w_query, w_key, w_value, w_out.T), num_img)
        wqkv_full = attn_full[:, :3 * n_qkv]
        wot_full = attn_full[:, 3 * n_qkv:]
        w_up, w_down_t, attn_full = lax.optimization_barrier((w_up, w_down.T, attn_full))
        wu_full = gather_rows(w_up)
        wdt_full = gather_rows(w_down_t)

        def contract(lhs, rhs, dim):
            return lax.dot_general(lhs, rhs, (((dim,), (dim,)), ((), ())), preferred_element_type=fp32)

        qkv_t = contract(wqkv_full, normed_t, 0).astype(bf16)
        d_attn_t = contract(wot_full, dy_t, 0).astype(bf16)
        attn_t, d_qkv_t, gq, gk = attn_call(qkv_t, d_attn_t, q_scale, k_scale, num_img)
        grad_w_attn = attn_grads_call(normed_t, dy_t, d_qkv_t, attn_t)
        d_normed = lax.dot_general(d_qkv_t, wqkv_full, (((0,), (1,)), ((), ())), preferred_element_type=fp32)

        grad_x, g_up, g_down_t, _, _, _, small = fused_call(
            mesh, normed, dy, x2, d_normed, normed_t, dy_t, wu_full, wdt_full, b_up, ln_scale, b_sum, gq, gk, num_img)
        n_up, n_wide, _ = small_rows(wu_full.shape[1], width)
        tp_lo = n_up + n_wide
        q_lo = tp_lo + n_wide
        g_attn = scatter_rows(grad_w_attn)
        return (grad_x.reshape(x_in.shape), g_attn[:, :n_qkv], g_attn[:, n_qkv:2 * n_qkv], g_attn[:, 2 * n_qkv:3 * n_qkv],
                g_attn[:, 3 * n_qkv:].T, g_up, small[:n_up].reshape(-1),
                g_down_t.T, small[n_up:tp_lo].reshape(-1), small[tp_lo:q_lo].reshape(-1),
                small[q_lo, :head_dim], small[q_lo + 1, :head_dim])

    return jax.shard_map(local_step, mesh=mesh, in_specs=in_specs, out_specs=out_specs, check_vma=False)
```

time: 1430 us -> 718 us (0.50)
  blocking collectives: 758 us -> 0 us
  Pallas kernels: 0 us -> 594 us
  matrix products: 471 us -> 67 us
  other arithmetic: 92 us -> 0 us
  waiting for transfers between devices: 60.6 us -> 0.73 us
    psum x3 -> x0, blocking collectives: 758 us -> none  [the longest x1 695 us: local_step(): d_normed = lax.psum(d_normed, 'tp')]
    pallas_call x0 -> x4, Pallas kernels: none -> 594 us  [the longest x1 419 us: fused_call(): pl.pallas_call(kern, out_shape=(shape((rows, width), bf16), shape((blk, n...]
    dot_general x21 -> x3, matrix products: 460 us -> 67 us  [the longest x2 37.9 us: contract(): lax.dot_general(lhs, rhs, (((dim,), (dim,)), ((), ())), preferred_element...]
    reduce_sum x11 -> x0, other arithmetic: 73.7 us -> none  [the longest x4 36.8 us: scaled_norm(): return centred * lax.rsqrt(row_var + EPS) * scale_vec]
    all_gather x5 -> x1, waiting for transfers between devices: 56.8 us -> 0.01 us  [local_step(): wdt_full = gather_rows(w_down_t)]
    unnamed x76 -> x31, local copies, waits for them, and re-layouts: 7.28 us -> 27.5 us
    convert_element_type x3 -> x0, other arithmetic: 18.1 us -> none  [the longest x1 7.48 us: local_step(): q_norm = qn_f.astype(bf16)]
    convert_element_type x4 -> x0, local copies, waits for them, and re-layouts: 17.5 us -> none  [the longest x1 6.04 us: local_step(): kn_f, k_pull = jax.vjp(scaled_norm, k_proj.astype(fp32), k_scale)]
  transfers between devices with their start and end apart: 12 -> 3, of which waited for: 3 -> 0; matrix products, arithmetic and copies ran while one was open for 41% -> 10% of each run, Pallas kernels for 0% -> 74%
where the time goes in v1:
time: 718 us; the launch traced here: 711 us
  Pallas kernels  594 us (83%)
  matrix products  67 us (9%)
  local copies, waits for them, and re-layouts  35.3 us (5%)
  between operations  14.2 us (2%)
    pallas_call x1, Pallas kernels, fused_call(): pl.pallas_call(kern, out_shape=(shape((rows, width), bf16), shape((blk, n...  419 us
    pallas_call x1, Pallas kernels, prep_call(): pl.pallas_call(functools.partial(prep_kernel, n_fsdp, n_img), grid=(n_img...  66.1 us
    pallas_call x1, Pallas kernels, attn_grads_call(): pl.pallas_call(functools.partial(outer_kernel, q_tiles), grid=(q_tiles +...  64.1 us
    pallas_call x1, Pallas kernels, attn_call(): pl.pallas_call(functools.partial(attn_kernel, n_heads, head_dim), grid=(n...  44.4 us
    dot_general x2, matrix products, contract(): lax.dot_general(lhs, rhs, (((dim,), (dim,)), ((), ())), preferred_element...  37.9 us
    dot_general x1, matrix products, local_step(): lax.dot_general(d_qkv_t, wqkv_full, (((0,), (1,)), ((), ())), preferred_e...  29 us
    unnamed x31, local copies, waits for them, and re-layouts  27.5 us
  transfers between devices with their start and end apart: 3, of which 0 were waited for; matrix products, arithmetic and copies ran while one was open for 10% of the time, Pallas kernels for 74%

profile of v1, /device:TPU:0, one launch (start us, length us, event | category | flops | bytes accessed | tf_op | source)
XLA Modules:
  0.0 711.4 jit_solution(4315594262644280454)
XLA Ops:
  7.2 0.0 all-gather.3.cloned.1.call-start
  7.2 0.7 reshape.57.gain.scale
  7.9 0.0 copy-start
  7.9 0.0 copy-start.1
  8.0 1.0 copy-done.1
  8.9 0.0 copy-start.2
  9.0 1.0 copy-done.2
  10.0 0.0 copy-start.3
  10.0 1.0 copy-done.3
  11.0 0.0 copy-start.4
  11.0 1.0 copy-done.4
  12.0 0.0 copy-start.12
  12.0 0.0 copy-start.13
  12.0 66.1 %prep.1 = (bf16[2048,2560]{1,0:T(8,128)(2,1)}, bf16[2560,2048]{1,0:T(8,128)(2,1)}, bf16[2560,2048]{1,0:T(8,128)(2,1)}, f32[8,2560]{1,0:T(8,128)S(1)}, bf16[2560,2560]{1,0:T(8,128)(2,1)}) custom-call(bf16[2048,2560]{1,0:T(8,128)(2,1)} %bitcast.29, bf16[2048,2560]{1,0:T(8,128)(2,1)} %bitcast.31, f32[1,2560]{1,0:T(1,128)S(1)} %reshape.57.gain.scale, ...), custom_call_target="tpu_custom_call" | custom-call | flops 60000002048 | bytes 52428800 | tf_op jit(solution)/shard_map/prep/pallas_call | solution.py:749
  78.1 0.0 copy-done
  78.1 0.0 copy-start.9
  78.1 0.6 copy-done.9
  78.7 0.0 all-gather.3.cloned.1.call-update
  78.7 0.0 all-gather.5.cloned.1.call-start
  78.8 0.7 all-gather.5.cloned.1.call-update
  79.5 0.0 reduce-scatter.2.cloned.1.call-start
  79.5 0.0 copy-done.12
  79.6 0.1 copy.24.qs
  79.7 0.0 copy-done.13
  79.7 0.1 copy.25.ks
  79.8 10.7 %fusion.9.do = bf16[640,2048]{1,0:T(8,128)(2,1)S(1)} fusion(bf16[2560,2048]{1,0:T(8,128)(2,1)} %get-tuple-element.30.dyt_hbm.dy_t, bf16[2560,2560]{1,0:T(8,128)(2,1)} %get-tuple-element.28), kind=kOutput, calls=%fused_computation.7 | convolution fusion | flops 6712197120 | bytes 16384000 | tf_op jit(solution)/shard_map/dot_general | solution.py:795
  90.5 27.2 %fusion.4.qkv = bf16[1920,2048]{1,0:T(8,128)(2,1)} fusion(bf16[2560,2048]{1,0:T(8,128)(2,1)} %get-tuple-element.29.ht_hbm.h_t, bf16[2560,2560]{1,0:T(8,128)(2,1)} %get-tuple-element.28), kind=kOutput, calls=%fused_computation.4 | convolution fusion | flops 20136591360 | bytes 28180480 | tf_op jit(solution)/shard_map/dot_general | solution.py:795
  117.7 0.0 copy-start.6
  117.7 3.2 copy-done.6
  120.9 44.4 %attention.1 = (bf16[640,2048]{1,0:T(8,128)(2,1)S(1)}, bf16[1920,2048]{1,0:T(8,128)(2,1)S(1)}, f32[80,256]{1,0:T(8,128)S(1)}, f32[80,256]{1,0:T(8,128)S(1)}) custom-call(bf16[1920,2048]{1,0:T(8,128)(2,1)S(1)} %copy-done.6, bf16[640,2048]{1,0:T(8,128)(2,1)S(1)} %fusion.9.do, f32[80,1]{1,0:T(8,128)S(1)} %copy.24.qs, f32[80,1]{1,0:T(8,128)S(1)} %copy.25.ks), custom_call_target="tpu_custom_call" | custom-call | flops 24999999488 | bytes 20971520 | tf_op jit(solution)/shard_map/attention/pallas_call | solution.py:605
  165.4 0.0 copy-start.7
  165.4 0.6 copy-done.7
  166.0 0.0 copy-start.8
  166.0 0.6 copy-done.8
  166.6 64.1 %attn_grads.1 = f32[2560,2560]{1,0:T(8,128)} custom-call(bf16[2560,2048]{1,0:T(8,128)(2,1)} %get-tuple-element.29.ht_hbm.h_t, bf16[2560,2048]{1,0:T(8,128)(2,1)} %get-tuple-element.30.dyt_hbm.dy_t, bf16[1920,2048]{1,0:T(8,128)(2,1)S(1)} %get-tuple-element.31.dqkv_t, bf16[640,2048]{1,0:T(8,128)(2,1)S(1)} %get-tuple-element.38.o_t), custom_call_target="tpu_custom_call" | custom-call | flops 26843545600 | bytes 100000000 | tf_op jit(solution)/shard_map/attn_grads/pallas_call | solution.py:639
  230.8 0.0 copy-start.5
  230.8 3.2 copy-done.5
  234.0 0.0 copy-start.11
  234.0 0.0 reduce-scatter.2.cloned.1.call-update
  234.0 0.7 copy-done.11
  234.7 0.6 reshape.60.bias
  235.3 29.0 %fusion.dna_hbm = f32[2048,2560]{1,0:T(8,128)} fusion(bf16[1920,2048]{1,0:T(8,128)(2,1)} %copy-done.5, bf16[2560,2560]{1,0:T(8,128)(2,1)} %get-tuple-element.28), kind=kOutput, calls=%fused_computation | convolution fusion | flops 20132659200 | bytes 38666240 | tf_op jit(solution)/shard_map/dot_general | solution.py:801
  264.3 0.0 all-gather.3.cloned.1.call-done.wu_hbm
  264.3 0.0 all-gather.5.cloned.1.call-done.wdt_hbm
  264.3 419.4 %mlp_chain.1 = (bf16[2048,2560]{1,0:T(8,128)(2,1)}, f32[320,2560]{1,0:T(8,128)}, f32[320,2560]{1,0:T(8,128)}, bf16[2048,2560]{1,0:T(8,128)(2,1)}, bf16[2048,2560...) custom-call(bf16[2048,2560]{1,0:T(8,128)(2,1)} %get-tuple-element.27.h_hbm, bf16[2048,2560]{1,0:T(8,128)(2,1)} %bitcast.32, ...), custom_call_target="tpu_custom_call" | custom-call | flops 199999995904 | bytes 200000000 | tf_op jit(solution)/shard_map/mlp_chain/pallas_call | solution.py:514
  683.7 1.3 slice_bitcast_fusion.4
  685.0 1.4 slice_bitcast_fusion.1
  686.4 0.0 reduce-scatter.2.cloned.1.call-done
  686.4 3.6 slice_bitcast_fusion
  690.0 0.0 copy-start.10
  690.0 8.9 %copy.29 = bf16[8,256,2560]{2,1,0:T(8,128)(2,1)} copy(bf16[8,256,2560]{2,1,0:T(8,128)(2,1)} %bitcast.24) | data formatting | bytes 20971520
  698.9 3.9 copy.30
  702.8 0.0 copy-done.10
  702.8 1.7 copy.31
Async XLA Ops:
  7.2 257.2 %all-gather.3.cloned.1.call-start = ((), (), s32[]{:S(2)}) async-start(), calls=%async_computation.1 | async-start | bytes 14745600 | tf_op jit(solution)/shard_map/all_gather | solution.py:791
  7.9 70.1 %copy-start = (f32[1,2560]{1,0:T(1,128)}, f32[1,2560]{1,0:T(1,128)S(1)}, u32[]{:S(2)}) copy-start(f32[1,2560]{1,0:T(1,128)S(1)} %reshape.57.gain.scale) | copy-start | bytes 30724
  7.9 1.0 copy-start.1
  8.9 1.0 copy-start.2
  10.0 1.0 copy-start.3
  11.0 1.0 copy-start.4
  12.0 67.6 %copy-start.12 = (f32[80]{0:T(128)S(1)}, f32[80]{0:T(128)}, u32[]{:S(2)}) copy-start(f32[80]{0:T(128)} %param.22) | copy-start | bytes 964
  12.0 67.7 %copy-start.13 = (f32[80]{0:T(128)S(1)}, f32[80]{0:T(128)}, u32[]{:S(2)}) copy-start(f32[80]{0:T(128)} %param.23) | copy-start | bytes 964
  78.1 0.6 copy-start.9
  78.7 185.6 %all-gather.5.cloned.1.call-start = ((), (), s32[]{:S(2)}) async-start(), calls=%async_computation.2 | async-start | bytes 14745600 | tf_op jit(solution)/shard_map/all_gather | solution.py:792
  79.5 606.9 %reduce-scatter.2.cloned.1.call-start = ((), (), s32[]{:S(2)}) async-start(), calls=%async_computation.3 | async-start | bytes 29491200 | tf_op jit(solution)/shard_map/reduce_scatter | solution.py:808
  117.7 3.2 copy-start.6
  165.4 0.6 copy-start.7
  166.0 0.6 copy-start.8
  230.8 3.2 copy-start.5
  234.0 0.7 copy-start.11
  690.0 12.8 %copy-start.10 = (f32[320,2560]{1,0:T(8,128)S(1)}, f32[320,2560]{1,0:T(8,128)}, u32[]{:S(2)}) copy-start(f32[320,2560]{1,0:T(8,128)} %get-tuple-element.41) | copy-start | bytes 9830404
Sparse Core Ops, SparseCore 0:
  78.9 74.3 all-gather.2
  155.1 74.0 all-gather.4
  234.1 159.7 reduce-scatter.1

commit v2 on v1

--- a/solution.py
+++ b/solution.py
@@ -10,9 +10,11 @@
 
 
 MESH = pl.DeviceIdType.MESH
+OFFSET = 5
 SKEW = 2
-SLOTS = 4
-STEP = 32
+SLOTS = 6
+SENDS = 4
+STEP = 16
 COLS = 256
 P_SLOTS, R0, R1, R2 = 6, 3, 4, 4
 TILE = 512
@@ -49,13 +51,35 @@
     last = n_tp - 1
     rows_half = rows // 2
     n_chunk = rows_half // STEP
+    n_half = n_tok // 2
     sib = {'fsdp': flipped(me, 1)}
     nbr = ({'fsdp': flipped(me, 2)}, {'fsdp': flipped(me, 4)})
 
-    load_w = [pltpu.make_async_copy(wu_hbm, wu.at[:, pl.ds(0, n_hid)], w_sem.at[0]),
-              pltpu.make_async_copy(wdt_hbm, wdt.at[:, pl.ds(0, n_hid)], w_sem.at[1])]
-    for c in load_w:
+    tile = min(TILE, n_hid)
+    f_tiles = n_hid // tile
+
+    def load_w(f):
+        cols = pl.ds(f * tile, tile)
+        return [pltpu.make_async_copy(wu_hbm.at[:, cols], wu.at[:, cols], w_sem.at[0, f]),
+                pltpu.make_async_copy(wdt_hbm.at[:, cols], wdt.at[:, cols], w_sem.at[1, f])]
+
+    def image_rows(i, side):
+        return pl.ds(pl.multiple_of(side * rows_half + i * n_half, n_half), n_half)
+
+    def image_loads(i):
+        slot = lax.rem(i, 2)
+        copies = []
+        for side in range(2):
+            half_rows = pl.ds(side * n_half, n_half)
+            copies += [pltpu.make_async_copy(h_hbm.at[image_rows(i, side)], hb.at[slot, half_rows], hb_sem.at[0, side, slot]),
+                       pltpu.make_async_copy(dy_hbm.at[image_rows(i, side)], yb.at[slot, half_rows], hb_sem.at[1, side, slot])]
+        return copies
+
+    for c in image_loads(0):
         c.start()
+    for f in range(f_tiles):
+        for c in load_w(f):
+            c.start()
     barrier = pltpu.get_barrier_semaphore()
     for rel in range(1, n_fsdp):
         pl.semaphore_signal(barrier, inc=1, device_id={'fsdp': flipped(me, rel)}, device_id_type=MESH)
@@ -69,10 +93,8 @@
         return pl.ds(pl.multiple_of(side * rows_half + k * STEP, STEP), STEP)
 
     def side_ends(side):
-        pos = my_tp if side == 0 else last - my_tp
-        nxt = {'tp': my_tp + 1 if side == 0 else my_tp - 1}
-        prv = {'tp': my_tp - 1 if side == 0 else my_tp + 1}
-        return pos, nxt, prv
+        pos = my_tp + side * (last - 2 * my_tp)
+        return pos, {'tp': my_tp + 1 - 2 * side}, {'tp': my_tp - 1 + 2 * side}
 
     def part_loads(side, k):
         slot = lax.rem(k, 2)
@@ -85,23 +107,24 @@
                 pltpu.make_async_copy(dy_hbm.at[rows_at(side, k)], dyb.at[side, slot], dy_sem.at[side, slot])]
 
     def fsend_at(side, k):
-        return remote(sbuf.at[side, lax.rem(k, 2)], recv.at[side, lax.rem(k, SLOTS)],
-                      fsend.at[side, lax.rem(k, 2)], frecv.at[side, lax.rem(k, SLOTS)], side_ends(side)[1])
+        return remote(sbuf.at[side, lax.rem(k, SENDS)], recv.at[side, lax.rem(k, SLOTS)],
+                      fsend.at[side, lax.rem(k, SENDS)], frecv.at[side, lax.rem(k, SLOTS)], side_ends(side)[1])
 
     def back_at(side, k):
-        return remote(dxb.at[side, lax.rem(k, 2)], gx.at[rows_at(side, k)],
-                      bsend.at[side, lax.rem(k, 2)], brecv.at[side, k], side_ends(side)[2])
+        return remote(dxb.at[side, lax.rem(k, SENDS)], gx.at[rows_at(side, k)],
+                      bsend.at[side, lax.rem(k, SENDS)], brecv.at[side, k], side_ends(side)[2])
 
     def relay_at(side, k):
         return remote(gx.at[rows_at(side, k)], gx.at[rows_at(side, k)],
-                      bsend.at[side, lax.rem(k, 2)], brecv.at[side, k], side_ends(side)[2])
+                      bsend.at[side, lax.rem(k, SENDS)], brecv.at[side, k], side_ends(side)[2])
 
     def local_at(side, k):
-        return pltpu.make_async_copy(dxb.at[side, lax.rem(k, 2)], gx.at[rows_at(side, k)], lsem.at[side, lax.rem(k, 2)])
-
-    def chain_step(side, i):
+        return pltpu.make_async_copy(dxb.at[side, lax.rem(k, SENDS)], gx.at[rows_at(side, k)],
+                                     lsem.at[side, lax.rem(k, SENDS)])
+
+    def side_step(side, i):
         pos, nxt, prv = side_ends(side)
-        k = i - 3 - 2 * side - SKEW * pos
+        k = i - OFFSET - SKEW * pos
 
         @pl.when((k + 1 >= 0) & (k + 1 < n_chunk))
         def _():
@@ -125,17 +148,17 @@
 
             @pl.when(pos < last)
             def _():
-                @pl.when(k >= 2)
+                @pl.when(k >= SENDS)
                 def _():
                     fsend_at(side, k).wait_send()
 
                 @pl.when(pos == 0)
                 def _():
-                    sbuf[side, slot] = part[side, slot] + part2[side, slot]
+                    sbuf[side, lax.rem(k, SENDS)] = part[side, slot] + part2[side, slot]
 
                 @pl.when(pos > 0)
                 def _():
-                    sbuf[side, slot] = part[side, slot] + part2[side, slot] + recv[side, lax.rem(k, SLOTS)]
+                    sbuf[side, lax.rem(k, SENDS)] = part[side, slot] + part2[side, slot] + recv[side, lax.rem(k, SLOTS)]
 
                 @pl.when(k >= SLOTS)
                 def _():
@@ -147,7 +170,7 @@
                 for c in root_loads(side, k):
                     c.wait()
 
-                @pl.when(k >= 2)
+                @pl.when(k >= SENDS)
                 def _():
                     back_at(side, k).wait_send()
                     local_at(side, k).wait()
@@ -163,7 +186,7 @@
                 mean_w = jnp.mean(w, axis=-1, keepdims=True)
                 mean_wx = jnp.mean(w * xh, axis=-1, keepdims=True)
                 d_x = inv * (w - mean_w - xh * mean_wx)
-                dxb[side, slot] = (dyb[side, slot].astype(f32) + d_x).astype(bf16)
+                dxb[side, lax.rem(k, SENDS)] = (dyb[side, slot].astype(f32) + d_x).astype(bf16)
                 back_at(side, k).start()
                 local_at(side, k).start()
 
@@ -171,7 +194,7 @@
             def _():
                 pl.semaphore_signal(credit.at[side], inc=1, device_id=prv, device_id_type=MESH)
 
-        kb = i - 3 - 2 * side - SKEW * last - SKEW * (last - pos)
+        kb = i - OFFSET - SKEW * last - SKEW * (last - pos)
 
         @pl.when((pos < last) & (kb >= 0) & (kb < n_chunk))
         def _():
@@ -179,23 +202,24 @@
 
             @pl.when(pos > 0)
             def _():
-                @pl.when(kb >= 2)
+                @pl.when(kb >= SENDS)
                 def _():
                     relay_at(side, kb).wait_send()
                 relay_at(side, kb).start()
 
-    def image_rows(i):
-        img = lax.rem(i, 2) * (n_img // 2) + i // 2
-        return pl.ds(pl.multiple_of(img * n_tok, n_tok), n_tok)
-
-    def image_loads(i):
-        slot = lax.rem(i, 2)
-        return [pltpu.make_async_copy(h_hbm.at[image_rows(i)], hb.at[slot], hb_sem.at[0, slot]),
-                pltpu.make_async_copy(dy_hbm.at[image_rows(i)], yb.at[slot], hb_sem.at[1, slot])]
+    def chain_step(i):
+        def body(side, carry):
+            side_step(side, i)
+            return carry
+        lax.fori_loop(0, 2, body, 0)
 
     def image_outs(i):
-        return [pltpu.make_async_copy(actb, act_hbm.at[image_rows(i)], out_sem.at[0]),
-                pltpu.make_async_copy(dhb, dh_hbm.at[image_rows(i)], out_sem.at[1])]
+        copies = []
+        for side in range(2):
+            half_rows = pl.ds(side * n_half, n_half)
+            copies += [pltpu.make_async_copy(actb.at[half_rows], act_hbm.at[image_rows(i, side)], out_sem.at[0, side]),
+                       pltpu.make_async_copy(dhb.at[half_rows], dh_hbm.at[image_rows(i, side)], out_sem.at[1, side])]
+        return copies
 
     n_tiles = width // COLS
     per_slot = psum.shape[1] // n_tok
@@ -203,72 +227,81 @@
     def dn_stage(i, t):
         slots = -(-n_tiles // per_slot)
         slot = lax.rem(i, P_SLOTS // slots) * slots + t // per_slot
-        return slot, pl.ds((t % per_slot) * n_tok, n_tok)
-
-    def dn_out(i, t):
-        slot, where = dn_stage(i, t)
-        return pltpu.make_async_copy(psum.at[slot, where], dn_hbm.at[image_rows(i), pl.ds(t * COLS, COLS)], dn_sem.at[t])
+        return slot, (t % per_slot) * n_tok
+
+    def dn_outs(i, t):
+        slot, lo = dn_stage(i, t)
+        return [pltpu.make_async_copy(psum.at[slot, pl.ds(lo + side * n_half, n_half)],
+                                      dn_hbm.at[image_rows(i, side), pl.ds(t * COLS, COLS)], dn_sem.at[side, t])
+                for side in range(2)]
 
     def finish_image(i):
         for c in image_outs(i):
             c.wait()
         for t in range(n_tiles):
-            dn_out(i, t).wait()
-
-    def mlp_hidden(i):
+            for c in dn_outs(i, t):
+                c.wait()
+
+    def mlp_hidden(i, f):
         slot = lax.rem(i, 2)
+        cols = pl.ds(f * tile, tile)
+
+        @pl.when(i == 0)
+        def _():
+            for c in load_w(f):
+                c.wait()
+        u = (jnp.dot(hb[slot], wu[:, cols], preferred_element_type=f32) + bias[:, cols]).astype(bf16).astype(f32)
+        d_act = jnp.dot(yb[slot], wdt[:, cols], preferred_element_type=f32).astype(bf16).astype(f32)
+        cdf = 0.5 * (1.0 + lax.erf(u * (0.5 ** 0.5)))
+        actb[:, cols] = (u * cdf).astype(bf16)
+        slope = cdf + u * (jnp.exp(-0.5 * u * u) * (1.0 / (2.0 * jnp.pi) ** 0.5))
+        d_u = (d_act * slope).astype(bf16)
+        dhb[:, cols] = d_u
+        gb[:, cols] += jnp.sum(d_u.astype(f32).reshape(-1, 8, tile), axis=0)
+
+    def mlp_back(i, t):
+        slot, lo = dn_stage(i, t)
+        psum[slot, pl.ds(lo, n_tok)] = lax.dot_general(dhb[...], wu[pl.ds(t * COLS, COLS), pl.ds(0, n_hid)],
+                                                       (((1,), (1,)), ((), ())), preferred_element_type=f32)
+        for c in dn_outs(i, t):
+            c.start()
+
+    load_t = [pltpu.make_async_copy(dyt_hbm, wdt.at[:, pl.ds(0, rows)], w_sem.at[1, 0]),
+              pltpu.make_async_copy(ht_hbm, wu.at[:, pl.ds(0, rows)], w_sem.at[0, 0])]
+
+    def phase1(i, carry):
+        @pl.when(i > 0)
+        def _():
+            finish_image(i - 1)
 
         @pl.when(i + 1 < n_img)
         def _():
             for c in image_loads(i + 1):
                 c.start()
+        chain_step(4 * i)
         for c in image_loads(i):
             c.wait()
-        tile = min(TILE, n_hid)
-        for f in range(0, n_hid, tile):
-            cols = pl.ds(f, tile)
-            u = (jnp.dot(hb[slot], wu[:, cols], preferred_element_type=f32) + bias[:, cols]).astype(bf16).astype(f32)
-            d_act = jnp.dot(yb[slot], wdt[:, cols], preferred_element_type=f32).astype(bf16).astype(f32)
-            cdf = 0.5 * (1.0 + lax.erf(u * (0.5 ** 0.5)))
-            actb[:, cols] = (u * cdf).astype(bf16)
-            slope = cdf + u * (jnp.exp(-0.5 * u * u) * (1.0 / (2.0 * jnp.pi) ** 0.5))
-            d_u = (d_act * slope).astype(bf16)
-            dhb[:, cols] = d_u
-            gb[:, cols] += jnp.sum(d_u.astype(f32).reshape(-1, 8, tile), axis=0)
+        for f in range(f_tiles):
+            if f == (f_tiles + 1) // 2:
+                chain_step(4 * i + 1)
+            mlp_hidden(i, f)
         for c in image_outs(i):
             c.start()
 
-    def mlp_back(i):
+        @pl.when(i == n_img - 1)
+        def _():
+            load_t[0].start()
+        chain_step(4 * i + 2)
         for t in range(n_tiles):
-            stage, where = dn_stage(i, t)
-            psum[stage, where] = lax.dot_general(dhb[...], wu[pl.ds(t * COLS, COLS), pl.ds(0, n_hid)],
-                                                 (((1,), (1,)), ((), ())), preferred_element_type=f32)
-            dn_out(i, t).start()
-
-    for c in image_loads(0):
-        c.start()
-    for c in load_w:
-        c.wait()
-
-    def phase1(i, carry):
-        @pl.when(i > 0)
-        def _():
-            finish_image(i - 1)
-        for side in range(2):
-            chain_step(side, 2 * i)
-        mlp_hidden(i)
-        for side in range(2):
-            chain_step(side, 2 * i + 1)
-        mlp_back(i)
+            if t == n_tiles // 2:
+                chain_step(4 * i + 3)
+            mlp_back(i, t)
         return carry
 
     lax.fori_loop(0, n_img, phase1, 0)
     finish_image(n_img - 1)
 
-    load_t = [pltpu.make_async_copy(ht_hbm, wu.at[:, pl.ds(0, rows)], w_sem.at[0]),
-              pltpu.make_async_copy(dyt_hbm, wdt.at[:, pl.ds(0, rows)], w_sem.at[1])]
-    for c in load_t:
-        c.start()
+    load_t[1].start()
     per_group = n_hid // COLS
     n_blocks = 2 * per_group
 
@@ -280,11 +313,11 @@
 
         @pl.when(j < per_group)
         def _():
+            pltpu.make_async_copy(act_hbm.at[:, cols_at(j)], bblk.at[slot], b_sem.at[slot]).start()
+
+        @pl.when(j >= per_group)
+        def _():
             pltpu.make_async_copy(dh_hbm.at[:, cols_at(j)], bblk.at[slot], b_sem.at[slot]).start()
-
-        @pl.when(j >= per_group)
-        def _():
-            pltpu.make_async_copy(act_hbm.at[:, cols_at(j)], bblk.at[slot], b_sem.at[slot]).start()
 
     def wait_block(j):
         slot = lax.rem(j, 2)
@@ -343,11 +376,11 @@
 
         @pl.when(j < per_group)
         def _():
+            dots(wdt)
+
+        @pl.when(j >= per_group)
+        def _():
             dots(wu)
-
-        @pl.when(j >= per_group)
-        def _():
-            dots(wdt)
 
         @pl.when(j >= R0)
         def _():
@@ -394,11 +427,11 @@
 
         @pl.when(j < per_group)
         def _():
+            grad_out(j, g_dn).start()
+
+        @pl.when(j >= per_group)
+        def _():
             grad_out(j, g_up).start()
-
-        @pl.when(j >= per_group)
-        def _():
-            grad_out(j, g_dn).start()
 
     start_block(0)
     load_t[0].wait()
@@ -409,19 +442,20 @@
             @pl.when((j >= lag) & (j - lag < n_blocks))
             def _():
                 stage(j - lag)
-        for side in range(2):
-            chain_step(side, n_img + i)
+        chain_step(4 * n_img + 2 * j)
 
         @pl.when(j < n_blocks)
         def _():
             stage_a(j)
+        chain_step(4 * n_img + 2 * j + 1)
 
         @pl.when((j >= 1) & (j - 1 < n_blocks))
         def _():
             stage_b(j - 1)
         return carry
 
-    n_iter = max(n_chunk + 5 + 2 * SKEW * last - n_img, n_img + n_blocks + 5)
+    n_steps = n_chunk + OFFSET + 2 * SKEW * last - 4 * n_img
+    n_iter = n_img + max((n_steps + 1) // 2, n_blocks + 5)
     lax.fori_loop(n_img, n_iter, phase2, 0)
 
     for j in range(n_blocks - P_SLOTS, n_blocks):
@@ -430,7 +464,7 @@
         s0_at(j).wait_send()
     for side in range(2):
         pos = side_ends(side)[0]
-        for k in (n_chunk - 2, n_chunk - 1):
+        for k in range(n_chunk - SENDS, n_chunk):
             @pl.when(pos < last)
             def _():
                 fsend_at(side, k).wait_send()
@@ -529,16 +563,16 @@
             vm((2, rows, COLS), bf16),
             vm((2, 2, STEP, width), f32), vm((2, 2, STEP, width), f32),
             vm((2, 2, STEP, width), bf16), vm((2, 2, STEP, width), bf16),
-            vm((2, SLOTS, STEP, width), f32), vm((2, 2, STEP, width), f32),
-            vm((2, 2, STEP, width), bf16),
+            vm((2, SLOTS, STEP, width), f32), vm((2, SENDS, STEP, width), f32),
+            vm((2, SENDS, STEP, width), bf16),
             vm((8, width), f32), vm(pack_shape, f32),
             vm((n_fsdp - 1,) + pack_shape, f32), vm((n_tp - 1, tp_rows, 128), f32),
-            dma((2,)), dma((2, 2)), dma((2,)), dma((width // COLS,)), dma((2,)),
+            dma((2, n_hid // min(TILE, n_hid))), dma((2, 2, 2)), dma((2, 2)), dma((2, width // COLS)), dma((2,)),
             dma((2,)), dma((R0,)), dma((2, P_SLOTS)), dma((2, R1)),
             dma((2, P_SLOTS)), dma((2, R2)), dma((P_SLOTS,)),
             reg, reg((2,)), reg((2,)),
             dma((2, 2)), dma((2, 2)), dma((2, 2)), dma((2, 2)),
-            dma((2, 2)), dma((2, SLOTS)), dma((2, 2)), dma((2, n_chunk)), dma((2, 2)),
+            dma((2, SENDS)), dma((2, SLOTS)), dma((2, SENDS)), dma((2, n_chunk)), dma((2, SENDS)),
             reg((2,)), dma((n_fsdp + n_tp - 2,)), dma((n_fsdp + n_tp - 2,)),
         ],
         compiler_params=pltpu.CompilerParams(collective_id=0, has_side_effects=True, vmem_limit_bytes=67_043_328),
@@ -616,38 +650,29 @@
     )(qkv_t, do_t, q_scale.reshape(head_dim, 1), k_scale.reshape(head_dim, 1))
 
 
-def outer_kernel(n_qkv_tiles, h_t, dy_t, dqkv_t, o_t, out):
-    n = pl.program_id(0)
-
+def outer_kernel(h_t, dy_t, dqkv_t, o_t, out):
     def nt(lhs, rhs):
         return lax.dot_general(lhs[...], rhs[...], (((1,), (1,)), ((), ())), preferred_element_type=jnp.float32)
 
-    @pl.when(n < n_qkv_tiles)
-    def _():
-        out[...] = nt(h_t, dqkv_t)
-
-    @pl.when(n >= n_qkv_tiles)
-    def _():
-        out[...] = nt(dy_t, o_t)
+    n_qkv = dqkv_t.shape[0]
+    out[:, pl.ds(0, n_qkv)] = nt(h_t, dqkv_t)
+    out[:, pl.ds(n_qkv, o_t.shape[0])] = nt(dy_t, o_t)
 
 
 def attn_grads_call(h_t, dy_t, d_qkv_t, o_t):
     width, rows = h_t.shape
-    n_feat = o_t.shape[0]
-    tile = 256
-    q_tiles = d_qkv_t.shape[0] // n_feat
+    n_all = d_qkv_t.shape[0] + o_t.shape[0]
+    tile = width // 4
+    lhs = pl.BlockSpec((tile, rows), lambda d: (d, 0))
+    once = lambda a: pl.BlockSpec(a.shape, lambda d: (0, 0), pipeline_mode=pl.Buffered(1))
     return pl.pallas_call(
-        functools.partial(outer_kernel, q_tiles),
-        grid=(q_tiles + 1, width // tile),
-        out_shape=jax.ShapeDtypeStruct((width, (q_tiles + 1) * n_feat), jnp.float32),
-        in_specs=[pl.BlockSpec((tile, rows), lambda n, d: (jnp.where(n < q_tiles, d, width // tile - 1), 0)),
-                  pl.BlockSpec((tile, rows), lambda n, d: (jnp.where(n < q_tiles, 0, d), 0)),
-                  pl.BlockSpec((n_feat, rows), lambda n, d: (jnp.minimum(n, q_tiles - 1), 0)),
-                  pl.BlockSpec((n_feat, rows), lambda n, d: (0, 0))],
-        out_specs=pl.BlockSpec((tile, n_feat), lambda n, d: (d, n)),
-        compiler_params=pltpu.CompilerParams(dimension_semantics=('arbitrary', 'arbitrary'), vmem_limit_bytes=40 << 20),
-        cost_estimate=pl.CostEstimate(flops=2 * width * rows * (q_tiles + 1) * n_feat, bytes_accessed=100_000_000,
-                                      transcendentals=0),
+        outer_kernel,
+        grid=(width // tile,),
+        out_shape=jax.ShapeDtypeStruct((width, n_all), jnp.float32),
+        in_specs=[lhs, lhs, once(d_qkv_t), once(o_t)],
+        out_specs=pl.BlockSpec((tile, n_all), lambda d: (d, 0)),
+        compiler_params=pltpu.CompilerParams(dimension_semantics=('arbitrary',), vmem_limit_bytes=56 << 20),
+        cost_estimate=pl.CostEstimate(flops=2 * width * rows * n_all, bytes_accessed=60_000_000, transcendentals=0),
         name='attn_grads',
     )(h_t, dy_t, d_qkv_t, o_t)
 

time: 718 us -> 679 us (0.946)
  Pallas kernels: 594 us -> 554 us
    pallas_call x1, Pallas kernels: 64.1 us -> 39.1 us  [attn_grads_call(): pl.pallas_call(outer_kernel, grid=(width // tile,), out_shape=jax.ShapeDt...]
    pallas_call x1, Pallas kernels: 419 us -> 405 us  [fused_call(): pl.pallas_call(kern, out_shape=(shape((rows, width), bf16), shape((blk, n...]
  transfers between devices with their start and end apart: 3 -> 3, of which waited for: 0 -> 0; matrix products, arithmetic and copies ran while one was open for 10% -> 10% of each run, Pallas kernels for 74% -> 73%
where the time goes in v2:
time: 679 us; the launch traced here: 669 us
  Pallas kernels  554 us (82%)
  matrix products  65.7 us (10%)
  local copies, waits for them, and re-layouts  33.6 us (5%)
  between operations  14.3 us (2%)
    pallas_call x1, Pallas kernels, fused_call(): pl.pallas_call(kern, out_shape=(shape((rows, width), bf16), shape((blk, n...  405 us
    pallas_call x1, Pallas kernels, prep_call(): pl.pallas_call(functools.partial(prep_kernel, n_fsdp, n_img), grid=(n_img...  66.1 us
    pallas_call x1, Pallas kernels, attn_call(): pl.pallas_call(functools.partial(attn_kernel, n_heads, head_dim), grid=(n...  44.5 us
    pallas_call x1, Pallas kernels, attn_grads_call(): pl.pallas_call(outer_kernel, grid=(width // tile,), out_shape=jax.ShapeDt...  39.1 us
    dot_general x2, matrix products, contract(): lax.dot_general(lhs, rhs, (((dim,), (dim,)), ((), ())), preferred_element...  36.7 us
    dot_general x1, matrix products, local_step(): lax.dot_general(d_qkv_t, wqkv_full, (((0,), (1,)), ((), ())), preferred_e...  29 us
    unnamed x31, local copies, waits for them, and re-layouts  25.8 us
  transfers between devices with their start and end apart: 3, of which 0 were waited for; matrix products, arithmetic and copies ran while one was open for 10% of the time, Pallas kernels for 73%

profile of v2, /device:TPU:0, one launch (start us, length us, event | category | flops | bytes accessed | tf_op | source)
XLA Modules:
  0.0 668.7 jit_solution(9046156249929778557)
XLA Ops:
  7.2 0.0 all-gather.3.cloned.1.call-start
  7.2 0.7 reshape.57.gain.scale
  7.9 0.0 copy-start
  7.9 0.0 copy-start.1
  8.0 1.0 copy-done.1
  8.9 0.0 copy-start.2
  9.0 1.0 copy-done.2
  10.0 0.0 copy-start.3
  10.0 1.0 copy-done.3
  11.0 0.0 copy-start.4
  11.0 1.0 copy-done.4
  12.0 0.0 copy-start.12
  12.0 0.0 copy-start.13
  12.0 66.1 %prep.1 = (bf16[2048,2560]{1,0:T(8,128)(2,1)}, bf16[2560,2048]{1,0:T(8,128)(2,1)}, bf16[2560,2048]{1,0:T(8,128)(2,1)}, f32[8,2560]{1,0:T(8,128)S(1)}, bf16[2560,2560]{1,0:T(8,128)(2,1)}) custom-call(bf16[2048,2560]{1,0:T(8,128)(2,1)} %bitcast.29, bf16[2048,2560]{1,0:T(8,128)(2,1)} %bitcast.31, f32[1,2560]{1,0:T(1,128)S(1)} %reshape.57.gain.scale, ...), custom_call_target="tpu_custom_call" | custom-call | flops 60000002048 | bytes 52428800 | tf_op jit(solution)/shard_map/prep/pallas_call | solution.py:774
  78.1 0.0 copy-done
  78.1 0.0 copy-start.9
  78.1 0.6 copy-done.9
  78.7 0.0 all-gather.3.cloned.1.call-update
  78.7 0.0 all-gather.5.cloned.1.call-start
  78.8 0.7 all-gather.5.cloned.1.call-update
  79.5 0.0 reduce-scatter.2.cloned.1.call-start
  79.5 0.0 copy-done.12
  79.6 0.1 copy.24.qs
  79.7 0.0 copy-done.13
  79.7 0.1 copy.25.ks
  79.8 10.7 %fusion.9.do = bf16[640,2048]{1,0:T(8,128)(2,1)S(1)} fusion(bf16[2560,2048]{1,0:T(8,128)(2,1)} %get-tuple-element.30.dyt_hbm.dy_t, bf16[2560,2560]{1,0:T(8,128)(2,1)} %get-tuple-element.28), kind=kOutput, calls=%fused_computation.7 | convolution fusion | flops 6712197120 | bytes 16384000 | tf_op jit(solution)/shard_map/dot_general | solution.py:820
  90.5 25.9 %fusion.4.qkv = bf16[1920,2048]{1,0:T(8,128)(2,1)S(1)} fusion(bf16[2560,2048]{1,0:T(8,128)(2,1)} %get-tuple-element.29.ht_hbm.h_t, bf16[2560,2560]{1,0:T(8,128)(2,1)} %get-tuple-element.28), kind=kOutput, calls=%fused_computation.4 | convolution fusion | flops 20136591360 | bytes 28180480 | tf_op jit(solution)/shard_map/dot_general | solution.py:820
  116.4 44.5 %attention.1 = (bf16[640,2048]{1,0:T(8,128)(2,1)S(1)}, bf16[1920,2048]{1,0:T(8,128)(2,1)S(1)}, f32[80,256]{1,0:T(8,128)S(1)}, f32[80,256]{1,0:T(8,128)S(1)}) custom-call(bf16[1920,2048]{1,0:T(8,128)(2,1)S(1)} %fusion.4.qkv, bf16[640,2048]{1,0:T(8,128)(2,1)S(1)} %fusion.9.do, f32[80,1]{1,0:T(8,128)S(1)} %copy.24.qs, f32[80,1]{1,0:T(8,128)S(1)} %copy.25.ks), custom_call_target="tpu_custom_call" | custom-call | flops 24999999488 | bytes 20971520 | tf_op jit(solution)/shard_map/attention/pallas_call | solution.py:639
  160.9 0.0 copy-start.5
  161.0 3.2 copy-done.5
  164.2 0.0 copy-start.6
  164.2 1.5 copy-done.6
  165.7 0.0 copy-start.7
  165.7 0.6 copy-done.7
  166.3 0.0 copy-start.8
  166.3 0.6 copy-done.8
  166.9 39.1 %attn_grads.1 = f32[2560,2560]{1,0:T(8,128)} custom-call(bf16[2560,2048]{1,0:T(8,128)(2,1)} %get-tuple-element.29.ht_hbm.h_t, bf16[2560,2048]{1,0:T(8,128)(2,1)} %get-tuple-element.30.dyt_hbm.dy_t, bf16[1920,2048]{1,0:T(8,128)(2,1)} %copy-done.5, bf16[640,2048]{1,0:T(8,128)(2,1)} %copy-done.6), custom_call_target="tpu_custom_call" | custom-call | flops 26843545600 | bytes 60000000 | tf_op jit(solution)/shard_map/attn_grads/pallas_call | solution.py:668
  206.1 0.0 copy-start.11
  206.1 0.0 reduce-scatter.2.cloned.1.call-update
  206.1 0.7 copy-done.11
  206.8 0.6 reshape.60.bias
  207.4 29.0 %fusion.dna_hbm = f32[2048,2560]{1,0:T(8,128)} fusion(bf16[1920,2048]{1,0:T(8,128)(2,1)} %copy-done.5, bf16[2560,2560]{1,0:T(8,128)(2,1)} %get-tuple-element.28), kind=kOutput, calls=%fused_computation | convolution fusion | flops 20132659200 | bytes 38666240 | tf_op jit(solution)/shard_map/dot_general | solution.py:826
  236.4 0.0 all-gather.3.cloned.1.call-done.wu_hbm
  236.4 0.0 all-gather.5.cloned.1.call-done.wdt_hbm
  236.4 404.5 %mlp_chain.1 = (bf16[2048,2560]{1,0:T(8,128)(2,1)}, f32[320,2560]{1,0:T(8,128)}, f32[320,2560]{1,0:T(8,128)}, bf16[2048,2560]{1,0:T(8,128)(2,1)}, bf16[2048,2560...) custom-call(bf16[2048,2560]{1,0:T(8,128)(2,1)} %get-tuple-element.27.h_hbm, bf16[2048,2560]{1,0:T(8,128)(2,1)} %bitcast.32, ...), custom_call_target="tpu_custom_call" | custom-call | flops 199999995904 | bytes 200000000 | tf_op jit(solution)/shard_map/mlp_chain/pallas_call | solution.py:548
  640.9 1.3 slice_bitcast_fusion.4
  642.2 1.4 slice_bitcast_fusion.1
  643.6 0.0 reduce-scatter.2.cloned.1.call-done
  643.6 3.6 slice_bitcast_fusion
  647.2 0.0 copy-start.10
  647.2 8.9 %copy.29 = bf16[8,256,2560]{2,1,0:T(8,128)(2,1)} copy(bf16[8,256,2560]{2,1,0:T(8,128)(2,1)} %bitcast.24) | data formatting | bytes 20971520
  656.1 3.9 copy.30
  660.0 0.0 copy-done.10
  660.0 1.7 copy.31
Async XLA Ops:
  7.2 229.2 %all-gather.3.cloned.1.call-start = ((), (), s32[]{:S(2)}) async-start(), calls=%async_computation.1 | async-start | bytes 14745600 | tf_op jit(solution)/shard_map/all_gather | solution.py:816
  7.9 70.1 %copy-start = (f32[1,2560]{1,0:T(1,128)}, f32[1,2560]{1,0:T(1,128)S(1)}, u32[]{:S(2)}) copy-start(f32[1,2560]{1,0:T(1,128)S(1)} %reshape.57.gain.scale) | copy-start | bytes 30724
  7.9 1.0 copy-start.1
  8.9 1.0 copy-start.2
  10.0 1.0 copy-start.3
  11.0 1.0 copy-start.4
  12.0 67.6 %copy-start.12 = (f32[80]{0:T(128)S(1)}, f32[80]{0:T(128)}, u32[]{:S(2)}) copy-start(f32[80]{0:T(128)} %param.22) | copy-start | bytes 964
  12.0 67.7 %copy-start.13 = (f32[80]{0:T(128)S(1)}, f32[80]{0:T(128)}, u32[]{:S(2)}) copy-start(f32[80]{0:T(128)} %param.23) | copy-start | bytes 964
  78.1 0.6 copy-start.9
  78.7 157.7 %all-gather.5.cloned.1.call-start = ((), (), s32[]{:S(2)}) async-start(), calls=%async_computation.2 | async-start | bytes 14745600 | tf_op jit(solution)/shard_map/all_gather | solution.py:817
  79.5 564.1 %reduce-scatter.2.cloned.1.call-start = ((), (), s32[]{:S(2)}) async-start(), calls=%async_computation.3 | async-start | bytes 29491200 | tf_op jit(solution)/shard_map/reduce_scatter | solution.py:833
  160.9 3.2 copy-start.5
  164.2 1.5 copy-start.6
  165.7 0.6 copy-start.7
  166.3 0.6 copy-start.8
  206.1 0.7 copy-start.11
  647.2 12.8 %copy-start.10 = (f32[320,2560]{1,0:T(8,128)S(1)}, f32[320,2560]{1,0:T(8,128)}, u32[]{:S(2)}) copy-start(f32[320,2560]{1,0:T(8,128)} %get-tuple-element.41) | copy-start | bytes 9830404
Sparse Core Ops, SparseCore 0:
  78.9 74.3 all-gather.2
  155.1 74.0 all-gather.4
  232.9 159.5 reduce-scatter.1

commit v3 on v2

--- a/solution.py
+++ b/solution.py
@@ -33,13 +33,14 @@
                                         device_id=where, device_id_type=MESH)
 
 
-def fused_kernel(cfg, h_hbm, dy_hbm, x_hbm, dna_hbm, ht_hbm, dyt_hbm, wu_hbm, wdt_hbm, bias, scale, b_sum, gq, gk,
+def fused_kernel(cfg, h_hbm, dy_hbm, x_hbm, wa_hbm, dqt_hbm, ht_hbm, dyt_hbm, wu_hbm, wd0_hbm, wd1_hbm, wd2_hbm,
+                 bias, scale, b_sum, gq, gk,
                  gx, g_up, g_dn, act_hbm, dh_hbm, dn_hbm, small_out,
                  wu, wdt, hb, yb, actb, dhb, gb, psum, s0, r0, r1, r2, bblk,
-                 part, part2, xb, dyb, recv, sbuf, dxb, ln_acc, pack, rs_f, rs_t,
+                 wqb, dqr, dqb, part, xb, dyb, recv, sbuf, dxb, ln_acc, pack, rs_f, rs_t,
                  w_sem, hb_sem, out_sem, dn_sem, b_sem, s0_send, r0_sem, d_send, r1_sem, xy_send, r2_sem, g_sem,
                  c0, c1, c2,
-                 part_sem, part2_sem, x_sem, dy_sem, fsend, frecv, bsend, brecv, lsem, credit, xs_send, xs_recv):
+                 wq_sem, dq_sem, part_sem, x_sem, dy_sem, fsend, frecv, bsend, brecv, lsem, credit, xs_send, xs_recv):
     n_tp, n_fsdp, n_img, n_tok = cfg
     f32, bf16 = jnp.float32, jnp.bfloat16
     rows, width = h_hbm.shape
@@ -60,8 +61,13 @@
 
     def load_w(f):
         cols = pl.ds(f * tile, tile)
+        lo = f * tile
+        for src in (wd0_hbm, wd1_hbm, wd2_hbm):
+            if lo < src.shape[1]:
+                break
+            lo -= src.shape[1]
         return [pltpu.make_async_copy(wu_hbm.at[:, cols], wu.at[:, cols], w_sem.at[0, f]),
-                pltpu.make_async_copy(wdt_hbm.at[:, cols], wdt.at[:, cols], w_sem.at[1, f])]
+                pltpu.make_async_copy(src.at[:, pl.ds(lo, tile)], wdt.at[:, cols], w_sem.at[1, f])]
 
     def image_rows(i, side):
         return pl.ds(pl.multiple_of(side * rows_half + i * n_half, n_half), n_half)
@@ -98,8 +104,7 @@
 
     def part_loads(side, k):
         slot = lax.rem(k, 2)
-        return [pltpu.make_async_copy(dn_hbm.at[rows_at(side, k)], part.at[side, slot], part_sem.at[side, slot]),
-                pltpu.make_async_copy(dna_hbm.at[rows_at(side, k)], part2.at[side, slot], part2_sem.at[side, slot])]
+        return [pltpu.make_async_copy(dn_hbm.at[rows_at(side, k)], part.at[side, slot], part_sem.at[side, slot])]
 
     def root_loads(side, k):
         slot = lax.rem(k, 2)
@@ -154,11 +159,11 @@
 
                 @pl.when(pos == 0)
                 def _():
-                    sbuf[side, lax.rem(k, SENDS)] = part[side, slot] + part2[side, slot]
+                    sbuf[side, lax.rem(k, SENDS)] = part[side, slot]
 
                 @pl.when(pos > 0)
                 def _():
-                    sbuf[side, lax.rem(k, SENDS)] = part[side, slot] + part2[side, slot] + recv[side, lax.rem(k, SLOTS)]
+                    sbuf[side, lax.rem(k, SENDS)] = part[side, slot] + recv[side, lax.rem(k, SLOTS)]
 
                 @pl.when(k >= SLOTS)
                 def _():
@@ -174,7 +179,7 @@
                 def _():
                     back_at(side, k).wait_send()
                     local_at(side, k).wait()
-                val = part[side, slot] + part2[side, slot] + recv[side, lax.rem(k, SLOTS)]
+                val = part[side, slot] + recv[side, lax.rem(k, SLOTS)]
                 d = val.astype(bf16).astype(f32)
                 xv = xb[side, slot].astype(f32)
                 cen = xv - jnp.mean(xv, axis=-1, keepdims=True)
@@ -259,17 +264,38 @@
         dhb[:, cols] = d_u
         gb[:, cols] += jnp.sum(d_u.astype(f32).reshape(-1, 8, tile), axis=0)
 
+    n_qkv = dqt_hbm.shape[0]
+
+    def dq_loads(i):
+        return [pltpu.make_async_copy(dqt_hbm.at[:, image_rows(i, side)], dqr.at[:, pl.ds(side * n_half, n_half)],
+                                      dq_sem.at[side]) for side in range(2)]
+
+    def wq_load(t):
+        return pltpu.make_async_copy(wa_hbm.at[pl.ds(t * COLS, COLS), pl.ds(0, n_qkv)], wqb.at[t % 2], wq_sem.at[t % 2])
+
     def mlp_back(i, t):
         slot, lo = dn_stage(i, t)
-        psum[slot, pl.ds(lo, n_tok)] = lax.dot_general(dhb[...], wu[pl.ds(t * COLS, COLS), pl.ds(0, n_hid)],
-                                                       (((1,), (1,)), ((), ())), preferred_element_type=f32)
+        if t + 1 < n_tiles:
+            wq_load(t + 1).start()
+        wq_load(t).wait()
+
+        def nt(lhs, rhs):
+            return lax.dot_general(lhs, rhs, (((1,), (1,)), ((), ())), preferred_element_type=f32)
+
+        psum[slot, pl.ds(lo, n_tok)] = (nt(dhb[...], wu[pl.ds(t * COLS, COLS), pl.ds(0, n_hid)])
+                                        + nt(dqb[...], wqb[t % 2]))
         for c in dn_outs(i, t):
             c.start()
 
     load_t = [pltpu.make_async_copy(dyt_hbm, wdt.at[:, pl.ds(0, rows)], w_sem.at[1, 0]),
               pltpu.make_async_copy(ht_hbm, wu.at[:, pl.ds(0, rows)], w_sem.at[0, 0])]
 
+    early = n_img // 2
+    steps1 = 3 * n_img + early
+
     def phase1(i, carry):
+        step = 3 * i + i - (i // early) * (i - early)
+
         @pl.when(i > 0)
         def _():
             finish_image(i - 1)
@@ -278,12 +304,15 @@
         def _():
             for c in image_loads(i + 1):
                 c.start()
-        chain_step(4 * i)
+        for c in dq_loads(i):
+            c.start()
+        wq_load(0).start()
+        chain_step(step)
         for c in image_loads(i):
             c.wait()
         for f in range(f_tiles):
             if f == (f_tiles + 1) // 2:
-                chain_step(4 * i + 1)
+                chain_step(step + 1)
             mlp_hidden(i, f)
         for c in image_outs(i):
             c.start()
@@ -291,10 +320,15 @@
         @pl.when(i == n_img - 1)
         def _():
             load_t[0].start()
-        chain_step(4 * i + 2)
+        chain_step(step + 2)
+        for c in dq_loads(i):
+            c.wait()
+        dqb[...] = dqr[...].T
         for t in range(n_tiles):
             if t == n_tiles // 2:
-                chain_step(4 * i + 3)
+                @pl.when(i < early)
+                def _():
+                    chain_step(step + 3)
             mlp_back(i, t)
         return carry
 
@@ -442,19 +476,19 @@
             @pl.when((j >= lag) & (j - lag < n_blocks))
             def _():
                 stage(j - lag)
-        chain_step(4 * n_img + 2 * j)
+        chain_step(steps1 + 2 * j)
 
         @pl.when(j < n_blocks)
         def _():
             stage_a(j)
-        chain_step(4 * n_img + 2 * j + 1)
+        chain_step(steps1 + 2 * j + 1)
 
         @pl.when((j >= 1) & (j - 1 < n_blocks))
         def _():
             stage_b(j - 1)
         return carry
 
-    n_steps = n_chunk + OFFSET + 2 * SKEW * last - 4 * n_img
+    n_steps = n_chunk + OFFSET + 2 * SKEW * last - steps1
     n_iter = n_img + max((n_steps + 1) // 2, n_blocks + 5)
     lax.fori_loop(n_img, n_iter, phase2, 0)
 
@@ -527,7 +561,7 @@
     return n_up, n_wide, n_wide + 2 + -(n_up + 2 * n_wide + 2) % 8
 
 
-def fused_call(mesh, normed, dy, x2, dn_attn, normed_t, dy_t, wu, wdt, b_up, ln_scale, b_sum, gq, gk, n_img):
+def fused_call(mesh, normed, dy, x2, w_attn, dqkv_t, normed_t, dy_t, wu, wds, b_up, ln_scale, b_sum, gq, gk, n_img):
     rows, width = x2.shape
     pack_up, pack_wide, tp_rows = small_rows(wu.shape[1], width)
     pack_shape = (pack_up + pack_wide + tp_rows, 128)
@@ -550,7 +584,7 @@
         out_shape=(shape((rows, width), bf16), shape((blk, n_hid), f32), shape((blk, n_hid), f32),
                    shape((rows, n_hid), bf16), shape((rows, n_hid), bf16), shape((rows, width), f32),
                    shape(pack_shape, f32)),
-        in_specs=[any_spec] * 8 + [vmem] * 5,
+        in_specs=[any_spec] * 11 + [vmem] * 5,
         out_specs=(any_spec,) * 6 + (vmem,),
         scratch_shapes=[
             vm((width, lane), bf16), vm((width, lane), bf16),
@@ -561,7 +595,8 @@
             vm((2, 4 * blk, COLS), f32), vm((R0, 4 * blk, COLS), f32),
             vm((2, R1, blk // 2, COLS), f32), vm((2, R2, blk, COLS), f32),
             vm((2, rows, COLS), bf16),
-            vm((2, 2, STEP, width), f32), vm((2, 2, STEP, width), f32),
+            vm((2, COLS, dqkv_t.shape[0]), bf16), vm((dqkv_t.shape[0], n_tok), bf16),
+            vm((n_tok, dqkv_t.shape[0]), bf16), vm((2, 2, STEP, width), f32),
             vm((2, 2, STEP, width), bf16), vm((2, 2, STEP, width), bf16),
             vm((2, SLOTS, STEP, width), f32), vm((2, SENDS, STEP, width), f32),
             vm((2, SENDS, STEP, width), bf16),
@@ -571,23 +606,100 @@
             dma((2,)), dma((R0,)), dma((2, P_SLOTS)), dma((2, R1)),
             dma((2, P_SLOTS)), dma((2, R2)), dma((P_SLOTS,)),
             reg, reg((2,)), reg((2,)),
-            dma((2, 2)), dma((2, 2)), dma((2, 2)), dma((2, 2)),
+            dma((2,)), dma((2,)), dma((2, 2)), dma((2, 2)), dma((2, 2)),
             dma((2, SENDS)), dma((2, SLOTS)), dma((2, SENDS)), dma((2, n_chunk)), dma((2, SENDS)),
             reg((2,)), dma((n_fsdp + n_tp - 2,)), dma((n_fsdp + n_tp - 2,)),
         ],
         compiler_params=pltpu.CompilerParams(collective_id=0, has_side_effects=True, vmem_limit_bytes=67_043_328),
         cost_estimate=pl.CostEstimate(flops=200_000_000_000, bytes_accessed=200_000_000, transcendentals=0),
         name='mlp_chain',
-    )(normed, dy, x2, dn_attn, normed_t, dy_t, wu, wdt, b_up.reshape(1, n_hid), ln_scale.reshape(1, width), b_sum, gq, gk)
-
-
-def attn_kernel(n_heads, head_dim, qkv, do, qs, ks, o_out, dqkv, gq, gk):
+    )(normed, dy, x2, w_attn, dqkv_t, normed_t, dy_t, wu, *wds, b_up.reshape(1, n_hid), ln_scale.reshape(1, width), b_sum, gq, gk)
+
+
+def gather_steps(me, src, shard, full, sems):
+    own_sem, put_sem, send, got, half_send, half_got, sib_send, sib_got = sems
+    blk = shard.shape[0]
+    half = blk // 2
+    sib = {'fsdp': flipped(me, 1)}
+    nbr = ({'fsdp': flipped(me, 2)}, {'fsdp': flipped(me, 4)})
+
+    def rows_of(rel):
+        return pl.ds(pl.multiple_of(flipped(me, rel) * blk, blk), blk)
+
+    def half_of(rel, d):
+        return pl.ds(pl.multiple_of(flipped(me, rel) * blk + d * half, half), half)
+
+    def loads():
+        copies, lo = [], 0
+        for j, ref in enumerate(src):
+            n = ref.shape[1]
+            copies.append(pltpu.make_async_copy(ref, shard.at[:, pl.ds(lo, n)], own_sem.at[j]))
+            lo += n
+        return copies
+
+    put = pltpu.make_async_copy(shard, full.at[rows_of(0)], put_sem)
+
+    def own_to(d):
+        return remote(shard, full.at[rows_of(0)], send.at[d], got.at[d], nbr[d])
+
+    def half_to(d):
+        where = half_of(4 - 2 * d, 1 - d)
+        return remote(full.at[where], full.at[where], half_send.at[d], half_got.at[d], nbr[d])
+
+    def to_sib(q):
+        return remote(shard if q == 0 else full.at[rows_of(2 * q)], full.at[rows_of(2 * q)], sib_send.at[q],
+                      sib_got.at[q], sib)
+
+    def begin():
+        for c in loads():
+            c.start()
+        barrier = pltpu.get_barrier_semaphore()
+        for where in (sib,) + nbr:
+            pl.semaphore_signal(barrier, inc=1, device_id=where, device_id_type=MESH)
+        pl.semaphore_wait(barrier, 3)
+        for c in loads():
+            c.wait()
+        for d in range(2):
+            own_to(d).start()
+        to_sib(0).start()
+        put.start()
+
+    def middle():
+        for d in range(2):
+            own_to(d).wait_recv()
+            half_to(1 - d).start()
+            to_sib(1 + d).start()
+
+    def end():
+        for d in range(2):
+            half_to(d).wait_recv()
+        to_sib(3).start()
+        put.wait()
+        for d in range(2):
+            own_to(d).wait_send()
+            half_to(d).wait_send()
+        for q in range(4):
+            to_sib(q).wait()
+
+    return begin, middle, end
+
+
+def gather_scratch(blk, n_cols, n_src):
+    dma = pltpu.SemaphoreType.DMA
+    return [pltpu.VMEM((blk, n_cols), jnp.bfloat16), dma((n_src,)), dma, dma((2,)), dma((2,)), dma((2,)), dma((2,)),
+            dma((4,)), dma((4,))]
+
+
+def attn_kernel(n_heads, head_dim, n_img, cut, qkv, do, qs, ks, w_shard, o_out, dqkv, gq, gk, w_full, shard, *sems):
     f32, bf16 = jnp.float32, jnp.bfloat16
     scale = head_dim ** -0.5
     n_feat = n_heads * head_dim
+    w_part = w_shard.at[:, pl.ds(cut, shard.shape[1])]
+    begin, middle, end = gather_steps(lax.axis_index('fsdp'), (w_part,), shard, w_full, sems)
 
     @pl.when(pl.program_id(0) == 0)
     def _():
+        begin()
         gq[...] = jnp.zeros_like(gq)
         gk[...] = jnp.zeros_like(gk)
 
@@ -627,30 +739,50 @@
         dqkv[q_rows, :] = norm_back(dqn, q_hat, q_inv, qs[...]).astype(bf16)
         dqkv[k_rows, :] = norm_back(dkn, k_hat, k_inv, ks[...]).astype(bf16)
 
-
-def attn_call(qkv_t, do_t, q_scale, k_scale, n_img):
+    @pl.when(pl.program_id(0) == n_img // 2)
+    def _():
+        middle()
+
+    @pl.when(pl.program_id(0) == n_img - 1)
+    def _():
+        end()
+
+
+def attn_call(qkv_t, do_t, q_scale, k_scale, w_shard, cut, n_cols, n_fsdp, n_img):
     n_feat, rows = do_t.shape
     head_dim = q_scale.shape[0]
     n_tok = rows // n_img
+    blk = w_shard.shape[0]
     f32, bf16 = jnp.float32, jnp.bfloat16
     col = lambda n: pl.BlockSpec((n, n_tok), lambda i: (0, i))
     whole = lambda shape: pl.BlockSpec(shape, lambda i: (0, 0))
+    any_spec = pl.BlockSpec(memory_space=pl.ANY)
     n_heads = n_feat // head_dim
+    shape = jax.ShapeDtypeStruct
     return pl.pallas_call(
-        functools.partial(attn_kernel, n_heads, head_dim),
+        functools.partial(attn_kernel, n_heads, head_dim, n_img, cut),
         grid=(n_img,),
-        out_shape=(jax.ShapeDtypeStruct((n_feat, rows), bf16), jax.ShapeDtypeStruct((3 * n_feat, rows), bf16),
-                   jax.ShapeDtypeStruct((head_dim, n_tok), f32), jax.ShapeDtypeStruct((head_dim, n_tok), f32)),
-        in_specs=[col(3 * n_feat), col(n_feat), whole((head_dim, 1)), whole((head_dim, 1))],
-        out_specs=(col(n_feat), col(3 * n_feat), whole((head_dim, n_tok)), whole((head_dim, n_tok))),
-        compiler_params=pltpu.CompilerParams(dimension_semantics=('arbitrary',), vmem_limit_bytes=32 << 20),
-        cost_estimate=pl.CostEstimate(flops=25_000_000_000, bytes_accessed=8 * n_feat * rows * 2,
+        out_shape=(shape((n_feat, rows), bf16), shape((3 * n_feat, rows), bf16), shape((head_dim, n_tok), f32),
+                   shape((head_dim, n_tok), f32), shape((n_fsdp * blk, n_cols), bf16)),
+        in_specs=[col(3 * n_feat), col(n_feat), whole((head_dim, 1)), whole((head_dim, 1)), any_spec],
+        out_specs=(col(n_feat), col(3 * n_feat), whole((head_dim, n_tok)), whole((head_dim, n_tok)), any_spec),
+        scratch_shapes=gather_scratch(blk, n_cols, 1),
+        compiler_params=pltpu.CompilerParams(dimension_semantics=('arbitrary',), collective_id=2, has_side_effects=True,
+                                             vmem_limit_bytes=60 << 20),
+        cost_estimate=pl.CostEstimate(flops=40_000_000_000, bytes_accessed=8 * n_feat * rows * 2,
                                       transcendentals=n_img * n_heads * n_tok * n_tok),
         name='attention',
-    )(qkv_t, do_t, q_scale.reshape(head_dim, 1), k_scale.reshape(head_dim, 1))
-
-
-def outer_kernel(h_t, dy_t, dqkv_t, o_t, out):
+    )(qkv_t, do_t, q_scale.reshape(head_dim, 1), k_scale.reshape(head_dim, 1), w_shard)
+
+
+def outer_kernel(n_steps, cut, h_t, dy_t, dqkv_t, o_t, w_shard, out, w_full, shard, *sems):
+    w_part = w_shard.at[:, pl.ds(cut, shard.shape[1])]
+    begin, middle, end = gather_steps(lax.axis_index('fsdp'), (w_part,), shard, w_full, sems)
+
+    @pl.when(pl.program_id(0) == 0)
+    def _():
+        begin()
+
     def nt(lhs, rhs):
         return lax.dot_general(lhs[...], rhs[...], (((1,), (1,)), ((), ())), preferred_element_type=jnp.float32)
 
@@ -658,75 +790,47 @@
     out[:, pl.ds(0, n_qkv)] = nt(h_t, dqkv_t)
     out[:, pl.ds(n_qkv, o_t.shape[0])] = nt(dy_t, o_t)
 
-
-def attn_grads_call(h_t, dy_t, d_qkv_t, o_t):
+    @pl.when(pl.program_id(0) == n_steps // 2)
+    def _():
+        middle()
+
+    @pl.when(pl.program_id(0) == n_steps - 1)
+    def _():
+        end()
+
+
+def attn_grads_call(h_t, dy_t, d_qkv_t, o_t, w_shard, cut, n_cols, n_fsdp):
     width, rows = h_t.shape
     n_all = d_qkv_t.shape[0] + o_t.shape[0]
-    tile = width // 4
+    n_steps = 4
+    tile = width // n_steps
+    blk = w_shard.shape[0]
     lhs = pl.BlockSpec((tile, rows), lambda d: (d, 0))
     once = lambda a: pl.BlockSpec(a.shape, lambda d: (0, 0), pipeline_mode=pl.Buffered(1))
+    any_spec = pl.BlockSpec(memory_space=pl.ANY)
     return pl.pallas_call(
-        outer_kernel,
-        grid=(width // tile,),
-        out_shape=jax.ShapeDtypeStruct((width, n_all), jnp.float32),
-        in_specs=[lhs, lhs, once(d_qkv_t), once(o_t)],
-        out_specs=pl.BlockSpec((tile, n_all), lambda d: (d, 0)),
-        compiler_params=pltpu.CompilerParams(dimension_semantics=('arbitrary',), vmem_limit_bytes=56 << 20),
+        functools.partial(outer_kernel, n_steps, cut),
+        grid=(n_steps,),
+        out_shape=(jax.ShapeDtypeStruct((width, n_all), jnp.float32),
+                   jax.ShapeDtypeStruct((n_fsdp * blk, n_cols), jnp.bfloat16)),
+        in_specs=[lhs, lhs, once(d_qkv_t), once(o_t), any_spec],
+        out_specs=(pl.BlockSpec((tile, n_all), lambda d: (d, 0)), any_spec),
+        scratch_shapes=gather_scratch(blk, n_cols, 1),
+        compiler_params=pltpu.CompilerParams(dimension_semantics=('arbitrary',), collective_id=3, has_side_effects=True,
+                                             vmem_limit_bytes=60 << 20),
         cost_estimate=pl.CostEstimate(flops=2 * width * rows * n_all, bytes_accessed=60_000_000, transcendentals=0),
         name='attn_grads',
-    )(h_t, dy_t, d_qkv_t, o_t)
-
-
-def prep_kernel(n_fsdp, n_img, x, dy, gain, wq, wk, wv, wo_t, h, h_t, dy_t, b_sum, w_full, shard, own_sem, put_sem,
-                send, got, half_send, half_got, sib_send, sib_got):
+    )(h_t, dy_t, d_qkv_t, o_t, w_shard)
+
+
+def prep_kernel(n_img, x, dy, gain, wq, wk, wv, wo_t, h, h_t, dy_t, b_sum, w_full, shard, *sems):
     f32, bf16 = jnp.float32, jnp.bfloat16
     i = pl.program_id(0)
-    me = lax.axis_index('fsdp')
-    blk = shard.shape[0]
-    half = blk // 2
-    sib = {'fsdp': flipped(me, 1)}
-    nbr = ({'fsdp': flipped(me, 2)}, {'fsdp': flipped(me, 4)})
-    pieces = (wq, wk, wv, wo_t)
-
-    def rows_of(rel):
-        return pl.ds(pl.multiple_of(flipped(me, rel) * blk, blk), blk)
-
-    def half_of(rel, d):
-        return pl.ds(pl.multiple_of(flipped(me, rel) * blk + d * half, half), half)
-
-    def load(j):
-        n = pieces[j].shape[1]
-        return pltpu.make_async_copy(pieces[j], shard.at[:, pl.ds(j * n, n)], own_sem.at[j])
-
-    def put():
-        return pltpu.make_async_copy(shard, w_full.at[rows_of(0)], put_sem)
-
-    def own_to(d):
-        return remote(shard, w_full.at[rows_of(0)], send.at[d], got.at[d], nbr[d])
-
-    def half_to(d):
-        rel = 4 - 2 * d
-        return remote(w_full.at[half_of(rel, 1 - d)], w_full.at[half_of(rel, 1 - d)], half_send.at[d], half_got.at[d],
-                      nbr[d])
-
-    def to_sib(q):
-        src = shard if q == 0 else w_full.at[rows_of(2 * q)]
-        return remote(src, w_full.at[rows_of(2 * q)], sib_send.at[q], sib_got.at[q], sib)
+    begin, middle, end = gather_steps(lax.axis_index('fsdp'), (wq, wk, wv, wo_t), shard, w_full, sems)
 
     @pl.when(i == 0)
     def _():
-        for j in range(4):
-            load(j).start()
-        barrier = pltpu.get_barrier_semaphore()
-        for where in (sib,) + nbr:
-            pl.semaphore_signal(barrier, inc=1, device_id=where, device_id_type=MESH)
-        pl.semaphore_wait(barrier, 3)
-        for j in range(4):
-            load(j).wait()
-        for d in range(2):
-            own_to(d).start()
-        to_sib(0).start()
-        put().start()
+        begin()
         b_sum[...] = jnp.zeros_like(b_sum)
 
     width = x.shape[1]
@@ -742,21 +846,8 @@
 
     @pl.when(i == n_img - 1)
     def _():
-        own_to(0).wait_recv()
-        half_to(1).start()
-        to_sib(1).start()
-        own_to(1).wait_recv()
-        half_to(0).start()
-        to_sib(2).start()
-        half_to(0).wait_recv()
-        half_to(1).wait_recv()
-        to_sib(3).start()
-        put().wait()
-        for d in range(2):
-            own_to(d).wait_send()
-            half_to(d).wait_send()
-        for q in range(4):
-            to_sib(q).wait()
+        middle()
+        end()
 
 
 def prep_call(mesh, x2, dy, ln_scale, attn_weights, n_img):
@@ -766,25 +857,71 @@
     blk = attn_weights[0].shape[0]
     n_all = sum(w.shape[1] for w in attn_weights)
     f32, bf16 = jnp.float32, jnp.bfloat16
-    dma = pltpu.SemaphoreType.DMA
     row = pl.BlockSpec((n_tok, width), lambda i: (i, 0))
     col = pl.BlockSpec((width, n_tok), lambda i: (0, i))
     any_spec = pl.BlockSpec(memory_space=pl.ANY)
     shape = jax.ShapeDtypeStruct
     return pl.pallas_call(
-        functools.partial(prep_kernel, n_fsdp, n_img),
+        functools.partial(prep_kernel, n_img),
         grid=(n_img,),
         out_shape=(shape((rows, width), bf16), shape((width, rows), bf16), shape((width, rows), bf16),
                    shape((8, width), f32), shape((width, n_all), bf16)),
         in_specs=[row, row, pl.BlockSpec((1, width), lambda i: (0, 0))] + [any_spec] * 4,
         out_specs=(row, col, col, pl.BlockSpec((8, width), lambda i: (0, 0)), any_spec),
-        scratch_shapes=[pltpu.VMEM((blk, n_all), bf16), dma((4,)), dma, dma((2,)), dma((2,)), dma((2,)), dma((2,)),
-                        dma((4,)), dma((4,))],
+        scratch_shapes=gather_scratch(blk, n_all, 4),
         compiler_params=pltpu.CompilerParams(dimension_semantics=('arbitrary',), collective_id=1, has_side_effects=True,
                                              vmem_limit_bytes=48 << 20),
         cost_estimate=pl.CostEstimate(flops=60_000_000_000, bytes_accessed=10 * rows * width, transcendentals=0),
         name='prep',
     )(x2, dy, ln_scale.reshape(1, width), *attn_weights)
+
+
+def hand_over_kernel(n_feat, gx, g_up, g_dn, g_at, o_gx, o_up, o_dn, o_q, o_k, o_v, o_o, b_gx, b_up, b_dn, b_at,
+                     in_sem, out_sem):
+    n_cut = b_gx.shape[0]
+    step = b_gx.shape[1]
+    loads, stores = [], []
+    for j in range(n_cut):
+        part = pl.ds(j * step, step)
+        loads.append((gx.at[part], b_gx.at[j]))
+        stores.append([(b_gx.at[j], o_gx.at[part])])
+    for src, buf, dst in ((g_up, b_up, o_up), (g_dn, b_dn, o_dn)):
+        loads.append((src, buf))
+        stores.append([(buf, dst)])
+    loads.append((g_at, b_at))
+    stores.append([(b_at.at[:, pl.ds(j * n_feat, n_feat)], dst) for j, dst in enumerate((o_q, o_k, o_v, o_o))])
+    for j, (src, buf) in enumerate(loads):
+        pltpu.make_async_copy(src, buf, in_sem.at[j]).start()
+    at, pending = 0, []
+    for j, (src, buf) in enumerate(loads):
+        pltpu.make_async_copy(src, buf, in_sem.at[j]).wait()
+        for src2, dst in stores[j]:
+            pending.append(pltpu.make_async_copy(src2, dst, out_sem.at[at]))
+            pending[-1].start()
+            at += 1
+    for c in pending:
+        c.wait()
+
+
+def hand_over(gx, g_up, g_dn, g_at, n_feat):
+    rows, width = gx.shape
+    blk = g_at.shape[0]
+    n_cut = 8
+    f32 = jnp.float32
+    shape, vm, dma = jax.ShapeDtypeStruct, pltpu.VMEM, pltpu.SemaphoreType.DMA
+    any_spec = pl.BlockSpec(memory_space=pl.ANY)
+    side = shape((blk, n_feat), f32)
+    return pl.pallas_call(
+        functools.partial(hand_over_kernel, n_feat),
+        out_shape=(shape(gx.shape, gx.dtype), shape(g_up.shape, f32), shape(g_dn.shape, f32), side, side, side, side),
+        in_specs=[any_spec] * 4,
+        out_specs=(any_spec,) * 7,
+        scratch_shapes=[vm((n_cut, rows // n_cut, width), gx.dtype), vm(g_up.shape, f32), vm(g_dn.shape, f32),
+                        vm(g_at.shape, f32), dma((n_cut + 3,)), dma((n_cut + 6,))],
+        compiler_params=pltpu.CompilerParams(vmem_limit_bytes=60 << 20),
+        cost_estimate=pl.CostEstimate(flops=1_000_000, bytes_accessed=40_000_000, transcendentals=0),
+        name='hand_over',
+    )(gx, g_up, g_dn, g_at)
 
 
 def solution(mesh):
@@ -805,6 +942,7 @@
         num_rows = num_img * num_tok
         width = x_in.shape[2]
         n_qkv = w_query.shape[1]
+        n_fsdp = mesh.shape['fsdp']
 
         x2 = x_in.reshape(num_rows, width)
         dy = grad_y.reshape(num_rows, width)
@@ -812,27 +950,32 @@
             mesh, x2, dy, ln_scale, (w_query, w_key, w_value, w_out.T), num_img)
         wqkv_full = attn_full[:, :3 * n_qkv]
         wot_full = attn_full[:, 3 * n_qkv:]
-        w_up, w_down_t, attn_full = lax.optimization_barrier((w_up, w_down.T, attn_full))
+        n_part = max(w_up.shape[1] // 5 // 128 * 128, 128)
+        cut1, cut2 = w_up.shape[1] - 4 * n_part, w_up.shape[1] - 2 * n_part
+        w_down_t = w_down.T
+        w_up, w_down_a, attn_full = lax.optimization_barrier((w_up, w_down_t[:, :cut1], attn_full))
         wu_full = gather_rows(w_up)
-        wdt_full = gather_rows(w_down_t)
+        wd_a = gather_rows(w_down_a)
 
         def contract(lhs, rhs, dim):
             return lax.dot_general(lhs, rhs, (((dim,), (dim,)), ((), ())), preferred_element_type=fp32)
 
         qkv_t = contract(wqkv_full, normed_t, 0).astype(bf16)
         d_attn_t = contract(wot_full, dy_t, 0).astype(bf16)
-        attn_t, d_qkv_t, gq, gk = attn_call(qkv_t, d_attn_t, q_scale, k_scale, num_img)
-        grad_w_attn = attn_grads_call(normed_t, dy_t, d_qkv_t, attn_t)
-        d_normed = lax.dot_general(d_qkv_t, wqkv_full, (((0,), (1,)), ((), ())), preferred_element_type=fp32)
+        attn_t, d_qkv_t, gq, gk, wd_b = attn_call(
+            qkv_t, d_attn_t, q_scale, k_scale, w_down_t, cut1, cut2 - cut1, n_fsdp, num_img)
+        grad_w_attn, wd_c = attn_grads_call(
+            normed_t, dy_t, d_qkv_t, attn_t, w_down_t, cut2, w_down_t.shape[1] - cut2, n_fsdp)
 
         grad_x, g_up, g_down_t, _, _, _, small = fused_call(
-            mesh, normed, dy, x2, d_normed, normed_t, dy_t, wu_full, wdt_full, b_up, ln_scale, b_sum, gq, gk, num_img)
+            mesh, normed, dy, x2, attn_full, d_qkv_t, normed_t, dy_t, wu_full, (wd_a, wd_b, wd_c), b_up, ln_scale,
+            b_sum, gq, gk, num_img)
         n_up, n_wide, _ = small_rows(wu_full.shape[1], width)
         tp_lo = n_up + n_wide
         q_lo = tp_lo + n_wide
         g_attn = scatter_rows(grad_w_attn)
-        return (grad_x.reshape(x_in.shape), g_attn[:, :n_qkv], g_attn[:, n_qkv:2 * n_qkv], g_attn[:, 2 * n_qkv:3 * n_qkv],
-                g_attn[:, 3 * n_qkv:].T, g_up, small[:n_up].reshape(-1),
+        grad_x, g_up, g_down_t, g_q, g_k, g_v, g_out_t = hand_over(grad_x, g_up, g_down_t, g_attn, n_qkv)
+        return (grad_x.reshape(x_in.shape), g_q, g_k, g_v, g_out_t.T, g_up, small[:n_up].reshape(-1),
                 g_down_t.T, small[n_up:tp_lo].reshape(-1), small[tp_lo:q_lo].reshape(-1),
                 small[q_lo, :head_dim], small[q_lo + 1, :head_dim])
 

time: 679 us -> 730 us (1.075)
  Pallas kernels: 554 us -> 657 us
  matrix products: 65.7 us -> 36.2 us
  local copies, waits for them, and re-layouts: 33.6 us -> 12.5 us
    pallas_call x1, Pallas kernels: 405 us -> 467 us  [fused_call(): pl.pallas_call(kern, out_shape=(shape((rows, width), bf16), shape((blk, n...]
    pallas_call x3 -> x4, Pallas kernels: 150 us -> 190 us  [the longest x1 66.2 us: prep_call(): pl.pallas_call(functools.partial(prep_kernel, n_img), grid=(n_img,), out_...]
    dot_general x1 -> x0, matrix products: 29 us -> none  [local_step(): lax.dot_general(d_qkv_t, wqkv_full, (((0,), (1,)), ((), ())), preferred_e...]
    unnamed x31 -> x26, local copies, waits for them, and re-layouts: 25.8 us -> 5.34 us
  transfers between devices with their start and end apart: 3 -> 3, of which waited for: 0 -> 0; matrix products, arithmetic and copies ran while one was open for 10% -> 6% of each run, Pallas kernels for 73% -> 80%
where the time goes in v3:
time: 730 us; the launch traced here: 721 us
  Pallas kernels  657 us (90%)
  matrix products  36.2 us (5%)
  between operations  14.3 us (2%)
  local copies, waits for them, and re-layouts  12.5 us (2%)
    pallas_call x1, Pallas kernels, fused_call(): pl.pallas_call(kern, out_shape=(shape((rows, width), bf16), shape((blk, n...  467 us
    pallas_call x1, Pallas kernels, prep_call(): pl.pallas_call(functools.partial(prep_kernel, n_img), grid=(n_img,), out_...  66.2 us
    pallas_call x1, Pallas kernels, attn_grads_call(): pl.pallas_call(functools.partial(outer_kernel, n_steps, cut), grid=(n_ste...  58.3 us
    pallas_call x1, Pallas kernels, attn_call(): pl.pallas_call(functools.partial(attn_kernel, n_heads, head_dim, n_img, c...  51.2 us
    dot_general x2, matrix products, contract(): lax.dot_general(lhs, rhs, (((dim,), (dim,)), ((), ())), preferred_element...  36.2 us
    pallas_call x1, Pallas kernels, hand_over(): pl.pallas_call(functools.partial(hand_over_kernel, n_feat), out_shape=(sh...  14.7 us
  transfers between devices with their start and end apart: 3, of which 0 were waited for; matrix products, arithmetic and copies ran while one was open for 6% of the time, Pallas kernels for 80%

profile of v3, /device:TPU:0, one launch (start us, length us, event | category | flops | bytes accessed | tf_op | source)
XLA Modules:
  0.0 720.6 jit_solution(8002149107013766929)
XLA Ops:
  7.2 0.0 all-gather.5.cloned.1.call-start
  7.2 0.7 reshape.57.gain.scale
  7.9 0.0 copy-start
  7.9 1.7 slice.32
  9.7 0.0 copy-start.1
  9.7 1.0 copy-done.1
  10.7 0.0 copy-start.2
  10.7 1.0 copy-done.2
  11.7 0.0 copy-start.3
  11.7 1.0 copy-done.3
  12.7 0.0 copy-start.4
  12.7 1.0 copy-done.4
  13.7 0.0 copy-start.7
  13.7 0.0 copy-start.8
  13.7 66.2 %prep.1 = (bf16[2048,2560]{1,0:T(8,128)(2,1)}, bf16[2560,2048]{1,0:T(8,128)(2,1)}, bf16[2560,2048]{1,0:T(8,128)(2,1)}, f32[8,2560]{1,0:T(8,128)S(1)}, bf16[2560,2560]{1,0:T(8,128)(2,1)}) custom-call(bf16[2048,2560]{1,0:T(8,128)(2,1)} %bitcast.27, bf16[2048,2560]{1,0:T(8,128)(2,1)} %bitcast.29, f32[1,2560]{1,0:T(1,128)S(1)} %reshape.57.gain.scale, ...), custom_call_target="tpu_custom_call" | custom-call | flops 60000002048 | bytes 52428800 | tf_op jit(solution)/shard_map/prep/pallas_call | solution.py:864
  79.8 0.0 copy-done
  79.8 0.0 copy-start.5
  79.9 0.6 copy-done.5
  80.5 0.0 all-gather.5.cloned.1.call-update
  80.5 0.0 all-gather.3.cloned.1.call-start
  80.6 0.0 slice-start
  80.6 0.7 all-gather.3.cloned.1.call-update
  81.3 0.0 reduce-scatter.2.cloned.1.call-start
  81.3 0.0 copy-done.7
  81.3 0.7 copy.24.qs
  82.0 0.0 copy-done.8
  82.0 0.7 copy.25.ks
  82.8 0.0 slice-start.1
  82.8 0.0 slice-start.2
  82.8 0.0 slice-start.3
  82.8 11.9 %fusion.7.do = bf16[640,2048]{1,0:T(8,128)(2,1)} fusion(bf16[2560,2048]{1,0:T(8,128)(2,1)} %get-tuple-element.42.dy_t.dyt_hbm, bf16[2560,2560]{1,0:T(8,128)(2,1)} %get-tuple-element.40.wa_hbm), kind=kOutput, calls=%fused_computation.5 | convolution fusion | flops 6712197120 | bytes 16384000 | tf_op jit(solution)/shard_map/dot_general | solution.py:961
  94.7 0.0 slice-done
  94.7 0.0 slice-done.1
  94.7 0.0 slice-done.2
  94.7 0.0 slice-done.3
  94.7 24.3 %fusion.2.qkv = bf16[1920,2048]{1,0:T(8,128)(2,1)} fusion(bf16[2560,2048]{1,0:T(8,128)(2,1)} %get-tuple-element.41.h_t.ht_hbm, bf16[2560,2560]{1,0:T(8,128)(2,1)S(1)} %bitcast.35), kind=kOutput, calls=%fused_computation.2 | convolution fusion | flops 20136591360 | bytes 28180480 | tf_op jit(solution)/shard_map/dot_general | solution.py:961
  119.0 51.2 %attention.1 = (bf16[640,2048]{1,0:T(8,128)(2,1)}, bf16[1920,2048]{1,0:T(8,128)(2,1)}, f32[80,256]{1,0:T(8,128)}, f32[80,256]{1,0:T(8,128)}, bf16[2560,1024]{1,0:T(8,128)(2,1)}) custom-call(bf16[1920,2048]{1,0:T(8,128)(2,1)} %fusion.2.qkv, bf16[640,2048]{1,0:T(8,128)(2,1)} %fusion.7.do, f32[80,1]{1,0:T(8,128)} %copy.24.qs, f32[80,1]{1,0:T(8,128)} %copy.25.ks, ...), custom_call_target="tpu_custom_call" | custom-call | flops 40000000000 | bytes 20971520 | tf_op jit(solution)/shard_map/attention/pallas_call | solution.py:762
  170.2 58.3 %attn_grads.1 = (f32[2560,2560]{1,0:T(8,128)}, bf16[2560,1024]{1,0:T(8,128)(2,1)}) custom-call(bf16[2560,2048]{1,0:T(8,128)(2,1)} %get-tuple-element.41.h_t.ht_hbm, bf16[2560,2048]{1,0:T(8,128)(2,1)} %get-tuple-element.42.dy_t.dyt_hbm, bf16[1920,2048]{1,0:T(8,128)(2,1)} %get-tuple-element.43.dqkv_t.dqt_hbm, bf16[640,2048]{1,0:T(8,128)(2,1)} %get-tuple-element.47.o_t, ...), custom_call_target="tpu_custom_call" | custom-call | flops 26843545600 | bytes 60000000 | tf_op jit(solution)/shard_map/attn_grads/pallas_call | solution.py:811
  228.5 0.0 copy-start.6
  228.5 0.0 reduce-scatter.2.cloned.1.call-update
  228.6 0.7 copy-done.6
  229.2 0.6 reshape.60.bias
  229.8 0.0 all-gather.5.cloned.1.call-done.wd0_hbm
  229.8 0.0 all-gather.3.cloned.1.call-done.wu_hbm
  229.8 466.5 %mlp_chain.1 = (bf16[2048,2560]{1,0:T(8,128)(2,1)}, f32[320,2560]{1,0:T(8,128)}, f32[320,2560]{1,0:T(8,128)}, bf16[2048,2560]{1,0:T(8,128)(2,1)}, bf16[2048,2560...) custom-call(bf16[2048,2560]{1,0:T(8,128)(2,1)} %get-tuple-element.38.h_hbm, bf16[2048,2560]{1,0:T(8,128)(2,1)} %bitcast.30, ...), custom_call_target="tpu_custom_call" | custom-call | flops 199999995904 | bytes 200000000 | tf_op jit(solution)/shard_map/mlp_chain/pallas_call | solution.py:582
  696.4 1.3 slice_bitcast_fusion.3
  697.6 1.4 slice_bitcast_fusion
  699.0 0.0 reduce-scatter.2.cloned.1.call-done.g_at
  699.0 14.7 %hand_over.1 = (bf16[2048,2560]{1,0:T(8,128)(2,1)}, f32[320,2560]{1,0:T(8,128)}, f32[320,2560]{1,0:T(8,128)}, f32[320,640]{1,0:T(8,128)}, f32[320,640]{1,0:T(8,1...) custom-call(bf16[2048,2560]{1,0:T(8,128)(2,1)} %get-tuple-element.52.gx, f32[320,2560]{1,0:T(8,128)} %get-tuple-element.53.g_up, ...), custom_call_target="tpu_custom_call" | custom-call | flops 1000000 | bytes 40000000 | tf_op jit(solution)/shard_map/hand_over/pallas_call | solution.py:914
  (1 shorter events, 0.0 us)
Async XLA Ops:
  7.2 222.7 %all-gather.5.cloned.1.call-start = ((), (), s32[]{:S(2)}) async-start(), calls=%async_computation.2 | async-start | bytes 2949120 | tf_op jit(solution)/shard_map/all_gather | solution.py:958
  7.9 71.9 %copy-start = (f32[1,2560]{1,0:T(1,128)}, f32[1,2560]{1,0:T(1,128)S(1)}, u32[]{:S(2)}) copy-start(f32[1,2560]{1,0:T(1,128)S(1)} %reshape.57.gain.scale) | copy-start | bytes 30724
  9.7 1.0 copy-start.1
  10.7 1.0 copy-start.2
  11.7 1.0 copy-start.3
  12.7 1.0 copy-start.4
  13.7 67.6 %copy-start.7 = (f32[80]{0:T(128)S(1)}, f32[80]{0:T(128)}, u32[]{:S(2)}) copy-start(f32[80]{0:T(128)} %param.22) | copy-start | bytes 964
  13.7 68.4 %copy-start.8 = (f32[80]{0:T(128)S(1)}, f32[80]{0:T(128)}, u32[]{:S(2)}) copy-start(f32[80]{0:T(128)} %param.23) | copy-start | bytes 964
  79.8 0.6 copy-start.5
  80.5 149.3 %all-gather.3.cloned.1.call-start = ((), (), s32[]{:S(2)}) async-start(), calls=%async_computation.1 | async-start | bytes 14745600 | tf_op jit(solution)/shard_map/all_gather | solution.py:957
  80.6 14.1 %slice-start = ((s8[13107200]{0:T(1024)(128)(4,1)}), s8[524288]{0:T(1024)(128)(4,1)S(1)}, s32[]{:S(2)}) async-start(s8[13107200]{0:T(1024)(128)(4,1)} %bitcast.34), calls=%async_computation.4 | async-start | bytes 1048576
  81.3 617.8 %reduce-scatter.2.cloned.1.call-start = ((), (), s32[]{:S(2)}) async-start(), calls=%async_computation.3 | async-start | bytes 29491200 | tf_op jit(solution)/shard_map/reduce_scatter | solution.py:976
  82.8 11.9 %slice-start.1 = ((s8[13107200]{0:T(1024)(128)(4,1)}), s8[4194304]{0:T(1024)(128)(4,1)S(1)}, s32[]{:S(2)}) async-start(s8[13107200]{0:T(1024)(128)(4,1)} %bitcast.34), calls=%async_computation.5 | async-start | bytes 8388608
  82.8 11.9 %slice-start.2 = ((s8[13107200]{0:T(1024)(128)(4,1)}), s8[4194304]{0:T(1024)(128)(4,1)S(1)}, s32[]{:S(2)}) async-start(s8[13107200]{0:T(1024)(128)(4,1)} %bitcast.34), calls=%async_computation.6 | async-start | bytes 8388608
  82.8 11.9 %slice-start.3 = ((s8[13107200]{0:T(1024)(128)(4,1)}), s8[4194304]{0:T(1024)(128)(4,1)S(1)}, s32[]{:S(2)}) async-start(s8[13107200]{0:T(1024)(128)(4,1)} %bitcast.34), calls=%async_computation.7 | async-start | bytes 8388608
  228.5 0.7 copy-start.6
Sparse Core Ops, SparseCore 0:
  80.6 29.9 all-gather.4
  112.5 97.7 all-gather.2
  228.7 159.4 reduce-scatter.1

commit v4 on v2

--- a/solution.py
+++ b/solution.py
@@ -293,7 +293,7 @@
             load_t[0].start()
         chain_step(4 * i + 2)
         for t in range(n_tiles):
-            if t == n_tiles // 2:
+            if t == n_tiles // 4 * 2:
                 chain_step(4 * i + 3)
             mlp_back(i, t)
         return carry
@@ -581,73 +581,273 @@
     )(normed, dy, x2, dn_attn, normed_t, dy_t, wu, wdt, b_up.reshape(1, n_hid), ln_scale.reshape(1, width), b_sum, gq, gk)
 
 
-def attn_kernel(n_heads, head_dim, qkv, do, qs, ks, o_out, dqkv, gq, gk):
+def gather_steps(me, blk, srcs, full, shard, sems):
+    own_sem, put_sem, send, got, half_send, half_got, sib_send, sib_got = sems
+    half = blk // 2
+    sib = {'fsdp': flipped(me, 1)}
+    nbr = ({'fsdp': flipped(me, 2)}, {'fsdp': flipped(me, 4)})
+
+    def rows_of(rel):
+        return pl.ds(pl.multiple_of(flipped(me, rel) * blk, blk), blk)
+
+    def half_of(rel, d):
+        return pl.ds(pl.multiple_of(flipped(me, rel) * blk + d * half, half), half)
+
+    own = full.at[rows_of(0)] if shard is None else shard
+    load = pltpu.make_async_copy(srcs, own, own_sem)
+
+    def own_to(d):
+        return remote(own, full.at[rows_of(0)], send.at[d], got.at[d], nbr[d])
+
+    def half_to(d):
+        where = half_of(4 - 2 * d, 1 - d)
+        return remote(full.at[where], full.at[where], half_send.at[d], half_got.at[d], nbr[d])
+
+    def to_sib(q):
+        return remote(own if q == 0 else full.at[rows_of(2 * q)], full.at[rows_of(2 * q)], sib_send.at[q],
+                      sib_got.at[q], sib)
+
+    def put():
+        return pltpu.make_async_copy(shard, full.at[rows_of(0)], put_sem)
+
+    def begin():
+        load.wait()
+        for d in range(2):
+            own_to(d).start()
+        to_sib(0).start()
+        if shard is not None:
+            put().start()
+
+    def middle():
+        for d in range(2):
+            own_to(d).wait_recv()
+            half_to(1 - d).start()
+            to_sib(1 + d).start()
+
+    def end():
+        for d in range(2):
+            half_to(d).wait_recv()
+        to_sib(3).start()
+        if shard is not None:
+            put().wait()
+        for d in range(2):
+            own_to(d).wait_send()
+            half_to(d).wait_send()
+        for q in range(4):
+            to_sib(q).wait()
+
+    return load.start, begin, middle, end
+
+
+def front_kernel(cfg, x, dy, wq, wk, wv, wo_t, w_up, gain, qs, ks,
+                 h, h_t, dy_t, w_qkv, w_full, o_t, dqkv_t, b_sum, gq, gk,
+                 xin, hst, ht_s, dyt_s, wp, wpt, shard, feat, ost, dst,
+                 in_sem, h_sem, t_sem, wout_sem, out_sem,
+                 own_sem, put_sem, send, got, half_send, half_got, sib_send, sib_got):
+    n_img, n_tok, n_heads, head_dim = cfg
     f32, bf16 = jnp.float32, jnp.bfloat16
+    rows, width = x.shape
+    blk = wq.shape[0]
+    n_feat = n_heads * head_dim
     scale = head_dim ** -0.5
-    n_feat = n_heads * head_dim
-
-    @pl.when(pl.program_id(0) == 0)
-    def _():
-        gq[...] = jnp.zeros_like(gq)
-        gk[...] = jnp.zeros_like(gk)
+    me = lax.axis_index('fsdp')
+
+    def sems(j):
+        return (own_sem.at[j], put_sem, send.at[j], got.at[j], half_send.at[j], half_got.at[j], sib_send.at[j],
+                sib_got.at[j])
+
+    gathers = [gather_steps(me, blk, src, wp.at[j], None, sems(j)) for j, src in enumerate((wq, wk, wv, wo_t))]
+    gathers.append(gather_steps(me, blk, w_up, w_full, shard, sems(4)))
+    for g in gathers:
+        g[0]()
+
+    def tile_rows(i):
+        return pl.ds(pl.multiple_of(i * n_tok, n_tok), n_tok)
+
+    def tile_loads(i):
+        slot = lax.rem(i, 2)
+        return [pltpu.make_async_copy(x.at[tile_rows(i)], xin.at[0, slot], in_sem.at[0, slot]),
+                pltpu.make_async_copy(dy.at[tile_rows(i)], xin.at[1, slot], in_sem.at[1, slot])]
+
+    def h_out(i):
+        slot = lax.rem(i, 2)
+        return pltpu.make_async_copy(hst.at[slot], h.at[tile_rows(i)], h_sem.at[slot])
+
+    for c in tile_loads(0):
+        c.start()
+    barrier = pltpu.get_barrier_semaphore()
+    for rel in (1, 2, 4):
+        pl.semaphore_signal(barrier, inc=1, device_id={'fsdp': flipped(me, rel)}, device_id_type=MESH)
+    pl.semaphore_wait(barrier, 3)
+    gathers[0][1]()
+    gathers[1][1]()
+    b_sum[...] = jnp.zeros_like(b_sum)
+    gq[...] = jnp.zeros_like(gq)
+    gk[...] = jnp.zeros_like(gk)
+
+    def layer_norm(i, carry):
+        slot = lax.rem(i, 2)
+
+        @pl.when(i + 1 < n_img)
+        def _():
+            for c in tile_loads(i + 1):
+                c.start()
+
+        @pl.when(i == n_img // 2)
+        def _():
+            gathers[0][2]()
+            gathers[2][1]()
+
+        @pl.when(i == n_img - 1)
+        def _():
+            gathers[1][2]()
+            gathers[3][1]()
+        for c in tile_loads(i):
+            c.wait()
+
+        @pl.when(i >= 2)
+        def _():
+            h_out(i - 2).wait()
+        cols = pl.ds(pl.multiple_of(i * n_tok, n_tok), n_tok)
+        xv = xin[0, slot].astype(f32)
+        cen = xv - jnp.mean(xv, axis=-1, keepdims=True)
+        inv = lax.rsqrt(jnp.mean(cen * cen, axis=-1, keepdims=True) + EPS)
+        hv = (cen * inv * gain[...]).astype(bf16)
+        hst[slot] = hv
+        h_out(i).start()
+        ht_s[:, cols] = hv.T
+        dv = xin[1, slot]
+        dyt_s[:, cols] = dv.T
+        b_sum[...] += jnp.sum(dv.astype(f32).reshape(-1, 8, width), axis=0)
+        return carry
+
+    lax.fori_loop(0, n_img, layer_norm, 0)
+    t_out = [pltpu.make_async_copy(ht_s, h_t, t_sem.at[0]), pltpu.make_async_copy(dyt_s, dy_t, t_sem.at[1])]
+    for c in t_out:
+        c.start()
+
+    n_tile = min(512, rows)
+
+    def project(p):
+        lhs = (ht_s, ht_s, ht_s, dyt_s)[p]
+        wpt[...] = wp[p].T
+
+        def body(n, carry):
+            cols = pl.ds(pl.multiple_of(n * n_tile, n_tile), n_tile)
+            feat[pl.ds(p * n_feat, n_feat), cols] = jnp.dot(wpt[...], lhs[:, cols], preferred_element_type=f32).astype(bf16)
+            return carry
+        lax.fori_loop(0, rows // n_tile, body, 0)
+
+    w_out = [pltpu.make_async_copy(wp.at[p], w_qkv.at[:, pl.ds(p * n_feat, n_feat)], wout_sem.at[p]) for p in range(3)]
+    for p in range(4):
+        gathers[p][3]()
+        if p < 3:
+            w_out[p].start()
+        project(p)
+        if p < 2:
+            gathers[p + 2][2]()
+        if p == 1:
+            gathers[4][1]()
 
     def norm(raw):
         cen = raw - jnp.mean(raw, axis=0, keepdims=True)
         inv = lax.rsqrt(jnp.mean(cen * cen, axis=0, keepdims=True) + EPS)
         return cen * inv, inv
 
-    def norm_back(d, hat, inv, gain):
-        w = d * gain
+    def norm_back(d, hat, inv, gn):
+        w = d * gn
         return inv * (w - jnp.mean(w, axis=0, keepdims=True) - hat * jnp.mean(w * hat, axis=0, keepdims=True))
 
     def mm(lhs, rhs, dims):
         return lax.dot_general(lhs, rhs, (dims, ((), ())), preferred_element_type=f32)
 
-    for h in range(n_heads):
-        lo = h * head_dim
-        q_rows, k_rows, v_rows = (pl.ds(j * n_feat + lo, head_dim) for j in range(3))
-        q_hat, q_inv = norm(qkv[q_rows, :].astype(f32))
-        k_hat, k_inv = norm(qkv[k_rows, :].astype(f32))
-        qn = (q_hat * qs[...]).astype(bf16)
-        kn = (k_hat * ks[...]).astype(bf16)
-        v = qkv[v_rows, :]
-        d_o = do[pl.ds(lo, head_dim), :]
-        logits = mm(kn, qn, ((0,), (0,))) * scale
-        e = jnp.exp(logits - jnp.max(logits, axis=0, keepdims=True))
-        p = e * (1.0 / jnp.sum(e, axis=0, keepdims=True))
-        pb = p.astype(bf16)
-        o_out[pl.ds(lo, head_dim), :] = mm(v, pb, ((1,), (0,))).astype(bf16)
-        dqkv[v_rows, :] = mm(d_o, pb, ((1,), (1,))).astype(bf16)
-        dp = mm(v, d_o, ((0,), (0,))).astype(bf16).astype(f32)
-        ds = (p * (dp - jnp.sum(p * dp, axis=0, keepdims=True)) * scale).astype(bf16)
-        dqn = mm(kn, ds, ((1,), (0,))).astype(bf16).astype(f32)
-        dkn = mm(qn, ds, ((1,), (1,))).astype(bf16).astype(f32)
-        gq[...] += dqn * q_hat
-        gk[...] += dkn * k_hat
-        dqkv[q_rows, :] = norm_back(dqn, q_hat, q_inv, qs[...]).astype(bf16)
-        dqkv[k_rows, :] = norm_back(dkn, k_hat, k_inv, ks[...]).astype(bf16)
-
-
-def attn_call(qkv_t, do_t, q_scale, k_scale, n_img):
-    n_feat, rows = do_t.shape
+    def outs(i):
+        slot = lax.rem(i, 2)
+        cols = pl.ds(pl.multiple_of(i * n_tok, n_tok), n_tok)
+        return [pltpu.make_async_copy(ost.at[slot], o_t.at[:, cols], out_sem.at[0, slot]),
+                pltpu.make_async_copy(dst.at[slot], dqkv_t.at[:, cols], out_sem.at[1, slot])]
+
+    def attention(i, carry):
+        slot = lax.rem(i, 2)
+        cols = pl.ds(pl.multiple_of(i * n_tok, n_tok), n_tok)
+
+        @pl.when(i == n_img // 2)
+        def _():
+            gathers[4][2]()
+
+        @pl.when(i >= 2)
+        def _():
+            for c in outs(i - 2):
+                c.wait()
+        for hd in range(n_heads):
+            lo = hd * head_dim
+            q_rows, k_rows, v_rows, o_rows = (pl.ds(j * n_feat + lo, head_dim) for j in range(4))
+            q_hat, q_inv = norm(feat[q_rows, cols].astype(f32))
+            k_hat, k_inv = norm(feat[k_rows, cols].astype(f32))
+            qn = (q_hat * qs[...]).astype(bf16)
+            kn = (k_hat * ks[...]).astype(bf16)
+            v = feat[v_rows, cols]
+            d_o = feat[o_rows, cols]
+            logits = mm(kn, qn, ((0,), (0,))) * scale
+            e = jnp.exp(logits - jnp.max(logits, axis=0, keepdims=True))
+            p = e * (1.0 / jnp.sum(e, axis=0, keepdims=True))
+            pb = p.astype(bf16)
+            ost[slot, pl.ds(lo, head_dim), :] = mm(v, pb, ((1,), (0,))).astype(bf16)
+            dst[slot, v_rows, :] = mm(d_o, pb, ((1,), (1,))).astype(bf16)
+            dp = mm(v, d_o, ((0,), (0,))).astype(bf16).astype(f32)
+            ds = (p * (dp - jnp.sum(p * dp, axis=0, keepdims=True)) * scale).astype(bf16)
+            dqn = mm(kn, ds, ((1,), (0,))).astype(bf16).astype(f32)
+            dkn = mm(qn, ds, ((1,), (1,))).astype(bf16).astype(f32)
+            gq[...] += dqn * q_hat
+            gk[...] += dkn * k_hat
+            dst[slot, q_rows, :] = norm_back(dqn, q_hat, q_inv, qs[...]).astype(bf16)
+            dst[slot, k_rows, :] = norm_back(dkn, k_hat, k_inv, ks[...]).astype(bf16)
+        for c in outs(i):
+            c.start()
+        return carry
+
+    lax.fori_loop(0, n_img, attention, 0)
+    gathers[4][3]()
+    for i in range(n_img - 2, n_img):
+        h_out(i).wait()
+        for c in outs(i):
+            c.wait()
+    for c in t_out + w_out:
+        c.wait()
+
+
+def front_call(mesh, x2, dy, ln_scale, attn_weights, w_up, q_scale, k_scale, n_img):
+    rows, width = x2.shape
+    n_tok = rows // n_img
+    blk, n_feat = attn_weights[0].shape
     head_dim = q_scale.shape[0]
-    n_tok = rows // n_img
+    n_hid = w_up.shape[1]
     f32, bf16 = jnp.float32, jnp.bfloat16
-    col = lambda n: pl.BlockSpec((n, n_tok), lambda i: (0, i))
-    whole = lambda shape: pl.BlockSpec(shape, lambda i: (0, 0))
-    n_heads = n_feat // head_dim
+    shape, vm, dma = jax.ShapeDtypeStruct, pltpu.VMEM, pltpu.SemaphoreType.DMA
+    any_spec = pl.BlockSpec(memory_space=pl.ANY)
+    vmem = pl.BlockSpec(memory_space=pltpu.VMEM)
     return pl.pallas_call(
-        functools.partial(attn_kernel, n_heads, head_dim),
-        grid=(n_img,),
-        out_shape=(jax.ShapeDtypeStruct((n_feat, rows), bf16), jax.ShapeDtypeStruct((3 * n_feat, rows), bf16),
-                   jax.ShapeDtypeStruct((head_dim, n_tok), f32), jax.ShapeDtypeStruct((head_dim, n_tok), f32)),
-        in_specs=[col(3 * n_feat), col(n_feat), whole((head_dim, 1)), whole((head_dim, 1))],
-        out_specs=(col(n_feat), col(3 * n_feat), whole((head_dim, n_tok)), whole((head_dim, n_tok))),
-        compiler_params=pltpu.CompilerParams(dimension_semantics=('arbitrary',), vmem_limit_bytes=32 << 20),
-        cost_estimate=pl.CostEstimate(flops=25_000_000_000, bytes_accessed=8 * n_feat * rows * 2,
-                                      transcendentals=n_img * n_heads * n_tok * n_tok),
-        name='attention',
-    )(qkv_t, do_t, q_scale.reshape(head_dim, 1), k_scale.reshape(head_dim, 1))
+        functools.partial(front_kernel, (n_img, n_tok, n_feat // head_dim, head_dim)),
+        out_shape=(shape((rows, width), bf16), shape((width, rows), bf16), shape((width, rows), bf16),
+                   shape((width, 3 * n_feat), bf16), shape((width, n_hid), bf16), shape((n_feat, rows), bf16),
+                   shape((3 * n_feat, rows), bf16), shape((8, width), f32), shape((head_dim, n_tok), f32),
+                   shape((head_dim, n_tok), f32)),
+        in_specs=[any_spec] * 7 + [vmem] * 3,
+        out_specs=(any_spec,) * 7 + (vmem,) * 3,
+        scratch_shapes=[
+            vm((2, 2, n_tok, width), bf16), vm((2, n_tok, width), bf16),
+            vm((width, rows), bf16), vm((width, rows), bf16),
+            vm((4, width, n_feat), bf16), vm((n_feat, width), bf16),
+            vm((blk, n_hid), bf16), vm((4 * n_feat, rows), bf16),
+            vm((2, n_feat, n_tok), bf16), vm((2, 3 * n_feat, n_tok), bf16),
+            dma((2, 2)), dma((2,)), dma((2,)), dma((3,)), dma((2, 2)),
+            dma((5,)), dma, dma((5, 2)), dma((5, 2)), dma((5, 2)), dma((5, 2)), dma((5, 4)), dma((5, 4)),
+        ],
+        compiler_params=pltpu.CompilerParams(collective_id=1, has_side_effects=True, vmem_limit_bytes=67_043_328),
+        cost_estimate=pl.CostEstimate(flops=60_000_000_000, bytes_accessed=100_000_000, transcendentals=5_000_000),
+        name='front',
+    )(x2, dy, *attn_weights, w_up, ln_scale.reshape(1, width), q_scale.reshape(head_dim, 1),
+      k_scale.reshape(head_dim, 1))
 
 
 def outer_kernel(h_t, dy_t, dqkv_t, o_t, out):
@@ -677,114 +877,52 @@
     )(h_t, dy_t, d_qkv_t, o_t)
 
 
-def prep_kernel(n_fsdp, n_img, x, dy, gain, wq, wk, wv, wo_t, h, h_t, dy_t, b_sum, w_full, shard, own_sem, put_sem,
-                send, got, half_send, half_got, sib_send, sib_got):
-    f32, bf16 = jnp.float32, jnp.bfloat16
-    i = pl.program_id(0)
-    me = lax.axis_index('fsdp')
-    blk = shard.shape[0]
-    half = blk // 2
-    sib = {'fsdp': flipped(me, 1)}
-    nbr = ({'fsdp': flipped(me, 2)}, {'fsdp': flipped(me, 4)})
-    pieces = (wq, wk, wv, wo_t)
-
-    def rows_of(rel):
-        return pl.ds(pl.multiple_of(flipped(me, rel) * blk, blk), blk)
-
-    def half_of(rel, d):
-        return pl.ds(pl.multiple_of(flipped(me, rel) * blk + d * half, half), half)
-
-    def load(j):
-        n = pieces[j].shape[1]
-        return pltpu.make_async_copy(pieces[j], shard.at[:, pl.ds(j * n, n)], own_sem.at[j])
-
-    def put():
-        return pltpu.make_async_copy(shard, w_full.at[rows_of(0)], put_sem)
-
-    def own_to(d):
-        return remote(shard, w_full.at[rows_of(0)], send.at[d], got.at[d], nbr[d])
-
-    def half_to(d):
-        rel = 4 - 2 * d
-        return remote(w_full.at[half_of(rel, 1 - d)], w_full.at[half_of(rel, 1 - d)], half_send.at[d], half_got.at[d],
-                      nbr[d])
-
-    def to_sib(q):
-        src = shard if q == 0 else w_full.at[rows_of(2 * q)]
-        return remote(src, w_full.at[rows_of(2 * q)], sib_send.at[q], sib_got.at[q], sib)
-
-    @pl.when(i == 0)
-    def _():
-        for j in range(4):
-            load(j).start()
-        barrier = pltpu.get_barrier_semaphore()
-        for where in (sib,) + nbr:
-            pl.semaphore_signal(barrier, inc=1, device_id=where, device_id_type=MESH)
-        pl.semaphore_wait(barrier, 3)
-        for j in range(4):
-            load(j).wait()
-        for d in range(2):
-            own_to(d).start()
-        to_sib(0).start()
-        put().start()
-        b_sum[...] = jnp.zeros_like(b_sum)
-
-    width = x.shape[1]
-    xv = x[...].astype(f32)
-    cen = xv - jnp.mean(xv, axis=-1, keepdims=True)
-    inv = lax.rsqrt(jnp.mean(cen * cen, axis=-1, keepdims=True) + EPS)
-    hv = (cen * inv * gain[...]).astype(bf16)
-    h[...] = hv
-    h_t[...] = hv.T
-    dv = dy[...]
-    dy_t[...] = dv.T
-    b_sum[...] += jnp.sum(dv.astype(f32).reshape(-1, 8, width), axis=0)
-
-    @pl.when(i == n_img - 1)
-    def _():
-        own_to(0).wait_recv()
-        half_to(1).start()
-        to_sib(1).start()
-        own_to(1).wait_recv()
-        half_to(0).start()
-        to_sib(2).start()
-        half_to(0).wait_recv()
-        half_to(1).wait_recv()
-        to_sib(3).start()
-        put().wait()
-        for d in range(2):
-            own_to(d).wait_send()
-            half_to(d).wait_send()
-        for q in range(4):
-            to_sib(q).wait()
-
-
-def prep_call(mesh, x2, dy, ln_scale, attn_weights, n_img):
-    rows, width = x2.shape
-    n_tok = rows // n_img
-    n_fsdp = mesh.shape['fsdp']
-    blk = attn_weights[0].shape[0]
-    n_all = sum(w.shape[1] for w in attn_weights)
-    f32, bf16 = jnp.float32, jnp.bfloat16
-    dma = pltpu.SemaphoreType.DMA
-    row = pl.BlockSpec((n_tok, width), lambda i: (i, 0))
-    col = pl.BlockSpec((width, n_tok), lambda i: (0, i))
+def hand_over_kernel(n_feat, gx, g_up, g_dn, g_at, o_gx, o_up, o_dn, o_q, o_k, o_v, o_o, b_gx, b_up, b_dn, b_at,
+                     in_sem, out_sem):
+    n_cut = b_gx.shape[0]
+    step = b_gx.shape[1]
+    loads, stores = [], []
+    for j in range(n_cut):
+        part = pl.ds(j * step, step)
+        loads.append((gx.at[part], b_gx.at[j]))
+        stores.append([(b_gx.at[j], o_gx.at[part])])
+    for src, buf, dst in ((g_up, b_up, o_up), (g_dn, b_dn, o_dn)):
+        loads.append((src, buf))
+        stores.append([(buf, dst)])
+    loads.append((g_at, b_at))
+    stores.append([(b_at.at[:, pl.ds(j * n_feat, n_feat)], dst) for j, dst in enumerate((o_q, o_k, o_v, o_o))])
+    for j, (src, buf) in enumerate(loads):
+        pltpu.make_async_copy(src, buf, in_sem.at[j]).start()
+    at, pending = 0, []
+    for j, (src, buf) in enumerate(loads):
+        pltpu.make_async_copy(src, buf, in_sem.at[j]).wait()
+        for src2, dst in stores[j]:
+            pending.append(pltpu.make_async_copy(src2, dst, out_sem.at[at]))
+            pending[-1].start()
+            at += 1
+    for c in pending:
+        c.wait()
+
+
+def hand_over(gx, g_up, g_dn, g_at, n_feat):
+    rows, width = gx.shape
+    blk = g_at.shape[0]
+    n_cut = 8
+    f32 = jnp.float32
+    shape, vm, dma = jax.ShapeDtypeStruct, pltpu.VMEM, pltpu.SemaphoreType.DMA
     any_spec = pl.BlockSpec(memory_space=pl.ANY)
-    shape = jax.ShapeDtypeStruct
+    side = shape((blk, n_feat), f32)
     return pl.pallas_call(
-        functools.partial(prep_kernel, n_fsdp, n_img),
-        grid=(n_img,),
-        out_shape=(shape((rows, width), bf16), shape((width, rows), bf16), shape((width, rows), bf16),
-                   shape((8, width), f32), shape((width, n_all), bf16)),
-        in_specs=[row, row, pl.BlockSpec((1, width), lambda i: (0, 0))] + [any_spec] * 4,
-        out_specs=(row, col, col, pl.BlockSpec((8, width), lambda i: (0, 0)), any_spec),
-        scratch_shapes=[pltpu.VMEM((blk, n_all), bf16), dma((4,)), dma, dma((2,)), dma((2,)), dma((2,)), dma((2,)),
-                        dma((4,)), dma((4,))],
-        compiler_params=pltpu.CompilerParams(dimension_semantics=('arbitrary',), collective_id=1, has_side_effects=True,
-                                             vmem_limit_bytes=48 << 20),
-        cost_estimate=pl.CostEstimate(flops=60_000_000_000, bytes_accessed=10 * rows * width, transcendentals=0),
-        name='prep',
-    )(x2, dy, ln_scale.reshape(1, width), *attn_weights)
+        functools.partial(hand_over_kernel, n_feat),
+        out_shape=(shape(gx.shape, gx.dtype), shape(g_up.shape, f32), shape(g_dn.shape, f32), side, side, side, side),
+        in_specs=[any_spec] * 4,
+        out_specs=(any_spec,) * 7,
+        scratch_shapes=[vm((n_cut, rows // n_cut, width), gx.dtype), vm(g_up.shape, f32), vm(g_dn.shape, f32),
+                        vm(g_at.shape, f32), dma((n_cut + 3,)), dma((n_cut + 6,))],
+        compiler_params=pltpu.CompilerParams(vmem_limit_bytes=60 << 20),
+        cost_estimate=pl.CostEstimate(flops=1_000_000, bytes_accessed=40_000_000, transcendentals=0),
+        name='hand_over',
+    )(gx, g_up, g_dn, g_at)
 
 
 def solution(mesh):
@@ -808,20 +946,10 @@
 
         x2 = x_in.reshape(num_rows, width)
         dy = grad_y.reshape(num_rows, width)
-        normed, normed_t, dy_t, b_sum, attn_full = prep_call(
-            mesh, x2, dy, ln_scale, (w_query, w_key, w_value, w_out.T), num_img)
-        wqkv_full = attn_full[:, :3 * n_qkv]
-        wot_full = attn_full[:, 3 * n_qkv:]
-        w_up, w_down_t, attn_full = lax.optimization_barrier((w_up, w_down.T, attn_full))
-        wu_full = gather_rows(w_up)
+        normed, normed_t, dy_t, wqkv_full, wu_full, attn_t, d_qkv_t, b_sum, gq, gk = front_call(
+            mesh, x2, dy, ln_scale, (w_query, w_key, w_value, w_out.T), w_up, q_scale, k_scale, num_img)
+        w_down_t, attn_t = lax.optimization_barrier((w_down.T, attn_t))
         wdt_full = gather_rows(w_down_t)
-
-        def contract(lhs, rhs, dim):
-            return lax.dot_general(lhs, rhs, (((dim,), (dim,)), ((), ())), preferred_element_type=fp32)
-
-        qkv_t = contract(wqkv_full, normed_t, 0).astype(bf16)
-        d_attn_t = contract(wot_full, dy_t, 0).astype(bf16)
-        attn_t, d_qkv_t, gq, gk = attn_call(qkv_t, d_attn_t, q_scale, k_scale, num_img)
         grad_w_attn = attn_grads_call(normed_t, dy_t, d_qkv_t, attn_t)
         d_normed = lax.dot_general(d_qkv_t, wqkv_full, (((0,), (1,)), ((), ())), preferred_element_type=fp32)
 
@@ -831,8 +959,8 @@
         tp_lo = n_up + n_wide
         q_lo = tp_lo + n_wide
         g_attn = scatter_rows(grad_w_attn)
-        return (grad_x.reshape(x_in.shape), g_attn[:, :n_qkv], g_attn[:, n_qkv:2 * n_qkv], g_attn[:, 2 * n_qkv:3 * n_qkv],
-                g_attn[:, 3 * n_qkv:].T, g_up, small[:n_up].reshape(-1),
+        grad_x, g_up, g_down_t, g_q, g_k, g_v, g_out_t = hand_over(grad_x, g_up, g_down_t, g_attn, n_qkv)
+        return (grad_x.reshape(x_in.shape), g_q, g_k, g_v, g_out_t.T, g_up, small[:n_up].reshape(-1),
                 g_down_t.T, small[n_up:tp_lo].reshape(-1), small[tp_lo:q_lo].reshape(-1),
                 small[q_lo, :head_dim], small[q_lo + 1, :head_dim])
 

time: 679 us -> 645 us (0.950)
  matrix products: 65.7 us -> 29 us
  local copies, waits for them, and re-layouts: 33.6 us -> 8 us
  Pallas kernels: 554 us -> 579 us
    dot_general x2 -> x0, matrix products: 36.7 us -> none  [contract(): lax.dot_general(lhs, rhs, (((dim,), (dim,)), ((), ())), preferred_element...]
    pallas_call x2, Pallas kernels: 111 us -> 136 us  [the longest x1 121 us: front_call(): pl.pallas_call(functools.partial(front_kernel, (n_img, n_tok, n_feat // h...]
    unnamed x31 -> x2, local copies, waits for them, and re-layouts: 25.8 us -> 0.68 us
  transfers between devices with their start and end apart: 3 -> 2, of which waited for: 0 -> 1; matrix products, arithmetic and copies ran while one was open for 10% -> 5% of each run, Pallas kernels for 73% -> 70%
where the time goes in v4:
time: 645 us; the launch traced here: 636 us
  Pallas kernels  579 us (90%)
  matrix products  29 us (4%)
  between operations  14.5 us (2%)
  local copies, waits for them, and re-layouts  8 us (1%)
    pallas_call x1, Pallas kernels, fused_call(): pl.pallas_call(kern, out_shape=(shape((rows, width), bf16), shape((blk, n...  404 us
    pallas_call x1, Pallas kernels, front_call(): pl.pallas_call(functools.partial(front_kernel, (n_img, n_tok, n_feat // h...  121 us
    pallas_call x1, Pallas kernels, attn_grads_call(): pl.pallas_call(outer_kernel, grid=(width // tile,), out_shape=jax.ShapeDt...  39.1 us
    dot_general x1, matrix products, local_step(): lax.dot_general(d_qkv_t, wqkv_full, (((0,), (1,)), ((), ())), preferred_e...  29 us
    pallas_call x1, Pallas kernels, hand_over(): pl.pallas_call(functools.partial(hand_over_kernel, n_feat), out_shape=(sh...  14.7 us
  transfers between devices with their start and end apart: 2, of which 1 were waited for; matrix products, arithmetic and copies ran while one was open for 5% of the time, Pallas kernels for 70%

profile of v4, /device:TPU:0, one launch (start us, length us, event | category | flops | bytes accessed | tf_op | source)
XLA Modules:
  0.0 636.1 jit_solution(7566945584728460738)
XLA Ops:
  7.2 0.0 all-gather.2.cloned.1.call-start
  7.2 1.3 reshape.57.gain.scale
  8.5 1.4 copy.24.qs
  9.9 1.4 copy.25.ks
  11.3 121.3 %front.1 = (bf16[2048,2560]{1,0:T(8,128)(2,1)}, bf16[2560,2048]{1,0:T(8,128)(2,1)}, bf16[2560,2048]{1,0:T(8,128)(2,1)}, bf16[2560,1920]{1,0:T(8,128)(2,1)}, bf16...) custom-call(bf16[2048,2560]{1,0:T(8,128)(2,1)} %bitcast.24, ...), custom_call_target="tpu_custom_call" | custom-call | flops 60000002048 | bytes 100000000 | tf_op jit(solution)/shard_map/front/pallas_call | solution.py:829
  132.5 0.0 all-gather.2.cloned.1.call-update
  132.6 0.0 reduce-scatter.2.cloned.1.call-start
  132.6 39.1 %attn_grads.1 = f32[2560,2560]{1,0:T(8,128)} custom-call(bf16[2560,2048]{1,0:T(8,128)(2,1)} %get-tuple-element.38.ht_hbm.h_t, bf16[2560,2048]{1,0:T(8,128)(2,1)} %get-tuple-element.39.dyt_hbm.dy_t, bf16[1920,2048]{1,0:T(8,128)(2,1)} %get-tuple-element.36.dqkv_t, bf16[640,2048]{1,0:T(8,128)(2,1)} %get-tuple-element.49.o_t), custom_call_target="tpu_custom_call" | custom-call | flops 26843545600 | bytes 60000000 | tf_op jit(solution)/shard_map/attn_grads/pallas_call | solution.py:868
  171.7 0.0 copy-start
  171.7 0.0 reduce-scatter.2.cloned.1.call-update
  171.8 0.7 copy-done
  172.4 0.6 reshape.60.bias
  173.1 29.0 %fusion.dna_hbm = f32[2048,2560]{1,0:T(8,128)} fusion(bf16[1920,2048]{1,0:T(8,128)(2,1)} %get-tuple-element.36.dqkv_t, bf16[2560,1920]{1,0:T(8,128)(2,1)} %get-tuple-element.37), kind=kOutput, calls=%fused_computation.5 | convolution fusion | flops 20132659200 | bytes 38666240 | tf_op jit(solution)/shard_map/dot_general | solution.py:954
  202.1 5.0 all-gather.2.cloned.1.call-done.wdt_hbm
  207.1 404.4 %mlp_chain.1 = (bf16[2048,2560]{1,0:T(8,128)(2,1)}, f32[320,2560]{1,0:T(8,128)}, f32[320,2560]{1,0:T(8,128)}, bf16[2048,2560]{1,0:T(8,128)(2,1)}, bf16[2048,2560...) custom-call(bf16[2048,2560]{1,0:T(8,128)(2,1)} %get-tuple-element.35.h_hbm, bf16[2048,2560]{1,0:T(8,128)(2,1)} %bitcast.27, ...), custom_call_target="tpu_custom_call" | custom-call | flops 199999995904 | bytes 200000000 | tf_op jit(solution)/shard_map/mlp_chain/pallas_call | solution.py:548
  611.5 1.3 slice_bitcast_fusion.3
  612.8 1.4 slice_bitcast_fusion
  614.2 0.0 reduce-scatter.2.cloned.1.call-done.g_at
  614.2 14.7 %hand_over.1 = (bf16[2048,2560]{1,0:T(8,128)(2,1)}, f32[320,2560]{1,0:T(8,128)}, f32[320,2560]{1,0:T(8,128)}, f32[320,640]{1,0:T(8,128)}, f32[320,640]{1,0:T(8,1...) custom-call(bf16[2048,2560]{1,0:T(8,128)(2,1)} %get-tuple-element.46.gx, f32[320,2560]{1,0:T(8,128)} %get-tuple-element.47.g_up, ...), custom_call_target="tpu_custom_call" | custom-call | flops 1000000 | bytes 40000000 | tf_op jit(solution)/shard_map/hand_over/pallas_call | solution.py:915
Async XLA Ops:
  7.2 199.9 %all-gather.2.cloned.1.call-start = ((), (), s32[]{:S(2)}) async-start(), calls=%async_computation.1 | async-start | bytes 14745600 | tf_op jit(solution)/shard_map/all_gather | solution.py:952
  132.6 481.6 %reduce-scatter.2.cloned.1.call-start = ((), (), s32[]{:S(2)}) async-start(), calls=%async_computation.2 | async-start | bytes 29491200 | tf_op jit(solution)/shard_map/reduce_scatter | solution.py:961
  171.7 0.7 copy-start
Sparse Core Ops, SparseCore 0:
  132.7 74.3 all-gather.1
  210.7 159.4 reduce-scatter.1

commit v5 on v4

--- a/solution.py
+++ b/solution.py
@@ -7,6 +7,7 @@
 from jax.sharding import PartitionSpec as P
 
 EPS = 1e-6
+LOG2E = 1.4426950408889634
 
 
 MESH = pl.DeviceIdType.MESH
@@ -28,18 +29,24 @@
     return out
 
 
+def as_row(tiles):
+    return jnp.concatenate([tiles[j:j + 1, :] for j in range(tiles.shape[0])], axis=1)
+
+
 def remote(src, dst, send, recv, where):
     return pltpu.make_async_remote_copy(src_ref=src, dst_ref=dst, send_sem=send, recv_sem=recv,
                                         device_id=where, device_id_type=MESH)
 
 
-def fused_kernel(cfg, h_hbm, dy_hbm, x_hbm, dna_hbm, ht_hbm, dyt_hbm, wu_hbm, wdt_hbm, bias, scale, b_sum, gq, gk,
+def fused_kernel(cfg, h_hbm, dy_hbm, x_hbm, dna_hbm, ht_hbm, dyt_hbm, wu_hbm, wdt_hbm, bias_t, scale_t, b_sum, gq, gk,
                  gx, g_up, g_dn, act_hbm, dh_hbm, dn_hbm, small_out,
                  wu, wdt, hb, yb, actb, dhb, gb, psum, s0, r0, r1, r2, bblk,
                  part, part2, xb, dyb, recv, sbuf, dxb, ln_acc, pack, rs_f, rs_t,
+                 bias, scale, lnb, ln_in,
                  w_sem, hb_sem, out_sem, dn_sem, b_sem, s0_send, r0_sem, d_send, r1_sem, xy_send, r2_sem, g_sem,
                  c0, c1, c2,
-                 part_sem, part2_sem, x_sem, dy_sem, fsend, frecv, bsend, brecv, lsem, credit, xs_send, xs_recv):
+                 part_sem, part2_sem, x_sem, dy_sem, fsend, frecv, bsend, brecv, lsem, credit, xs_send, xs_recv,
+                 ln_send, ln_recv):
     n_tp, n_fsdp, n_img, n_tok = cfg
     f32, bf16 = jnp.float32, jnp.bfloat16
     rows, width = h_hbm.shape
@@ -81,11 +88,14 @@
         for c in load_w(f):
             c.start()
     barrier = pltpu.get_barrier_semaphore()
-    for rel in range(1, n_fsdp):
-        pl.semaphore_signal(barrier, inc=1, device_id={'fsdp': flipped(me, rel)}, device_id_type=MESH)
-    for rel in range(1, n_tp):
-        pl.semaphore_signal(barrier, inc=1, device_id={'tp': flipped(my_tp, rel)}, device_id_type=MESH)
-    pl.semaphore_wait(barrier, n_fsdp + n_tp - 2)
+    for t in range(n_tp):
+        for rel in range(n_fsdp):
+            if t or rel:
+                pl.semaphore_signal(barrier, inc=1, device_id={'tp': flipped(my_tp, t), 'fsdp': flipped(me, rel)},
+                                    device_id_type=MESH)
+    pl.semaphore_wait(barrier, n_fsdp * n_tp - 1)
+    bias[...] = as_row(bias_t[...])
+    scale[...] = as_row(scale_t[...])
     ln_acc[...] = jnp.zeros_like(ln_acc)
     gb[...] = jnp.zeros_like(gb)
 
@@ -433,6 +443,88 @@
         def _():
             grad_out(j, g_up).start()
 
+    lanes = 128
+    n_up, n_wide = n_hid // lanes, width // lanes
+    n_rows = pack.shape[0]
+    tp_lo = n_up + n_wide
+
+    def tree(terms):
+        while len(terms) > 1:
+            terms = [terms[j] + terms[j + 1] for j in range(0, len(terms), 2)]
+        return terms[0]
+
+    def to_fsdp(rel):
+        return remote(pack, rs_f.at[rel - 1], xs_send.at[rel - 1], xs_recv.at[rel - 1], {'fsdp': flipped(me, rel)})
+
+    def to_tp(rel):
+        return remote(pack.at[pl.ds(tp_lo, n_rows - tp_lo)], rs_t.at[rel - 1], xs_send.at[n_fsdp + rel - 2],
+                      xs_recv.at[n_fsdp + rel - 2], {'tp': flipped(my_tp, rel)})
+
+    def smalls_begin():
+        pack[...] = jnp.zeros_like(pack)
+        gb_row = jnp.sum(gb[...], axis=0, keepdims=True)
+        for j in range(n_up):
+            pack[pl.ds(j, 1), :] = gb_row[:, j * lanes:(j + 1) * lanes]
+        bs_row = jnp.sum(b_sum[...], axis=0, keepdims=True)
+        for j in range(n_wide):
+            pack[pl.ds(n_up + j, 1), :] = bs_row[:, j * lanes:(j + 1) * lanes]
+        for j, ref in enumerate((gq, gk)):
+            pack[pl.ds(tp_lo + j, 1), pl.ds(0, ref.shape[0])] = jnp.sum(ref[...].T, axis=0, keepdims=True)
+        for rel in range(1, n_fsdp):
+            to_fsdp(rel).start()
+
+    def smalls_middle():
+        for rel in range(1, n_fsdp):
+            to_fsdp(rel).wait()
+        pack[...] = tree([pack[...]] + [rs_f[rel - 1] for rel in range(1, n_fsdp)])
+        for rel in range(1, n_tp):
+            to_tp(rel).start()
+
+    def smalls_end():
+        for rel in range(1, n_tp):
+            to_tp(rel).wait()
+        small_out[pl.ds(0, tp_lo), :] = pack[pl.ds(0, tp_lo), :]
+        small_out[pl.ds(tp_lo, n_rows - tp_lo), :] = tree(
+            [pack[pl.ds(tp_lo, n_rows - tp_lo)]] + [rs_t[rel - 1] for rel in range(1, n_tp)])
+
+    is_root = (my_tp == 0) | (my_tp == last)
+    root_side = (last - my_tp) // last
+
+    def ln_to(t, rel):
+        return remote(lnb, ln_in.at[root_side * n_fsdp + rel], ln_send.at[t * n_fsdp + rel],
+                      ln_recv.at[root_side * n_fsdp + rel], {'tp': flipped(my_tp, t), 'fsdp': flipped(me, rel)})
+
+    ln_places = [(t, rel) for t in range(n_tp) for rel in range(n_fsdp) if t or rel]
+
+    def ln_begin():
+        @pl.when(is_root)
+        def _():
+            lnb[...] = jnp.zeros_like(lnb)
+            ln_row = jnp.sum(ln_acc[...], axis=0, keepdims=True)
+            for j in range(n_wide):
+                lnb[pl.ds(j, 1), :] = ln_row[:, j * lanes:(j + 1) * lanes]
+            ln_in[root_side * n_fsdp] = lnb[...]
+            for t, rel in ln_places:
+                ln_to(t, rel).start()
+
+    def ln_end():
+        for side in range(2):
+            for rel in range(n_fsdp):
+                def arrived():
+                    remote(lnb, ln_in.at[side * n_fsdp + rel], ln_send.at[rel], ln_recv.at[side * n_fsdp + rel],
+                           {'fsdp': flipped(me, rel)}).wait_recv()
+                if rel:
+                    arrived()
+                else:
+                    pl.when(my_tp != (1 - side) * last)(arrived)
+
+        @pl.when(is_root)
+        def _():
+            for t, rel in ln_places:
+                ln_to(t, rel).wait_send()
+        small_out[pl.ds(n_rows, lnb.shape[0]), :] = (tree([ln_in[rel] for rel in range(n_fsdp)])
+                                                     + tree([ln_in[n_fsdp + rel] for rel in range(n_fsdp)]))
+
     start_block(0)
     load_t[0].wait()
 
@@ -452,7 +544,11 @@
         @pl.when((j >= 1) & (j - 1 < n_blocks))
         def _():
             stage_b(j - 1)
+        for at, act in ((0, smalls_begin), (3, smalls_middle), (6, smalls_end), (ln_at, ln_begin)):
+            pl.when(j == at)(act)
         return carry
+
+    ln_at = (OFFSET + n_chunk - 1 + SKEW * last - 4 * n_img) // 2
 
     n_steps = n_chunk + OFFSET + 2 * SKEW * last - 4 * n_img
     n_iter = n_img + max((n_steps + 1) // 2, n_blocks + 5)
@@ -477,59 +573,17 @@
             def _():
                 back_at(side, k).wait_send()
                 local_at(side, k).wait()
-
-    lanes = 128
-    n_rows = pack.shape[0]
-    tp_lo = n_rows - rs_t.shape[1]
-    pack[...] = jnp.zeros_like(pack)
-    gb_row = jnp.sum(gb[...], axis=0, keepdims=True)
-    for j in range(n_hid // lanes):
-        pack[pl.ds(j, 1), :] = gb_row[:, j * lanes:(j + 1) * lanes]
-    ln_row = jnp.sum(ln_acc[...], axis=0, keepdims=True)
-    bs_row = jnp.sum(b_sum[...], axis=0, keepdims=True)
-    n_wide = width // lanes
-    for j in range(n_wide):
-        pack[pl.ds(tp_lo - n_wide + j, 1), :] = bs_row[:, j * lanes:(j + 1) * lanes]
-        pack[pl.ds(tp_lo + j, 1), :] = ln_row[:, j * lanes:(j + 1) * lanes]
-    for j, ref in enumerate((gq, gk)):
-        pack[pl.ds(tp_lo + n_wide + j, 1), pl.ds(0, ref.shape[0])] = jnp.sum(ref[...].T, axis=0, keepdims=True)
-
-    def to_fsdp(rel):
-        return remote(pack, rs_f.at[rel - 1], xs_send.at[rel - 1], xs_recv.at[rel - 1], {'fsdp': flipped(me, rel)})
-
-    for rel in range(1, n_fsdp):
-        to_fsdp(rel).start()
-    for rel in range(1, n_fsdp):
-        to_fsdp(rel).wait()
-
-    def tree(terms):
-        while len(terms) > 1:
-            terms = [terms[j] + terms[j + 1] for j in range(0, len(terms), 2)]
-        return terms[0]
-
-    pack[...] = tree([pack[...]] + [rs_f[rel - 1] for rel in range(1, n_fsdp)])
-
-    def to_tp(rel):
-        return remote(pack.at[pl.ds(tp_lo, n_rows - tp_lo)], rs_t.at[rel - 1], xs_send.at[n_fsdp + rel - 2],
-                      xs_recv.at[n_fsdp + rel - 2], {'tp': flipped(my_tp, rel)})
-
-    for rel in range(1, n_tp):
-        to_tp(rel).start()
-    for rel in range(1, n_tp):
-        to_tp(rel).wait()
-    small_out[...] = pack[...]
-    small_out[pl.ds(tp_lo, n_rows - tp_lo), :] = tree(
-        [pack[pl.ds(tp_lo, n_rows - tp_lo)]] + [rs_t[rel - 1] for rel in range(1, n_tp)])
+    ln_end()
 
 
 def small_rows(n_hid, width):
     n_up, n_wide = n_hid // 128, width // 128
-    return n_up, n_wide, n_wide + 2 + -(n_up + 2 * n_wide + 2) % 8
+    return n_up, n_wide, 2 + -(n_up + n_wide + 2) % 8, -(-n_wide // 8) * 8
 
 
 def fused_call(mesh, normed, dy, x2, dn_attn, normed_t, dy_t, wu, wdt, b_up, ln_scale, b_sum, gq, gk, n_img):
     rows, width = x2.shape
-    pack_up, pack_wide, tp_rows = small_rows(wu.shape[1], width)
+    pack_up, pack_wide, tp_rows, ln_rows = small_rows(wu.shape[1], width)
     pack_shape = (pack_up + pack_wide + tp_rows, 128)
     n_hid = wu.shape[1]
     n_tok = rows // n_img
@@ -549,7 +603,7 @@
         kern,
         out_shape=(shape((rows, width), bf16), shape((blk, n_hid), f32), shape((blk, n_hid), f32),
                    shape((rows, n_hid), bf16), shape((rows, n_hid), bf16), shape((rows, width), f32),
-                   shape(pack_shape, f32)),
+                   shape((pack_shape[0] + ln_rows, 128), f32)),
         in_specs=[any_spec] * 8 + [vmem] * 5,
         out_specs=(any_spec,) * 6 + (vmem,),
         scratch_shapes=[
@@ -567,6 +621,8 @@
             vm((2, SENDS, STEP, width), bf16),
             vm((8, width), f32), vm(pack_shape, f32),
             vm((n_fsdp - 1,) + pack_shape, f32), vm((n_tp - 1, tp_rows, 128), f32),
+            vm((1, n_hid), f32), vm((1, width), f32),
+            vm((ln_rows, 128), f32), vm((2 * n_fsdp, ln_rows, 128), f32),
             dma((2, n_hid // min(TILE, n_hid))), dma((2, 2, 2)), dma((2, 2)), dma((2, width // COLS)), dma((2,)),
             dma((2,)), dma((R0,)), dma((2, P_SLOTS)), dma((2, R1)),
             dma((2, P_SLOTS)), dma((2, R2)), dma((P_SLOTS,)),
@@ -574,11 +630,12 @@
             dma((2, 2)), dma((2, 2)), dma((2, 2)), dma((2, 2)),
             dma((2, SENDS)), dma((2, SLOTS)), dma((2, SENDS)), dma((2, n_chunk)), dma((2, SENDS)),
             reg((2,)), dma((n_fsdp + n_tp - 2,)), dma((n_fsdp + n_tp - 2,)),
+            dma((n_tp * n_fsdp,)), dma((2 * n_fsdp,)),
         ],
         compiler_params=pltpu.CompilerParams(collective_id=0, has_side_effects=True, vmem_limit_bytes=67_043_328),
         cost_estimate=pl.CostEstimate(flops=200_000_000_000, bytes_accessed=200_000_000, transcendentals=0),
         name='mlp_chain',
-    )(normed, dy, x2, dn_attn, normed_t, dy_t, wu, wdt, b_up.reshape(1, n_hid), ln_scale.reshape(1, width), b_sum, gq, gk)
+    )(normed, dy, x2, dn_attn, normed_t, dy_t, wu, wdt, b_up.reshape(-1, 128), ln_scale.reshape(-1, 128), b_sum, gq, gk)
 
 
 def gather_steps(me, blk, srcs, full, shard, sems):
@@ -639,9 +696,9 @@
     return load.start, begin, middle, end
 
 
-def front_kernel(cfg, x, dy, wq, wk, wv, wo_t, w_up, gain, qs, ks,
+def front_kernel(cfg, x, dy, wq, wk, wv, wo_t, w_up, gain_t, q_row, k_row,
                  h, h_t, dy_t, w_qkv, w_full, o_t, dqkv_t, b_sum, gq, gk,
-                 xin, hst, ht_s, dyt_s, wp, wpt, shard, feat, ost, dst,
+                 xin, hst, ht_s, dyt_s, wp, wpt, shard, feat, ost, dst, gain, qs, ks,
                  in_sem, h_sem, t_sem, wout_sem, out_sem,
                  own_sem, put_sem, send, got, half_send, half_got, sib_send, sib_got):
     n_img, n_tok, n_heads, head_dim = cfg
@@ -681,6 +738,9 @@
     pl.semaphore_wait(barrier, 3)
     gathers[0][1]()
     gathers[1][1]()
+    gain[...] = as_row(gain_t[...])
+    for row, col in ((q_row, qs), (k_row, ks)):
+        col[...] = jnp.broadcast_to(row[...], (8, head_dim)).T[:, :1]
     b_sum[...] = jnp.zeros_like(b_sum)
     gq[...] = jnp.zeros_like(gq)
     gk[...] = jnp.zeros_like(gk)
@@ -788,14 +848,18 @@
             kn = (k_hat * ks[...]).astype(bf16)
             v = feat[v_rows, cols]
             d_o = feat[o_rows, cols]
-            logits = mm(kn, qn, ((0,), (0,))) * scale
-            e = jnp.exp(logits - jnp.max(logits, axis=0, keepdims=True))
-            p = e * (1.0 / jnp.sum(e, axis=0, keepdims=True))
-            pb = p.astype(bf16)
+            pbs, dss = [], []
+            for c in range(0, n_tok, 128):
+                logits = mm(kn, qn[:, c:c + 128], ((0,), (0,)))
+                e = jnp.exp2((logits - jnp.max(logits, axis=0, keepdims=True)) * (scale * LOG2E))
+                p = e * (1.0 / jnp.sum(e, axis=0, keepdims=True))
+                pbs.append(p.astype(bf16))
+                dp = mm(v, d_o[:, c:c + 128], ((0,), (0,))).astype(bf16).astype(f32)
+                dss.append((p * (dp - jnp.sum(p * dp, axis=0, keepdims=True)) * scale).astype(bf16))
+            pb = jnp.concatenate(pbs, axis=1)
+            ds = jnp.concatenate(dss, axis=1)
             ost[slot, pl.ds(lo, head_dim), :] = mm(v, pb, ((1,), (0,))).astype(bf16)
             dst[slot, v_rows, :] = mm(d_o, pb, ((1,), (1,))).astype(bf16)
-            dp = mm(v, d_o, ((0,), (0,))).astype(bf16).astype(f32)
-            ds = (p * (dp - jnp.sum(p * dp, axis=0, keepdims=True)) * scale).astype(bf16)
             dqn = mm(kn, ds, ((1,), (0,))).astype(bf16).astype(f32)
             dkn = mm(qn, ds, ((1,), (1,))).astype(bf16).astype(f32)
             gq[...] += dqn * q_hat
@@ -840,14 +904,14 @@
             vm((4, width, n_feat), bf16), vm((n_feat, width), bf16),
             vm((blk, n_hid), bf16), vm((4 * n_feat, rows), bf16),
             vm((2, n_feat, n_tok), bf16), vm((2, 3 * n_feat, n_tok), bf16),
+            vm((1, width), f32), vm((head_dim, 1), f32), vm((head_dim, 1), f32),
             dma((2, 2)), dma((2,)), dma((2,)), dma((3,)), dma((2, 2)),
             dma((5,)), dma, dma((5, 2)), dma((5, 2)), dma((5, 2)), dma((5, 2)), dma((5, 4)), dma((5, 4)),
         ],
         compiler_params=pltpu.CompilerParams(collective_id=1, has_side_effects=True, vmem_limit_bytes=67_043_328),
         cost_estimate=pl.CostEstimate(flops=60_000_000_000, bytes_accessed=100_000_000, transcendentals=5_000_000),
         name='front',
-    )(x2, dy, *attn_weights, w_up, ln_scale.reshape(1, width), q_scale.reshape(head_dim, 1),
-      k_scale.reshape(head_dim, 1))
+    )(x2, dy, *attn_weights, w_up, ln_scale.reshape(-1, 128), q_scale.reshape(1, head_dim), k_scale.reshape(1, head_dim))
 
 
 def outer_kernel(h_t, dy_t, dqkv_t, o_t, out):
@@ -877,7 +941,8 @@
     )(h_t, dy_t, d_qkv_t, o_t)
 
 
-def hand_over_kernel(n_feat, gx, g_up, g_dn, g_at, o_gx, o_up, o_dn, o_q, o_k, o_v, o_o, b_gx, b_up, b_dn, b_at,
+def hand_over_kernel(n_feat, gx, g_up, g_dn, g_at, small, o_gx, o_up, o_dn, o_q, o_k, o_v, o_o, s_up, s_dn, s_ln, s_q,
+                     s_k, b_gx, b_up, b_dn, b_at,
                      in_sem, out_sem):
     n_cut = b_gx.shape[0]
     step = b_gx.shape[1]
@@ -893,6 +958,13 @@
     stores.append([(b_at.at[:, pl.ds(j * n_feat, n_feat)], dst) for j, dst in enumerate((o_q, o_k, o_v, o_o))])
     for j, (src, buf) in enumerate(loads):
         pltpu.make_async_copy(src, buf, in_sem.at[j]).start()
+    n_up, n_wide = s_up.shape[0], s_ln.shape[0]
+    tp_lo = n_up + n_wide
+    s_up[...] = small[pl.ds(0, n_up), :]
+    s_dn[...] = small[pl.ds(n_up, n_wide), :]
+    s_q[...] = small[pl.ds(tp_lo, 1), pl.ds(0, s_q.shape[1])]
+    s_k[...] = small[pl.ds(tp_lo + 1, 1), pl.ds(0, s_k.shape[1])]
+    s_ln[...] = small[pl.ds(small.shape[0] - -(-n_wide // 8) * 8, n_wide), :]
     at, pending = 0, []
     for j, (src, buf) in enumerate(loads):
         pltpu.make_async_copy(src, buf, in_sem.at[j]).wait()
@@ -904,7 +976,7 @@
         c.wait()
 
 
-def hand_over(gx, g_up, g_dn, g_at, n_feat):
+def hand_over(gx, g_up, g_dn, g_at, small, n_feat, head_dim):
     rows, width = gx.shape
     blk = g_at.shape[0]
     n_cut = 8
@@ -912,17 +984,21 @@
     shape, vm, dma = jax.ShapeDtypeStruct, pltpu.VMEM, pltpu.SemaphoreType.DMA
     any_spec = pl.BlockSpec(memory_space=pl.ANY)
     side = shape((blk, n_feat), f32)
+    vmem = pl.BlockSpec(memory_space=pltpu.VMEM)
+    n_up, n_wide = g_up.shape[1] // 128, width // 128
     return pl.pallas_call(
         functools.partial(hand_over_kernel, n_feat),
-        out_shape=(shape(gx.shape, gx.dtype), shape(g_up.shape, f32), shape(g_dn.shape, f32), side, side, side, side),
-        in_specs=[any_spec] * 4,
-        out_specs=(any_spec,) * 7,
+        out_shape=(shape(gx.shape, gx.dtype), shape(g_up.shape, f32), shape(g_dn.shape, f32), side, side, side, side,
+                   shape((n_up, 128), f32), shape((n_wide, 128), f32), shape((n_wide, 128), f32), shape((1, head_dim), f32),
+                   shape((1, head_dim), f32)),
+        in_specs=[any_spec] * 4 + [vmem],
+        out_specs=(any_spec,) * 7 + (vmem,) * 5,
         scratch_shapes=[vm((n_cut, rows // n_cut, width), gx.dtype), vm(g_up.shape, f32), vm(g_dn.shape, f32),
                         vm(g_at.shape, f32), dma((n_cut + 3,)), dma((n_cut + 6,))],
         compiler_params=pltpu.CompilerParams(vmem_limit_bytes=60 << 20),
         cost_estimate=pl.CostEstimate(flops=1_000_000, bytes_accessed=40_000_000, transcendentals=0),
         name='hand_over',
-    )(gx, g_up, g_dn, g_at)
+    )(gx, g_up, g_dn, g_at, small)
 
 
 def solution(mesh):
@@ -955,13 +1031,10 @@
 
         grad_x, g_up, g_down_t, _, _, _, small = fused_call(
             mesh, normed, dy, x2, d_normed, normed_t, dy_t, wu_full, wdt_full, b_up, ln_scale, b_sum, gq, gk, num_img)
-        n_up, n_wide, _ = small_rows(wu_full.shape[1], width)
-        tp_lo = n_up + n_wide
-        q_lo = tp_lo + n_wide
         g_attn = scatter_rows(grad_w_attn)
-        grad_x, g_up, g_down_t, g_q, g_k, g_v, g_out_t = hand_over(grad_x, g_up, g_down_t, g_attn, n_qkv)
-        return (grad_x.reshape(x_in.shape), g_q, g_k, g_v, g_out_t.T, g_up, small[:n_up].reshape(-1),
-                g_down_t.T, small[n_up:tp_lo].reshape(-1), small[tp_lo:q_lo].reshape(-1),
-                small[q_lo, :head_dim], small[q_lo + 1, :head_dim])
+        (grad_x, g_up, g_down_t, g_q, g_k, g_v, g_out_t, s_up, s_down, s_ln, s_q, s_k) = hand_over(
+            grad_x, g_up, g_down_t, g_attn, small, n_qkv, head_dim)
+        return (grad_x.reshape(x_in.shape), g_q, g_k, g_v, g_out_t.T, g_up, s_up.reshape(-1), g_down_t.T,
+                s_down.reshape(-1), s_ln.reshape(-1), s_q.reshape(-1), s_k.reshape(-1))
 
     return jax.shard_map(local_step, mesh=mesh, in_specs=in_specs, out_specs=out_specs, check_vma=False)

time: 645 us -> 629 us (0.975)
  Pallas kernels: 579 us -> 568 us
  local copies, waits for them, and re-layouts: 8 us -> 0 us
    pallas_call x1, Pallas kernels: 404 us -> 395 us  [fused_call(): pl.pallas_call(kern, out_shape=(shape((rows, width), bf16), shape((blk, n...]
where the time goes in v5:
time: 629 us; the launch traced here: 618 us
  Pallas kernels  568 us (90%)
  matrix products  29.1 us (5%)
  between operations  14.5 us (2%)
  waiting for transfers between devices  6.29 us (1%)
    pallas_call x1, Pallas kernels, fused_call(): pl.pallas_call(kern, out_shape=(shape((rows, width), bf16), shape((blk, n...  395 us
    pallas_call x1, Pallas kernels, front_call(): pl.pallas_call(functools.partial(front_kernel, (n_img, n_tok, n_feat // h...  118 us
    pallas_call x1, Pallas kernels, attn_grads_call(): pl.pallas_call(outer_kernel, grid=(width // tile,), out_shape=jax.ShapeDt...  38.9 us
    dot_general x1, matrix products, local_step(): lax.dot_general(d_qkv_t, wqkv_full, (((0,), (1,)), ((), ())), preferred_e...  29.1 us
    pallas_call x1, Pallas kernels, hand_over(): pl.pallas_call(functools.partial(hand_over_kernel, n_feat), out_shape=(sh...  16.1 us
  transfers between devices with their start and end apart: 2, of which 1 were waited for; matrix products, arithmetic and copies ran while one was open for 5% of the time, Pallas kernels for 70%

profile of v5, /device:TPU:0, one launch (start us, length us, event | category | flops | bytes accessed | tf_op | source)
XLA Modules:
  0.0 617.9 jit_solution(9728677222503441515)
XLA Ops:
  7.2 0.0 all-gather.2.cloned.1.call-start
  7.2 117.8 %front.1 = (bf16[2048,2560]{1,0:T(8,128)(2,1)}, bf16[2560,2048]{1,0:T(8,128)(2,1)}, bf16[2560,2048]{1,0:T(8,128)(2,1)}, bf16[2560,1920]{1,0:T(8,128)(2,1)}, bf16...) custom-call(bf16[2048,2560]{1,0:T(8,128)(2,1)} %bitcast.19, ...), custom_call_target="tpu_custom_call" | custom-call | flops 60000002048 | bytes 100000000 | tf_op jit(solution)/shard_map/front/pallas_call | solution.py:893
  125.0 0.0 all-gather.2.cloned.1.call-update
  125.0 0.2 reduce-scatter.2.cloned.1.call-start
  125.2 38.9 %attn_grads.1 = f32[2560,2560]{1,0:T(8,128)} custom-call(bf16[2560,2048]{1,0:T(8,128)(2,1)} %get-tuple-element.43.ht_hbm.h_t, bf16[2560,2048]{1,0:T(8,128)(2,1)} %get-tuple-element.44.dyt_hbm.dy_t, bf16[1920,2048]{1,0:T(8,128)(2,1)} %get-tuple-element.41.dqkv_t, bf16[640,2048]{1,0:T(8,128)(2,1)} %get-tuple-element.54.o_t), custom_call_target="tpu_custom_call" | custom-call | flops 26843545600 | bytes 60000000 | tf_op jit(solution)/shard_map/attn_grads/pallas_call | solution.py:932
  164.2 0.0 reduce-scatter.2.cloned.1.call-update
  164.2 29.1 %fusion.dna_hbm = f32[2048,2560]{1,0:T(8,128)} fusion(bf16[1920,2048]{1,0:T(8,128)(2,1)} %get-tuple-element.41.dqkv_t, bf16[2560,1920]{1,0:T(8,128)(2,1)} %get-tuple-element.42), kind=kOutput, calls=%fused_computation | convolution fusion | flops 20132659200 | bytes 38666240 | tf_op jit(solution)/shard_map/dot_general | solution.py:1030
  193.3 6.2 %all-gather.2.cloned.1.call-done.wdt_hbm = bf16[2560,2560]{1,0:T(8,128)(2,1)} async-done(((bf16[320,2560]{1,0:T(8,128)(2,1)}), bf16[2560,2560]{1,0:T(8,128)(2,1)}) %all-gather.2.cloned.1.call-update) | async-done | bytes 13107216 | tf_op jit(solution)/shard_map/all_gather | solution.py:1028
  199.5 395.0 %mlp_chain.1 = (bf16[2048,2560]{1,0:T(8,128)(2,1)}, f32[320,2560]{1,0:T(8,128)}, f32[320,2560]{1,0:T(8,128)}, bf16[2048,2560]{1,0:T(8,128)(2,1)}, bf16[2048,2560...) custom-call(bf16[2048,2560]{1,0:T(8,128)(2,1)} %get-tuple-element.40.h_hbm, bf16[2048,2560]{1,0:T(8,128)(2,1)} %bitcast.22, ...), custom_call_target="tpu_custom_call" | custom-call | flops 199999995904 | bytes 200000000 | tf_op jit(solution)/shard_map/mlp_chain/pallas_call | solution.py:602
  594.6 0.0 reduce-scatter.2.cloned.1.call-done.g_at
  594.6 16.1 %hand_over.1 = (bf16[2048,2560]{1,0:T(8,128)(2,1)}, f32[320,2560]{1,0:T(8,128)}, f32[320,2560]{1,0:T(8,128)}, f32[320,640]{1,0:T(8,128)}, f32[320,640]{1,0:T(8,1...) custom-call(bf16[2048,2560]{1,0:T(8,128)(2,1)} %get-tuple-element.51, ...), custom_call_target="tpu_custom_call" | custom-call | flops 1000000 | bytes 40000000 | tf_op jit(solution)/shard_map/hand_over/pallas_call | solution.py:989
Async XLA Ops:
  7.2 192.3 %all-gather.2.cloned.1.call-start = ((), (), s32[]{:S(2)}) async-start(), calls=%async_computation.1 | async-start | bytes 14745600 | tf_op jit(solution)/shard_map/all_gather | solution.py:1028
  125.0 469.6 %reduce-scatter.2.cloned.1.call-start = ((), (), s32[]{:S(2)}) async-start(), calls=%async_computation.2 | async-start | bytes 29491200 | tf_op jit(solution)/shard_map/reduce_scatter | solution.py:1034
Sparse Core Ops, SparseCore 0:
  125.1 74.3 all-gather.1
  203.2 161.2 reduce-scatter.1

commit v6 on v5

--- a/solution.py
+++ b/solution.py
@@ -279,7 +279,12 @@
     load_t = [pltpu.make_async_copy(dyt_hbm, wdt.at[:, pl.ds(0, rows)], w_sem.at[1, 0]),
               pltpu.make_async_copy(ht_hbm, wu.at[:, pl.ds(0, rows)], w_sem.at[0, 0])]
 
+    early = n_img // 2
+    steps1 = 3 * n_img + early
+
     def phase1(i, carry):
+        step = 3 * i + i - (i // early) * (i - early)
+
         @pl.when(i > 0)
         def _():
             finish_image(i - 1)
@@ -288,12 +293,12 @@
         def _():
             for c in image_loads(i + 1):
                 c.start()
-        chain_step(4 * i)
+        chain_step(step)
         for c in image_loads(i):
             c.wait()
         for f in range(f_tiles):
             if f == (f_tiles + 1) // 2:
-                chain_step(4 * i + 1)
+                chain_step(step + 1)
             mlp_hidden(i, f)
         for c in image_outs(i):
             c.start()
@@ -301,10 +306,12 @@
         @pl.when(i == n_img - 1)
         def _():
             load_t[0].start()
-        chain_step(4 * i + 2)
+        chain_step(step + 2)
         for t in range(n_tiles):
             if t == n_tiles // 4 * 2:
-                chain_step(4 * i + 3)
+                @pl.when(i < early)
+                def _():
+                    chain_step(step + 3)
             mlp_back(i, t)
         return carry
 
@@ -534,12 +541,12 @@
             @pl.when((j >= lag) & (j - lag < n_blocks))
             def _():
                 stage(j - lag)
-        chain_step(4 * n_img + 2 * j)
+        chain_step(steps1 + 2 * j)
 
         @pl.when(j < n_blocks)
         def _():
             stage_a(j)
-        chain_step(4 * n_img + 2 * j + 1)
+        chain_step(steps1 + 2 * j + 1)
 
         @pl.when((j >= 1) & (j - 1 < n_blocks))
         def _():
@@ -548,9 +555,9 @@
             pl.when(j == at)(act)
         return carry
 
-    ln_at = (OFFSET + n_chunk - 1 + SKEW * last - 4 * n_img) // 2
-
-    n_steps = n_chunk + OFFSET + 2 * SKEW * last - 4 * n_img
+    ln_at = (OFFSET + n_chunk - 1 + SKEW * last - steps1) // 2
+
+    n_steps = n_chunk + OFFSET + 2 * SKEW * last - steps1
     n_iter = n_img + max((n_steps + 1) // 2, n_blocks + 5)
     lax.fori_loop(n_img, n_iter, phase2, 0)
 
@@ -956,8 +963,11 @@
         stores.append([(buf, dst)])
     loads.append((g_at, b_at))
     stores.append([(b_at.at[:, pl.ds(j * n_feat, n_feat)], dst) for j, dst in enumerate((o_q, o_k, o_v, o_o))])
-    for j, (src, buf) in enumerate(loads):
-        pltpu.make_async_copy(src, buf, in_sem.at[j]).start()
+    def load(j):
+        return pltpu.make_async_copy(*loads[j], in_sem.at[j])
+
+    for j in range(3):
+        load(j).start()
     n_up, n_wide = s_up.shape[0], s_ln.shape[0]
     tp_lo = n_up + n_wide
     s_up[...] = small[pl.ds(0, n_up), :]
@@ -966,8 +976,10 @@
     s_k[...] = small[pl.ds(tp_lo + 1, 1), pl.ds(0, s_k.shape[1])]
     s_ln[...] = small[pl.ds(small.shape[0] - -(-n_wide // 8) * 8, n_wide), :]
     at, pending = 0, []
-    for j, (src, buf) in enumerate(loads):
-        pltpu.make_async_copy(src, buf, in_sem.at[j]).wait()
+    for j in range(len(loads)):
+        load(j).wait()
+        if j + 3 < len(loads):
+            load(j + 3).start()
         for src2, dst in stores[j]:
             pending.append(pltpu.make_async_copy(src2, dst, out_sem.at[at]))
             pending[-1].start()

time: 629 us -> 623 us (level)
  no operation moved by 1% of the time
where the time goes in v6:
time: 623 us; the launch traced here: 615 us
  Pallas kernels  564 us (91%)
  matrix products  29.1 us (5%)
  between operations  14.5 us (2%)
  waiting for transfers between devices  6.29 us (1%)
    pallas_call x1, Pallas kernels, fused_call(): pl.pallas_call(kern, out_shape=(shape((rows, width), bf16), shape((blk, n...  391 us
    pallas_call x1, Pallas kernels, front_call(): pl.pallas_call(functools.partial(front_kernel, (n_img, n_tok, n_feat // h...  118 us
    pallas_call x1, Pallas kernels, attn_grads_call(): pl.pallas_call(outer_kernel, grid=(width // tile,), out_shape=jax.ShapeDt...  38.9 us
    dot_general x1, matrix products, local_step(): lax.dot_general(d_qkv_t, wqkv_full, (((0,), (1,)), ((), ())), preferred_e...  29.1 us
    pallas_call x1, Pallas kernels, hand_over(): pl.pallas_call(functools.partial(hand_over_kernel, n_feat), out_shape=(sh...  16.4 us
  transfers between devices with their start and end apart: 2, of which 1 were waited for; matrix products, arithmetic and copies ran while one was open for 5% of the time, Pallas kernels for 70%

profile of v6, /device:TPU:0, one launch (start us, length us, event | category | flops | bytes accessed | tf_op | source)
XLA Modules:
  0.0 614.6 jit_solution(5588603777652873088)
XLA Ops:
  7.2 0.0 all-gather.2.cloned.1.call-start
  7.2 117.8 %front.1 = (bf16[2048,2560]{1,0:T(8,128)(2,1)}, bf16[2560,2048]{1,0:T(8,128)(2,1)}, bf16[2560,2048]{1,0:T(8,128)(2,1)}, bf16[2560,1920]{1,0:T(8,128)(2,1)}, bf16...) custom-call(bf16[2048,2560]{1,0:T(8,128)(2,1)} %bitcast.19, ...), custom_call_target="tpu_custom_call" | custom-call | flops 60000002048 | bytes 100000000 | tf_op jit(solution)/shard_map/front/pallas_call | solution.py:900
  125.0 0.0 all-gather.2.cloned.1.call-update
  125.0 0.2 reduce-scatter.2.cloned.1.call-start
  125.2 38.9 %attn_grads.1 = f32[2560,2560]{1,0:T(8,128)} custom-call(bf16[2560,2048]{1,0:T(8,128)(2,1)} %get-tuple-element.43.ht_hbm.h_t, bf16[2560,2048]{1,0:T(8,128)(2,1)} %get-tuple-element.44.dyt_hbm.dy_t, bf16[1920,2048]{1,0:T(8,128)(2,1)} %get-tuple-element.41.dqkv_t, bf16[640,2048]{1,0:T(8,128)(2,1)} %get-tuple-element.54.o_t), custom_call_target="tpu_custom_call" | custom-call | flops 26843545600 | bytes 60000000 | tf_op jit(solution)/shard_map/attn_grads/pallas_call | solution.py:939
  164.2 0.0 reduce-scatter.2.cloned.1.call-update
  164.2 29.1 %fusion.dna_hbm = f32[2048,2560]{1,0:T(8,128)} fusion(bf16[1920,2048]{1,0:T(8,128)(2,1)} %get-tuple-element.41.dqkv_t, bf16[2560,1920]{1,0:T(8,128)(2,1)} %get-tuple-element.42), kind=kOutput, calls=%fused_computation | convolution fusion | flops 20132659200 | bytes 38666240 | tf_op jit(solution)/shard_map/dot_general | solution.py:1042
  193.3 6.2 %all-gather.2.cloned.1.call-done.wdt_hbm = bf16[2560,2560]{1,0:T(8,128)(2,1)} async-done(((bf16[320,2560]{1,0:T(8,128)(2,1)}), bf16[2560,2560]{1,0:T(8,128)(2,1)}) %all-gather.2.cloned.1.call-update) | async-done | bytes 13107216 | tf_op jit(solution)/shard_map/all_gather | solution.py:1040
  199.5 391.3 %mlp_chain.1 = (bf16[2048,2560]{1,0:T(8,128)(2,1)}, f32[320,2560]{1,0:T(8,128)}, f32[320,2560]{1,0:T(8,128)}, bf16[2048,2560]{1,0:T(8,128)(2,1)}, bf16[2048,2560...) custom-call(bf16[2048,2560]{1,0:T(8,128)(2,1)} %get-tuple-element.40.h_hbm, bf16[2048,2560]{1,0:T(8,128)(2,1)} %bitcast.22, ...), custom_call_target="tpu_custom_call" | custom-call | flops 199999995904 | bytes 200000000 | tf_op jit(solution)/shard_map/mlp_chain/pallas_call | solution.py:609
  590.8 0.0 reduce-scatter.2.cloned.1.call-done.g_at
  590.9 16.4 %hand_over.1 = (bf16[2048,2560]{1,0:T(8,128)(2,1)}, f32[320,2560]{1,0:T(8,128)}, f32[320,2560]{1,0:T(8,128)}, f32[320,640]{1,0:T(8,128)}, f32[320,640]{1,0:T(8,1...) custom-call(bf16[2048,2560]{1,0:T(8,128)(2,1)} %get-tuple-element.51, ...), custom_call_target="tpu_custom_call" | custom-call | flops 1000000 | bytes 40000000 | tf_op jit(solution)/shard_map/hand_over/pallas_call | solution.py:1001
Async XLA Ops:
  7.2 192.3 %all-gather.2.cloned.1.call-start = ((), (), s32[]{:S(2)}) async-start(), calls=%async_computation.1 | async-start | bytes 14745600 | tf_op jit(solution)/shard_map/all_gather | solution.py:1040
  125.0 465.8 %reduce-scatter.2.cloned.1.call-start = ((), (), s32[]{:S(2)}) async-start(), calls=%async_computation.2 | async-start | bytes 29491200 | tf_op jit(solution)/shard_map/reduce_scatter | solution.py:1046
Sparse Core Ops, SparseCore 0:
  125.1 74.3 all-gather.1
  203.2 171.8 reduce-scatter.1

commit v7 on v6

--- a/solution.py
+++ b/solution.py
@@ -13,6 +13,7 @@
 MESH = pl.DeviceIdType.MESH
 OFFSET = 5
 SKEW = 2
+BACK = 1
 SLOTS = 6
 SENDS = 4
 STEP = 16
@@ -204,7 +205,7 @@
             def _():
                 pl.semaphore_signal(credit.at[side], inc=1, device_id=prv, device_id_type=MESH)
 
-        kb = i - OFFSET - SKEW * last - SKEW * (last - pos)
+        kb = i - OFFSET - SKEW * last - BACK * (last - pos)
 
         @pl.when((pos < last) & (kb >= 0) & (kb < n_chunk))
         def _():
@@ -537,15 +538,18 @@
 
     def phase2(i, carry):
         j = i - n_img
-        for lag, stage in ((5, stage_d), (3, stage_c)):
-            @pl.when((j >= lag) & (j - lag < n_blocks))
-            def _():
-                stage(j - lag)
+        @pl.when((j >= 3) & (j - 3 < n_blocks))
+        def _():
+            stage_c(j - 3)
         chain_step(steps1 + 2 * j)
 
         @pl.when(j < n_blocks)
         def _():
             stage_a(j)
+
+        @pl.when((j >= 4) & (j - 4 < n_blocks))
+        def _():
+            stage_d(j - 4)
         chain_step(steps1 + 2 * j + 1)
 
         @pl.when((j >= 1) & (j - 1 < n_blocks))
@@ -557,8 +561,8 @@
 
     ln_at = (OFFSET + n_chunk - 1 + SKEW * last - steps1) // 2
 
-    n_steps = n_chunk + OFFSET + 2 * SKEW * last - steps1
-    n_iter = n_img + max((n_steps + 1) // 2, n_blocks + 5)
+    n_steps = n_chunk + OFFSET + (SKEW + BACK) * last - steps1
+    n_iter = n_img + max((n_steps + 1) // 2, n_blocks + 4)
     lax.fori_loop(n_img, n_iter, phase2, 0)
 
     for j in range(n_blocks - P_SLOTS, n_blocks):

time: 623 us -> 630 us (1.011)
  Pallas kernels: 564 us -> 571 us
    pallas_call x1, Pallas kernels: 391 us -> 398 us  [fused_call(): pl.pallas_call(kern, out_shape=(shape((rows, width), bf16), shape((blk, n...]
where the time goes in v7:
time: 630 us; the launch traced here: 621 us
  Pallas kernels  571 us (91%)
  matrix products  29.1 us (5%)
  between operations  14.5 us (2%)
    pallas_call x1, Pallas kernels, fused_call(): pl.pallas_call(kern, out_shape=(shape((rows, width), bf16), shape((blk, n...  398 us
    pallas_call x1, Pallas kernels, front_call(): pl.pallas_call(functools.partial(front_kernel, (n_img, n_tok, n_feat // h...  118 us
    pallas_call x1, Pallas kernels, attn_grads_call(): pl.pallas_call(outer_kernel, grid=(width // tile,), out_shape=jax.ShapeDt...  38.9 us
    dot_general x1, matrix products, local_step(): lax.dot_general(d_qkv_t, wqkv_full, (((0,), (1,)), ((), ())), preferred_e...  29.1 us
    pallas_call x1, Pallas kernels, hand_over(): pl.pallas_call(functools.partial(hand_over_kernel, n_feat), out_shape=(sh...  16.4 us
  transfers between devices with their start and end apart: 2, of which 1 were waited for; matrix products, arithmetic and copies ran while one was open for 5% of the time, Pallas kernels for 70%

profile of v7, /device:TPU:0, one launch (start us, length us, event | category | flops | bytes accessed | tf_op | source)
XLA Modules:
  0.0 620.9 jit_solution(15285979477469504939)
XLA Ops:
  7.2 0.0 all-gather.2.cloned.1.call-start
  7.2 117.8 %front.1 = (bf16[2048,2560]{1,0:T(8,128)(2,1)}, bf16[2560,2048]{1,0:T(8,128)(2,1)}, bf16[2560,2048]{1,0:T(8,128)(2,1)}, bf16[2560,1920]{1,0:T(8,128)(2,1)}, bf16...) custom-call(bf16[2048,2560]{1,0:T(8,128)(2,1)} %bitcast.19, ...), custom_call_target="tpu_custom_call" | custom-call | flops 60000002048 | bytes 100000000 | tf_op jit(solution)/shard_map/front/pallas_call | solution.py:904
  125.0 0.0 all-gather.2.cloned.1.call-update
  125.0 0.2 reduce-scatter.2.cloned.1.call-start
  125.2 38.9 %attn_grads.1 = f32[2560,2560]{1,0:T(8,128)} custom-call(bf16[2560,2048]{1,0:T(8,128)(2,1)} %get-tuple-element.43.ht_hbm.h_t, bf16[2560,2048]{1,0:T(8,128)(2,1)} %get-tuple-element.44.dyt_hbm.dy_t, bf16[1920,2048]{1,0:T(8,128)(2,1)} %get-tuple-element.41.dqkv_t, bf16[640,2048]{1,0:T(8,128)(2,1)} %get-tuple-element.54.o_t), custom_call_target="tpu_custom_call" | custom-call | flops 26843545600 | bytes 60000000 | tf_op jit(solution)/shard_map/attn_grads/pallas_call | solution.py:943
  164.2 0.0 reduce-scatter.2.cloned.1.call-update
  164.2 29.1 %fusion.dna_hbm = f32[2048,2560]{1,0:T(8,128)} fusion(bf16[1920,2048]{1,0:T(8,128)(2,1)} %get-tuple-element.41.dqkv_t, bf16[2560,1920]{1,0:T(8,128)(2,1)} %get-tuple-element.42), kind=kOutput, calls=%fused_computation | convolution fusion | flops 20132659200 | bytes 38666240 | tf_op jit(solution)/shard_map/dot_general | solution.py:1046
  193.3 6.2 %all-gather.2.cloned.1.call-done.wdt_hbm = bf16[2560,2560]{1,0:T(8,128)(2,1)} async-done(((bf16[320,2560]{1,0:T(8,128)(2,1)}), bf16[2560,2560]{1,0:T(8,128)(2,1)}) %all-gather.2.cloned.1.call-update) | async-done | bytes 13107216 | tf_op jit(solution)/shard_map/all_gather | solution.py:1044
  199.5 397.6 %mlp_chain.1 = (bf16[2048,2560]{1,0:T(8,128)(2,1)}, f32[320,2560]{1,0:T(8,128)}, f32[320,2560]{1,0:T(8,128)}, bf16[2048,2560]{1,0:T(8,128)(2,1)}, bf16[2048,2560...) custom-call(bf16[2048,2560]{1,0:T(8,128)(2,1)} %get-tuple-element.40.h_hbm, bf16[2048,2560]{1,0:T(8,128)(2,1)} %bitcast.22, ...), custom_call_target="tpu_custom_call" | custom-call | flops 199999995904 | bytes 200000000 | tf_op jit(solution)/shard_map/mlp_chain/pallas_call | solution.py:613
  597.2 0.0 reduce-scatter.2.cloned.1.call-done.g_at
  597.2 16.4 %hand_over.1 = (bf16[2048,2560]{1,0:T(8,128)(2,1)}, f32[320,2560]{1,0:T(8,128)}, f32[320,2560]{1,0:T(8,128)}, f32[320,640]{1,0:T(8,128)}, f32[320,640]{1,0:T(8,1...) custom-call(bf16[2048,2560]{1,0:T(8,128)(2,1)} %get-tuple-element.51, ...), custom_call_target="tpu_custom_call" | custom-call | flops 1000000 | bytes 40000000 | tf_op jit(solution)/shard_map/hand_over/pallas_call | solution.py:1005
Async XLA Ops:
  7.2 192.3 %all-gather.2.cloned.1.call-start = ((), (), s32[]{:S(2)}) async-start(), calls=%async_computation.1 | async-start | bytes 14745600 | tf_op jit(solution)/shard_map/all_gather | solution.py:1044
  125.0 472.2 %reduce-scatter.2.cloned.1.call-start = ((), (), s32[]{:S(2)}) async-start(), calls=%async_computation.2 | async-start | bytes 29491200 | tf_op jit(solution)/shard_map/reduce_scatter | solution.py:1050
Sparse Core Ops, SparseCore 0:
  125.1 74.3 all-gather.1
  203.2 166.1 reduce-scatter.1
